TPU v7x, 32 devices: a whole 2x2x4 slice. The times are simulated.
32 devices in a mesh: dp: 2 (over x), col: 4 (over z), row: 4 (over y, core).
Axes of the slice: x: 2, y: 2, z: 4, core: 2. Of those that a mesh axis runs over, the one named last changes fastest.
Arguments:
- left_mat: bfloat16 [65536, 2048], P(('dp', 'row'), 'col'), parts along dimension 0
- right_mat: bfloat16 [2048, 8192], P('row', 'col')
Outputs:
- output: bfloat16 [65536, 8192], P(('dp', 'row'), 'col'), parts along dimension 0
There are 2 independent parts. A program takes and returns all parts, laid end to end along the dimension named above; an argument that names none is the same for every part.
All inputs are finite; a program needn't handle non-finite values.
Results may differ from a plain program's by a relative error of at most 0.001.
Values are sent between devices in bfloat16 or wider.
A program may use at most 1 GiB of HBM per device.

v0:
```python
import jax
import jax.numpy as jnp
from jax import lax
from jax.experimental import pallas as pl
from jax.experimental.pallas import tpu as pltpu
from jax.sharding import PartitionSpec as P


GROUPS = (256, 1024, 1024, 1024, 1024, 1024, 1024, 768, 512, 256, 256)
BM = 256


def _mm_kernel(own, near, far, mid, b_ref, *rest):
    out_ref = rest[-1]
    lhs = jnp.concatenate([own[...], near[...], far[...], mid[...]], axis=1)
    out_ref[...] = jnp.dot(lhs, b_ref[...], preferred_element_type=jnp.float32).astype(out_ref.dtype)


def _group_product(a, near, far, mid, b, c, rows, cols, off, size):
    bm = BM if size > BM else BM // 2
    depth = a.shape[1]
    total = b.shape[0]
    piece = pl.BlockSpec((bm, depth), lambda i: (i, 0))
    own = pl.BlockSpec((bm, depth), lambda i: (off // bm + i, 0))
    whole = pl.BlockSpec((total, cols), lambda i: (0, 0), pipeline_mode=pl.Buffered(1))
    out = pl.BlockSpec((bm, cols), lambda i: (off // bm + i, 0))
    in_specs = [own, piece, piece, piece, whole]
    args = [a, near, far, mid, b]
    alias = {}
    if c is not None:
        in_specs.append(pl.BlockSpec(memory_space=pl.ANY))
        args.append(c)
        alias = {5: 0}
    return pl.pallas_call(
        _mm_kernel,
        grid=(size // bm,),
        out_shape=jax.ShapeDtypeStruct((rows, cols), jnp.bfloat16),
        in_specs=in_specs,
        out_specs=out,
        input_output_aliases=alias,
        compiler_params=pltpu.CompilerParams(dimension_semantics=("arbitrary",), vmem_limit_bytes=28 * 2**20),
        cost_estimate=pl.CostEstimate(
            flops=2 * size * total * cols,
            bytes_accessed=size * (total + cols) * 2,
            transcendentals=0,
        ),
        name="group_product",
    )(*args)


def solution(mesh):
    side = mesh.shape["row"]
    with_near = [(p, p ^ 1) for p in range(side)]
    with_far = [(p, side - 1 - p) for p in range(side)]

    def local(a, b_own):
        rows, depth = a.shape
        cols = b_own.shape[1]
        offs = [sum(GROUPS[:g]) for g in range(len(GROUPS))]
        row_pos, col_pos = lax.axis_index("row"), lax.axis_index("col")

        parts = [lax.slice_in_dim(a, o, o + s) for o, s in zip(offs, GROUPS)]
        near = [lax.ppermute(x, "col", with_near) for x in parts]
        far = [lax.ppermute(x, "col", with_far) for x in parts]
        mid = [lax.ppermute(x, "col", with_near) for x in far]

        b = jnp.zeros((side * depth, cols), b_own.dtype)
        for s in range(side):
            blk = b_own if s == 0 else lax.ppermute(b_own, "row", [(p, (p - s) % side) for p in range(side)])
            rel = lax.rem(row_pos + s, side) ^ col_pos
            b = lax.dynamic_update_slice_in_dim(b, blk, (rel ^ (rel // 2)) * depth, 0)

        c = None
        for g, (off, size) in enumerate(zip(offs, GROUPS)):
            c = _group_product(a, near[g], far[g], mid[g], b, c, rows, cols, off, size)
        return c

    return jax.shard_map(
        local, mesh=mesh, in_specs=(P(("dp", "row"), "col"), P("row", "col")),
        out_specs=P(("dp", "row"), "col"), check_vma=False,
    )
```

profile of v0, /device:TPU:28, one launch (start us, length us, event | category | flops | bytes accessed | tf_op | source)
XLA Modules:
  0.0 555.3 jit_solution(12774033768903213800)
XLA Ops:
  4.3 10.1 %collective-permute-done.34.far = bf16[256,512]{1,0:T(8,128)(2,1)S(1)} collective-permute-done((bf16[256,512]{1,0:T(8,128)(2,1)S(1)}, bf16[256,512]{1,0:T(8,128)(2,1)S(1)}, u32[]{:S(2)}, u32[]{:S(2)}) %collective-permute-start.34) | collective-permute-done | bytes 262176 | tf_op jit(solution)/shard_map/ppermute | solution.py:64
  14.4 2.6 collective-permute-start.35
  17.0 5.2 fusion.1
  25.0 25.1 %collective-permute-done.31.far = bf16[1024,512]{1,0:T(8,128)(2,1)S(1)} collective-permute-done((bf16[1024,512]{1,0:T(8,128)(2,1)S(1)}, bf16[1024,512]{1,0:T(8,128)(2,1)S(1)}, u32[]{:S(2)}, u32[]{:S(2)}) %collective-permute-start.31) | collective-permute-done | bytes 1048608 | tf_op jit(solution)/shard_map/ppermute | solution.py:64
  51.4 21.1 %collective-permute-done.30.near = bf16[1024,512]{1,0:T(8,128)(2,1)S(1)} collective-permute-done((bf16[1024,512]{1,0:T(8,128)(2,1)S(1)}, bf16[1024,512]{1,0:T(8,128)(2,1)S(1)}, u32[]{:S(2)}, u32[]{:S(2)}) %collective-permute-start.30) | collective-permute-done | bytes 1048608 | tf_op jit(solution)/shard_map/ppermute | solution.py:63
  75.5 17.6 %collective-permute-done.4 = bf16[512,2048]{1,0:T(8,128)(2,1)} collective-permute-done((bf16[512,2048]{1,0:T(8,128)(2,1)}, bf16[512,2048]{1,0:T(8,128)(2,1)}, u32[]{:S(2)}, u32[]{:S(2)}) %collective-permute-start.4) | collective-permute-done | bytes 2097184 | tf_op jit(solution)/shard_map/ppermute | solution.py:69
  93.5 4.4 broadcast_in_dim.3
  97.9 3.2 constant_dynamic-update-slice_fusion.3
  105.1 3.3 constant_dynamic-update-slice_fusion.2
  108.4 3.2 constant_dynamic-update-slice_fusion.1
  111.6 5.8 %collective-permute-start.24 = (bf16[1024,512]{1,0:T(8,128)(2,1)S(1)}, bf16[1024,512]{1,0:T(8,128)(2,1)S(1)}, u32[]{:S(2)}, u32[]{:S(2)}) collective-permute-start(bf16[1024,512]{1,0:T(8,128)(2,1)S(1)} %copy-done.10), channel_id=1, source_target_pairs={{0,4},{4,0},{8,12},{12,8},{1,5},{5,1},{9,13},{13,9},{2,6},{6,2},{1... | collective-permute-start | bytes 3145736 | tf_op jit(solution)/shard_map/ppermute | solution.py:63
  117.4 17.2 %collective-permute-done.27.near = bf16[1024,512]{1,0:T(8,128)(2,1)S(1)} collective-permute-done((bf16[1024,512]{1,0:T(8,128)(2,1)}, bf16[1024,512]{1,0:T(8,128)(2,1)S(1)}, u32[]{:S(2)}, u32[]{:S(2)}) %collective-permute-start.27) | collective-permute-done | bytes 1048608 | tf_op jit(solution)/shard_map/ppermute | solution.py:63
  134.6 2.8 collective-permute-start.22
  137.5 3.2 constant_dynamic-update-slice_fusion.b_ref
  140.7 3.4 copy-done
  144.1 6.9 %group_product.11.rest_0_ = bf16[8192,2048]{1,0:T(8,128)(2,1)} custom-call(bf16[8192,512]{1,0:T(8,128)(2,1)S(1)} %copy-done, bf16[256,512]{1,0:T(8,128)(2,1)S(1)} %copy-done.4, bf16[256,512]{1,0:T(8,128)(2,1)S(1)} %collective-permute-done.34.far, bf16[256,512]{1,0:T(8,128)(2,1)S(1)} %copy-done.6, bf16[2048,2048]{1,0:T(8,128)(2,1)} %constant_dynamic-update-slice_fusion.b_ref), custom_call_target="tpu_custom_call" | custom-call | flops 2147483648 | bytes 2097152 | tf_op jit(solution)/shard_map/group_product/pallas_call | solution.py:34
  152.0 8.0 %collective-permute-done.32.mid = bf16[1024,512]{1,0:T(8,128)(2,1)} collective-permute-done((bf16[1024,512]{1,0:T(8,128)(2,1)S(1)}, bf16[1024,512]{1,0:T(8,128)(2,1)}, u32[]{:S(2)}, u32[]{:S(2)}) %collective-permute-start.32) | collective-permute-done | bytes 1048608 | tf_op jit(solution)/shard_map/ppermute | solution.py:65
  162.2 13.8 %group_product.12.rest_0_ = bf16[8192,2048]{1,0:T(8,128)(2,1)} custom-call(bf16[8192,512]{1,0:T(8,128)(2,1)S(1)} %copy-done, bf16[1024,512]{1,0:T(8,128)(2,1)S(1)} %copy-done.2, bf16[1024,512]{1,0:T(8,128)(2,1)S(1)} %collective-permute-done.31.far, bf16[1024,512]{1,0:T(8,128)(2,1)} %collective-permute-done.32.mid, ...), custom_call_target="tpu_custom_call", output_to_operand_aliasing={{}: (5, {})} | custom-call | flops 8589934592 | bytes 8388608 | tf_op jit(solution)/shard_map/group_product/pallas_call | solution.py:34
  176.0 9.0 %collective-permute-done.24.near = bf16[1024,512]{1,0:T(8,128)(2,1)S(1)} collective-permute-done((bf16[1024,512]{1,0:T(8,128)(2,1)S(1)}, bf16[1024,512]{1,0:T(8,128)(2,1)S(1)}, u32[]{:S(2)}, u32[]{:S(2)}) %collective-permute-start.24) | collective-permute-done | bytes 1048608 | tf_op jit(solution)/shard_map/ppermute | solution.py:63
  185.1 22.4 %collective-permute-done.22.far = bf16[1024,512]{1,0:T(8,128)(2,1)S(1)} collective-permute-done((bf16[1024,512]{1,0:T(8,128)(2,1)S(1)}, bf16[1024,512]{1,0:T(8,128)(2,1)S(1)}, u32[]{:S(2)}, u32[]{:S(2)}) %collective-permute-start.22) | collective-permute-done | bytes 1048608 | tf_op jit(solution)/shard_map/ppermute | solution.py:64
  208.9 21.2 %collective-permute-done.29.mid = bf16[1024,512]{1,0:T(8,128)(2,1)S(1)} collective-permute-done((bf16[1024,512]{1,0:T(8,128)(2,1)S(1)}, bf16[1024,512]{1,0:T(8,128)(2,1)S(1)}, u32[]{:S(2)}, u32[]{:S(2)}) %collective-permute-start.29) | collective-permute-done | bytes 1048608 | tf_op jit(solution)/shard_map/ppermute | solution.py:65
  230.0 13.7 %group_product.13.rest_0_ = bf16[8192,2048]{1,0:T(8,128)(2,1)} custom-call(bf16[8192,512]{1,0:T(8,128)(2,1)S(1)} %copy-done, bf16[1024,512]{1,0:T(8,128)(2,1)S(1)} %collective-permute-done.27.near, bf16[1024,512]{1,0:T(8,128)(2,1)S(1)} %collective-permute-done.28.far, ...), custom_call_target="tpu_custom_call", output_to_operand_aliasing={{}: (5, {})} | custom-call | flops 8589934592 | bytes 8388608 | tf_op jit(solution)/shard_map/group_product/pallas_call | solution.py:34
  243.7 8.8 %collective-permute-done.19.far = bf16[1024,512]{1,0:T(8,128)(2,1)S(1)} collective-permute-done((bf16[1024,512]{1,0:T(8,128)(2,1)S(1)}, bf16[1024,512]{1,0:T(8,128)(2,1)S(1)}, u32[]{:S(2)}, u32[]{:S(2)}) %collective-permute-start.19) | collective-permute-done | bytes 1048608 | tf_op jit(solution)/shard_map/ppermute | solution.py:64
  252.5 19.7 %collective-permute-done.26.mid = bf16[1024,512]{1,0:T(8,128)(2,1)S(1)} collective-permute-done((bf16[1024,512]{1,0:T(8,128)(2,1)}, bf16[1024,512]{1,0:T(8,128)(2,1)S(1)}, u32[]{:S(2)}, u32[]{:S(2)}) %collective-permute-start.26) | collective-permute-done | bytes 1048608 | tf_op jit(solution)/shard_map/ppermute | solution.py:65
  272.2 2.4 collective-permute-start.20
  274.5 13.8 %group_product.14.rest_0_ = bf16[8192,2048]{1,0:T(8,128)(2,1)} custom-call(bf16[8192,512]{1,0:T(8,128)(2,1)S(1)} %copy-done, bf16[1024,512]{1,0:T(8,128)(2,1)S(1)} %collective-permute-done.24.near, bf16[1024,512]{1,0:T(8,128)(2,1)} %collective-permute-done.25.far, bf16[1024,512]{1,0:T(8,128)(2,1)S(1)} %collective-permute-done.26.mid, ...), custom_call_target="tpu_custom_call", output_to_operand_aliasing={{}: (5, {})} | custom-call | flops 8589934592 | bytes 8388608 | tf_op jit(solution)/shard_map/group_product/pallas_call | solution.py:34
  288.4 9.0 %collective-permute-done.21.near = bf16[1024,512]{1,0:T(8,128)(2,1)S(1)} collective-permute-done((bf16[1024,512]{1,0:T(8,128)(2,1)S(1)}, bf16[1024,512]{1,0:T(8,128)(2,1)S(1)}, u32[]{:S(2)}, u32[]{:S(2)}) %collective-permute-start.21) | collective-permute-done | bytes 1048608 | tf_op jit(solution)/shard_map/ppermute | solution.py:63
  297.4 22.6 %collective-permute-done.16.far = bf16[1024,512]{1,0:T(8,128)(2,1)S(1)} collective-permute-done((bf16[1024,512]{1,0:T(8,128)(2,1)S(1)}, bf16[1024,512]{1,0:T(8,128)(2,1)S(1)}, u32[]{:S(2)}, u32[]{:S(2)}) %collective-permute-start.16) | collective-permute-done | bytes 1048608 | tf_op jit(solution)/shard_map/ppermute | solution.py:64
  321.4 18.2 %collective-permute-done.23.mid = bf16[1024,512]{1,0:T(8,128)(2,1)S(1)} collective-permute-done((bf16[1024,512]{1,0:T(8,128)(2,1)S(1)}, bf16[1024,512]{1,0:T(8,128)(2,1)S(1)}, u32[]{:S(2)}, u32[]{:S(2)}) %collective-permute-start.23) | collective-permute-done | bytes 1048608 | tf_op jit(solution)/shard_map/ppermute | solution.py:65
  339.6 2.4 collective-permute-start.17
  342.0 13.7 %group_product.15.rest_0_ = bf16[8192,2048]{1,0:T(8,128)(2,1)} custom-call(bf16[8192,512]{1,0:T(8,128)(2,1)S(1)} %copy-done, bf16[1024,512]{1,0:T(8,128)(2,1)S(1)} %collective-permute-done.21.near, bf16[1024,512]{1,0:T(8,128)(2,1)S(1)} %collective-permute-done.22.far, ...), custom_call_target="tpu_custom_call", output_to_operand_aliasing={{}: (5, {})} | custom-call | flops 8589934592 | bytes 8388608 | tf_op jit(solution)/shard_map/group_product/pallas_call | solution.py:34
  355.7 6.3 %collective-permute-done.18.near = bf16[1024,512]{1,0:T(8,128)(2,1)S(1)} collective-permute-done((bf16[1024,512]{1,0:T(8,128)(2,1)S(1)}, bf16[1024,512]{1,0:T(8,128)(2,1)S(1)}, u32[]{:S(2)}, u32[]{:S(2)}) %collective-permute-start.18) | collective-permute-done | bytes 1048608 | tf_op jit(solution)/shard_map/ppermute | solution.py:63
  362.1 2.4 collective-permute-start.12
  364.5 20.0 %collective-permute-done.20.mid = bf16[1024,512]{1,0:T(8,128)(2,1)S(1)} collective-permute-done((bf16[1024,512]{1,0:T(8,128)(2,1)S(1)}, bf16[1024,512]{1,0:T(8,128)(2,1)S(1)}, u32[]{:S(2)}, u32[]{:S(2)}) %collective-permute-start.20) | collective-permute-done | bytes 1048608 | tf_op jit(solution)/shard_map/ppermute | solution.py:65
  384.5 2.4 collective-permute-start.10
  387.0 13.7 %group_product.16.rest_0_ = bf16[8192,2048]{1,0:T(8,128)(2,1)} custom-call(bf16[8192,512]{1,0:T(8,128)(2,1)S(1)} %copy-done, bf16[1024,512]{1,0:T(8,128)(2,1)S(1)} %collective-permute-done.18.near, bf16[1024,512]{1,0:T(8,128)(2,1)S(1)} %collective-permute-done.19.far, ...), custom_call_target="tpu_custom_call", output_to_operand_aliasing={{}: (5, {})} | custom-call | flops 8589934592 | bytes 8388608 | tf_op jit(solution)/shard_map/group_product/pallas_call | solution.py:34
  400.7 26.1 %collective-permute-done.13.far = bf16[768,512]{1,0:T(8,128)(2,1)S(1)} collective-permute-done((bf16[768,512]{1,0:T(8,128)(2,1)S(1)}, bf16[768,512]{1,0:T(8,128)(2,1)S(1)}, u32[]{:S(2)}, u32[]{:S(2)}) %collective-permute-start.13) | collective-permute-done | bytes 786464 | tf_op jit(solution)/shard_map/ppermute | solution.py:64
  428.2 18.1 %collective-permute-done.17.mid = bf16[1024,512]{1,0:T(8,128)(2,1)S(1)} collective-permute-done((bf16[1024,512]{1,0:T(8,128)(2,1)S(1)}, bf16[1024,512]{1,0:T(8,128)(2,1)S(1)}, u32[]{:S(2)}, u32[]{:S(2)}) %collective-permute-start.17) | collective-permute-done | bytes 1048608 | tf_op jit(solution)/shard_map/ppermute | solution.py:65
  446.3 2.4 collective-permute-start.14
  448.8 13.7 %group_product.17.rest_0_ = bf16[8192,2048]{1,0:T(8,128)(2,1)} custom-call(bf16[8192,512]{1,0:T(8,128)(2,1)S(1)} %copy-done, bf16[1024,512]{1,0:T(8,128)(2,1)S(1)} %collective-permute-done.15.near, bf16[1024,512]{1,0:T(8,128)(2,1)S(1)} %collective-permute-done.16.far, ...), custom_call_target="tpu_custom_call", output_to_operand_aliasing={{}: (5, {})} | custom-call | flops 8589934592 | bytes 8388608 | tf_op jit(solution)/shard_map/group_product/pallas_call | solution.py:34
  462.5 14.8 %collective-permute-done.10.far = bf16[512,512]{1,0:T(8,128)(2,1)S(1)} collective-permute-done((bf16[512,512]{1,0:T(8,128)(2,1)S(1)}, bf16[512,512]{1,0:T(8,128)(2,1)S(1)}, u32[]{:S(2)}, u32[]{:S(2)}) %collective-permute-start.10) | collective-permute-done | bytes 524320 | tf_op jit(solution)/shard_map/ppermute | solution.py:64
  478.7 29.4 %collective-permute-done.14.mid = bf16[768,512]{1,0:T(8,128)(2,1)S(1)} collective-permute-done((bf16[768,512]{1,0:T(8,128)(2,1)S(1)}, bf16[768,512]{1,0:T(8,128)(2,1)S(1)}, u32[]{:S(2)}, u32[]{:S(2)}) %collective-permute-start.14) | collective-permute-done | bytes 786464 | tf_op jit(solution)/shard_map/ppermute | solution.py:65
  508.1 2.4 collective-permute-start.11
  510.6 11.4 %group_product.18.rest_0_ = bf16[8192,2048]{1,0:T(8,128)(2,1)} custom-call(bf16[8192,512]{1,0:T(8,128)(2,1)S(1)} %copy-done, bf16[768,512]{1,0:T(8,128)(2,1)S(1)} %collective-permute-done.12.near, bf16[768,512]{1,0:T(8,128)(2,1)S(1)} %collective-permute-done.13.far, ...), custom_call_target="tpu_custom_call", output_to_operand_aliasing={{}: (5, {})} | custom-call | flops 6442450944 | bytes 6291456 | tf_op jit(solution)/shard_map/group_product/pallas_call | solution.py:34
  524.3 6.3 %collective-permute-done.11.mid = bf16[512,512]{1,0:T(8,128)(2,1)S(1)} collective-permute-done((bf16[512,512]{1,0:T(8,128)(2,1)S(1)}, bf16[512,512]{1,0:T(8,128)(2,1)S(1)}, u32[]{:S(2)}, u32[]{:S(2)}) %collective-permute-start.11) | collective-permute-done | bytes 524320 | tf_op jit(solution)/shard_map/ppermute | solution.py:65
  530.6 9.0 %group_product.19.rest_0_ = bf16[8192,2048]{1,0:T(8,128)(2,1)} custom-call(bf16[8192,512]{1,0:T(8,128)(2,1)S(1)} %copy-done, bf16[512,512]{1,0:T(8,128)(2,1)S(1)} %collective-permute-done.9.near, bf16[512,512]{1,0:T(8,128)(2,1)S(1)} %collective-permute-done.10.far, bf16[512,512]{1,0:T(8,128)(2,1)S(1)} %collective-permute-done.11.mid, ...), custom_call_target="tpu_custom_call", output_to_operand_aliasing={{}: (5, {})} | custom-call | flops 4294967296 | bytes 4194304 | tf_op jit(solution)/shard_map/group_product/pallas_call | solution.py:34
  541.8 6.7 %group_product.20.rest_0_ = bf16[8192,2048]{1,0:T(8,128)(2,1)} custom-call(bf16[8192,512]{1,0:T(8,128)(2,1)S(1)} %copy-done, bf16[256,512]{1,0:T(8,128)(2,1)S(1)} %collective-permute-done.6.near, bf16[256,512]{1,0:T(8,128)(2,1)S(1)} %collective-permute-done.7.far, bf16[256,512]{1,0:T(8,128)(2,1)S(1)} %collective-permute-done.8.mid, ...), custom_call_target="tpu_custom_call", output_to_operand_aliasing={{}: (5, {})} | custom-call | flops 2147483648 | bytes 2097152 | tf_op jit(solution)/shard_map/group_product/pallas_call | solution.py:34
  548.6 6.7 %group_product.21 = bf16[8192,2048]{1,0:T(8,128)(2,1)} custom-call(bf16[8192,512]{1,0:T(8,128)(2,1)S(1)} %copy-done, bf16[256,512]{1,0:T(8,128)(2,1)S(1)} %collective-permute-done.near, bf16[256,512]{1,0:T(8,128)(2,1)S(1)} %collective-permute-done.1.far, bf16[256,512]{1,0:T(8,128)(2,1)S(1)} %collective-permute-done.2.mid, ...), custom_call_target="tpu_custom_call", output_to_operand_aliasing={{}: (5, {})} | custom-call | flops 2147483648 | bytes 2097152 | tf_op jit(solution)/shard_map/group_product/pallas_call | solution.py:34
  (74 shorter events, 29.2 us)
Async XLA Ops:
  0.0 73.5 %collective-permute-start.3 = (bf16[512,2048]{1,0:T(8,128)(2,1)}, bf16[512,2048]{1,0:T(8,128)(2,1)}, u32[]{:S(2)}, u32[]{:S(2)}) collective-permute-start(bf16[512,2048]{1,0:T(8,128)(2,1)} %param.3), channel_id=1, source_target_pairs={{0,3},{1,0},{2,1},{3,2},{4,7},{5,4},{6,5},{7,6},{8,11},{9,8},{10,9... | collective-permute-start | bytes 6291464 | tf_op jit(solution)/shard_map/ppermute | solution.py:69
  0.0 93.1 %collective-permute-start.4 = (bf16[512,2048]{1,0:T(8,128)(2,1)}, bf16[512,2048]{1,0:T(8,128)(2,1)}, u32[]{:S(2)}, u32[]{:S(2)}) collective-permute-start(bf16[512,2048]{1,0:T(8,128)(2,1)} %param.3), channel_id=1, source_target_pairs={{0,2},{1,3},{2,0},{3,1},{4,6},{5,7},{6,4},{7,5},{8,10},{9,11},{10,... | collective-permute-start | bytes 6291464 | tf_op jit(solution)/shard_map/ppermute | solution.py:69
  3.4 11.0 %collective-permute-start.34 = (bf16[256,512]{1,0:T(8,128)(2,1)S(1)}, bf16[256,512]{1,0:T(8,128)(2,1)S(1)}, u32[]{:S(2)}, u32[]{:S(2)}) collective-permute-start(bf16[256,512]{1,0:T(8,128)(2,1)S(1)} %get-tuple-element.5), channel_id=1, source_target_pairs={{0,12},{4,8},{8,4},{12,0},{1,13},{5,9},{9,5},{13,1},{2,14},{6,10},... | collective-permute-start | bytes 786440 | tf_op jit(solution)/shard_map/ppermute | solution.py:64
  3.6 19.9 %collective-permute-start.33 = (bf16[256,512]{1,0:T(8,128)(2,1)S(1)}, bf16[256,512]{1,0:T(8,128)(2,1)S(1)}, u32[]{:S(2)}, u32[]{:S(2)}) collective-permute-start(bf16[256,512]{1,0:T(8,128)(2,1)S(1)} %get-tuple-element.5), channel_id=1, source_target_pairs={{0,4},{4,0},{8,12},{12,8},{1,5},{5,1},{9,13},{13,9},{2,6},{6,2},{1... | collective-permute-start | bytes 786440 | tf_op jit(solution)/shard_map/ppermute | solution.py:63
  14.4 9.9 %collective-permute-start.35 = (bf16[256,512]{1,0:T(8,128)(2,1)S(1)}, bf16[256,512]{1,0:T(8,128)(2,1)S(1)}, u32[]{:S(2)}, u32[]{:S(2)}) collective-permute-start(bf16[256,512]{1,0:T(8,128)(2,1)S(1)} %collective-permute-done.34.far), channel_id=1, source_target_pairs={{0,4},{4,0},{8,12},{12,8},{1,5},{5,1},{9,13},{13,9},{2,6},{6,2},{1... | collective-permute-start | bytes 786440 | tf_op jit(solution)/shard_map/ppermute | solution.py:65
  22.2 27.9 %collective-permute-start.31 = (bf16[1024,512]{1,0:T(8,128)(2,1)S(1)}, bf16[1024,512]{1,0:T(8,128)(2,1)S(1)}, u32[]{:S(2)}, u32[]{:S(2)}) collective-permute-start(bf16[1024,512]{1,0:T(8,128)(2,1)S(1)} %get-tuple-element.8), channel_id=1, source_target_pairs={{0,12},{4,8},{8,4},{12,0},{1,13},{5,9},{9,5},{13,1},{2,14},{6,10},... | collective-permute-start | bytes 3145736 | tf_op jit(solution)/shard_map/ppermute | solution.py:64
  24.3 48.3 %collective-permute-start.30 = (bf16[1024,512]{1,0:T(8,128)(2,1)S(1)}, bf16[1024,512]{1,0:T(8,128)(2,1)S(1)}, u32[]{:S(2)}, u32[]{:S(2)}) collective-permute-start(bf16[1024,512]{1,0:T(8,128)(2,1)S(1)} %get-tuple-element.8), channel_id=1, source_target_pairs={{0,4},{4,0},{8,12},{12,8},{1,5},{5,1},{9,13},{13,9},{2,6},{6,2},{1... | collective-permute-start | bytes 3145736 | tf_op jit(solution)/shard_map/ppermute | solution.py:63
  25.0 112.5 %collective-permute-start.5 = (bf16[512,2048]{1,0:T(8,128)(2,1)}, bf16[512,2048]{1,0:T(8,128)(2,1)}, u32[]{:S(2)}, u32[]{:S(2)}) collective-permute-start(bf16[512,2048]{1,0:T(8,128)(2,1)} %param.3), channel_id=1, source_target_pairs={{0,1},{1,2},{2,3},{3,0},{4,5},{5,6},{6,7},{7,4},{8,9},{9,10},{10,1... | collective-permute-start | bytes 6291464 | tf_op jit(solution)/shard_map/ppermute | solution.py:69
  50.1 61.5 %collective-permute-start.28 = (bf16[1024,512]{1,0:T(8,128)(2,1)}, bf16[1024,512]{1,0:T(8,128)(2,1)S(1)}, u32[]{:S(2)}, u32[]{:S(2)}) collective-permute-start(bf16[1024,512]{1,0:T(8,128)(2,1)} %get-tuple-element.9), channel_id=1, source_target_pairs={{0,12},{4,8},{8,4},{12,0},{1,13},{5,9},{9,5},{13,1},{2,14},{6,10},... | collective-permute-start | bytes 3145736 | tf_op jit(solution)/shard_map/ppermute | solution.py:64
  73.5 61.1 %collective-permute-start.27 = (bf16[1024,512]{1,0:T(8,128)(2,1)}, bf16[1024,512]{1,0:T(8,128)(2,1)S(1)}, u32[]{:S(2)}, u32[]{:S(2)}) collective-permute-start(bf16[1024,512]{1,0:T(8,128)(2,1)} %get-tuple-element.9), channel_id=1, source_target_pairs={{0,4},{4,0},{8,12},{12,8},{1,5},{5,1},{9,13},{13,9},{2,6},{6,2},{1... | collective-permute-start | bytes 3145736 | tf_op jit(solution)/shard_map/ppermute | solution.py:63
  73.5 77.4 %collective-permute-start.25 = (bf16[1024,512]{1,0:T(8,128)(2,1)}, bf16[1024,512]{1,0:T(8,128)(2,1)}, u32[]{:S(2)}, u32[]{:S(2)}) collective-permute-start(bf16[1024,512]{1,0:T(8,128)(2,1)} %get-tuple-element.10), channel_id=1, source_target_pairs={{0,12},{4,8},{8,4},{12,0},{1,13},{5,9},{9,5},{13,1},{2,14},{6,10},... | collective-permute-start | bytes 3145736 | tf_op jit(solution)/shard_map/ppermute | solution.py:64
  93.1 66.8 %collective-permute-start.32 = (bf16[1024,512]{1,0:T(8,128)(2,1)S(1)}, bf16[1024,512]{1,0:T(8,128)(2,1)}, u32[]{:S(2)}, u32[]{:S(2)}) collective-permute-start(bf16[1024,512]{1,0:T(8,128)(2,1)S(1)} %collective-permute-done.31.far), channel_id=1, source_target_pairs={{0,4},{4,0},{8,12},{12,8},{1,5},{5,1},{9,13},{13,9},{2,6},{6,2},{1... | collective-permute-start | bytes 3145736 | tf_op jit(solution)/shard_map/ppermute | solution.py:65
  105.1 6.5 %copy-start.10 = (bf16[1024,512]{1,0:T(8,128)(2,1)S(1)}, bf16[1024,512]{1,0:T(8,128)(2,1)}, u32[]{:S(2)}) copy-start(bf16[1024,512]{1,0:T(8,128)(2,1)} %get-tuple-element.10) | copy-start | bytes 3145732
  105.1 29.6 %copy-start.9 = (bf16[1024,512]{1,0:T(8,128)(2,1)S(1)}, bf16[1024,512]{1,0:T(8,128)(2,1)}, u32[]{:S(2)}) copy-start(bf16[1024,512]{1,0:T(8,128)(2,1)} %get-tuple-element.11) | copy-start | bytes 3145732
  105.1 35.7 %copy-start.4 = (bf16[256,512]{1,0:T(8,128)(2,1)S(1)}, bf16[256,512]{1,0:T(8,128)(2,1)}, u32[]{:S(2)}) copy-start(bf16[256,512]{1,0:T(8,128)(2,1)} %copy-done.3) | copy-start | bytes 786436
  105.1 35.7 %copy-start.6 = (bf16[256,512]{1,0:T(8,128)(2,1)S(1)}, bf16[256,512]{1,0:T(8,128)(2,1)}, u32[]{:S(2)}) copy-start(bf16[256,512]{1,0:T(8,128)(2,1)} %copy-done.5) | copy-start | bytes 786436
  111.6 73.5 %collective-permute-start.24 = (bf16[1024,512]{1,0:T(8,128)(2,1)S(1)}, bf16[1024,512]{1,0:T(8,128)(2,1)S(1)}, u32[]{:S(2)}, u32[]{:S(2)}) collective-permute-start(bf16[1024,512]{1,0:T(8,128)(2,1)S(1)} %copy-done.10), channel_id=1, source_target_pairs={{0,4},{4,0},{8,12},{12,8},{1,5},{5,1},{9,13},{13,9},{2,6},{6,2},{1... | collective-permute-start | bytes 3145736 | tf_op jit(solution)/shard_map/ppermute | solution.py:63
  134.6 72.9 %collective-permute-start.22 = (bf16[1024,512]{1,0:T(8,128)(2,1)S(1)}, bf16[1024,512]{1,0:T(8,128)(2,1)S(1)}, u32[]{:S(2)}, u32[]{:S(2)}) collective-permute-start(bf16[1024,512]{1,0:T(8,128)(2,1)S(1)} %copy-done.9), channel_id=1, source_target_pairs={{0,12},{4,8},{8,4},{12,0},{1,13},{5,9},{9,5},{13,1},{2,14},{6,10},... | collective-permute-start | bytes 3145736 | tf_op jit(solution)/shard_map/ppermute | solution.py:64
  137.5 92.6 %collective-permute-start.29 = (bf16[1024,512]{1,0:T(8,128)(2,1)S(1)}, bf16[1024,512]{1,0:T(8,128)(2,1)S(1)}, u32[]{:S(2)}, u32[]{:S(2)}) collective-permute-start(bf16[1024,512]{1,0:T(8,128)(2,1)S(1)} %collective-permute-done.28.far), channel_id=1, source_target_pairs={{0,4},{4,0},{8,12},{12,8},{1,5},{5,1},{9,13},{13,9},{2,6},{6,2},{1... | collective-permute-start | bytes 3145736 | tf_op jit(solution)/shard_map/ppermute | solution.py:65
  140.7 3.4 copy-start
  144.1 6.9 %copy-start.8 = (bf16[1024,512]{1,0:T(8,128)(2,1)S(1)}, bf16[1024,512]{1,0:T(8,128)(2,1)}, u32[]{:S(2)}) copy-start(bf16[1024,512]{1,0:T(8,128)(2,1)} %get-tuple-element.12) | copy-start | bytes 3145732
  144.1 18.1 %copy-start.2 = (bf16[1024,512]{1,0:T(8,128)(2,1)S(1)}, bf16[1024,512]{1,0:T(8,128)(2,1)}, u32[]{:S(2)}) copy-start(bf16[1024,512]{1,0:T(8,128)(2,1)} %copy-done.1) | copy-start | bytes 3145732
  151.0 56.5 %copy-start.7 = (bf16[1024,512]{1,0:T(8,128)(2,1)S(1)}, bf16[1024,512]{1,0:T(8,128)(2,1)}, u32[]{:S(2)}) copy-start(bf16[1024,512]{1,0:T(8,128)(2,1)} %get-tuple-element.13) | copy-start | bytes 3145732
  151.0 101.5 %collective-permute-start.19 = (bf16[1024,512]{1,0:T(8,128)(2,1)S(1)}, bf16[1024,512]{1,0:T(8,128)(2,1)S(1)}, u32[]{:S(2)}, u32[]{:S(2)}) collective-permute-start(bf16[1024,512]{1,0:T(8,128)(2,1)S(1)} %copy-done.8), channel_id=1, source_target_pairs={{0,12},{4,8},{8,4},{12,0},{1,13},{5,9},{9,5},{13,1},{2,14},{6,10},... | collective-permute-start | bytes 3145736 | tf_op jit(solution)/shard_map/ppermute | solution.py:64
  159.9 112.2 %collective-permute-start.26 = (bf16[1024,512]{1,0:T(8,128)(2,1)}, bf16[1024,512]{1,0:T(8,128)(2,1)S(1)}, u32[]{:S(2)}, u32[]{:S(2)}) collective-permute-start(bf16[1024,512]{1,0:T(8,128)(2,1)} %collective-permute-done.25.far), channel_id=1, source_target_pairs={{0,4},{4,0},{8,12},{12,8},{1,5},{5,1},{9,13},{13,9},{2,6},{6,2},{1... | collective-permute-start | bytes 3145736 | tf_op jit(solution)/shard_map/ppermute | solution.py:65
  185.1 112.3 %collective-permute-start.21 = (bf16[1024,512]{1,0:T(8,128)(2,1)S(1)}, bf16[1024,512]{1,0:T(8,128)(2,1)S(1)}, u32[]{:S(2)}, u32[]{:S(2)}) collective-permute-start(bf16[1024,512]{1,0:T(8,128)(2,1)S(1)} %copy-done.9), channel_id=1, source_target_pairs={{0,4},{4,0},{8,12},{12,8},{1,5},{5,1},{9,13},{13,9},{2,6},{6,2},{1... | collective-permute-start | bytes 3145736 | tf_op jit(solution)/shard_map/ppermute | solution.py:63
  207.5 112.5 %collective-permute-start.16 = (bf16[1024,512]{1,0:T(8,128)(2,1)S(1)}, bf16[1024,512]{1,0:T(8,128)(2,1)S(1)}, u32[]{:S(2)}, u32[]{:S(2)}) collective-permute-start(bf16[1024,512]{1,0:T(8,128)(2,1)S(1)} %copy-done.7), channel_id=1, source_target_pairs={{0,12},{4,8},{8,4},{12,0},{1,13},{5,9},{9,5},{13,1},{2,14},{6,10},... | collective-permute-start | bytes 3145736 | tf_op jit(solution)/shard_map/ppermute | solution.py:64
  230.0 109.6 %collective-permute-start.23 = (bf16[1024,512]{1,0:T(8,128)(2,1)S(1)}, bf16[1024,512]{1,0:T(8,128)(2,1)S(1)}, u32[]{:S(2)}, u32[]{:S(2)}) collective-permute-start(bf16[1024,512]{1,0:T(8,128)(2,1)S(1)} %collective-permute-done.22.far), channel_id=1, source_target_pairs={{0,4},{4,0},{8,12},{12,8},{1,5},{5,1},{9,13},{13,9},{2,6},{6,2},{1... | collective-permute-start | bytes 3145736 | tf_op jit(solution)/shard_map/ppermute | solution.py:65
  243.7 76.3 %copy-start.11 = (bf16[768,512]{1,0:T(8,128)(2,1)S(1)}, bf16[768,512]{1,0:T(8,128)(2,1)}, u32[]{:S(2)}) copy-start(bf16[768,512]{1,0:T(8,128)(2,1)} %slice.36) | copy-start | bytes 2359300
  252.5 109.5 %collective-permute-start.18 = (bf16[1024,512]{1,0:T(8,128)(2,1)S(1)}, bf16[1024,512]{1,0:T(8,128)(2,1)S(1)}, u32[]{:S(2)}, u32[]{:S(2)}) collective-permute-start(bf16[1024,512]{1,0:T(8,128)(2,1)S(1)} %copy-done.8), channel_id=1, source_target_pairs={{0,4},{4,0},{8,12},{12,8},{1,5},{5,1},{9,13},{13,9},{2,6},{6,2},{1... | collective-permute-start | bytes 3145736 | tf_op jit(solution)/shard_map/ppermute | solution.py:63
  272.2 112.4 %collective-permute-start.20 = (bf16[1024,512]{1,0:T(8,128)(2,1)S(1)}, bf16[1024,512]{1,0:T(8,128)(2,1)S(1)}, u32[]{:S(2)}, u32[]{:S(2)}) collective-permute-start(bf16[1024,512]{1,0:T(8,128)(2,1)S(1)} %collective-permute-done.19.far), channel_id=1, source_target_pairs={{0,4},{4,0},{8,12},{12,8},{1,5},{5,1},{9,13},{13,9},{2,6},{6,2},{1... | collective-permute-start | bytes 3145736 | tf_op jit(solution)/shard_map/ppermute | solution.py:65
  288.4 96.2 %copy-start.12 = (bf16[512,512]{1,0:T(8,128)(2,1)S(1)}, bf16[512,512]{1,0:T(8,128)(2,1)}, u32[]{:S(2)}) copy-start(bf16[512,512]{1,0:T(8,128)(2,1)} %slice.35) | copy-start | bytes 1572868
  297.4 129.4 %collective-permute-start.15 = (bf16[1024,512]{1,0:T(8,128)(2,1)S(1)}, bf16[1024,512]{1,0:T(8,128)(2,1)S(1)}, u32[]{:S(2)}, u32[]{:S(2)}) collective-permute-start(bf16[1024,512]{1,0:T(8,128)(2,1)S(1)} %copy-done.7), channel_id=1, source_target_pairs={{0,4},{4,0},{8,12},{12,8},{1,5},{5,1},{9,13},{13,9},{2,6},{6,2},{1... | collective-permute-start | bytes 3145736 | tf_op jit(solution)/shard_map/ppermute | solution.py:63
  320.0 106.7 %collective-permute-start.13 = (bf16[768,512]{1,0:T(8,128)(2,1)S(1)}, bf16[768,512]{1,0:T(8,128)(2,1)S(1)}, u32[]{:S(2)}, u32[]{:S(2)}) collective-permute-start(bf16[768,512]{1,0:T(8,128)(2,1)S(1)} %copy-done.11), channel_id=1, source_target_pairs={{0,12},{4,8},{8,4},{12,0},{1,13},{5,9},{9,5},{13,1},{2,14},{6,10},... | collective-permute-start | bytes 2359304 | tf_op jit(solution)/shard_map/ppermute | solution.py:64
  339.6 106.7 %collective-permute-start.17 = (bf16[1024,512]{1,0:T(8,128)(2,1)S(1)}, bf16[1024,512]{1,0:T(8,128)(2,1)S(1)}, u32[]{:S(2)}, u32[]{:S(2)}) collective-permute-start(bf16[1024,512]{1,0:T(8,128)(2,1)S(1)} %collective-permute-done.16.far), channel_id=1, source_target_pairs={{0,4},{4,0},{8,12},{12,8},{1,5},{5,1},{9,13},{13,9},{2,6},{6,2},{1... | collective-permute-start | bytes 3145736 | tf_op jit(solution)/shard_map/ppermute | solution.py:65
  355.7 71.0 %copy-start.14 = (bf16[256,512]{1,0:T(8,128)(2,1)S(1)}, bf16[256,512]{1,0:T(8,128)(2,1)}, u32[]{:S(2)}) copy-start(bf16[256,512]{1,0:T(8,128)(2,1)} %get-tuple-element.6) | copy-start | bytes 786436
  362.1 115.3 %collective-permute-start.12 = (bf16[768,512]{1,0:T(8,128)(2,1)S(1)}, bf16[768,512]{1,0:T(8,128)(2,1)S(1)}, u32[]{:S(2)}, u32[]{:S(2)}) collective-permute-start(bf16[768,512]{1,0:T(8,128)(2,1)S(1)} %copy-done.11), channel_id=1, source_target_pairs={{0,4},{4,0},{8,12},{12,8},{1,5},{5,1},{9,13},{13,9},{2,6},{6,2},{1... | collective-permute-start | bytes 2359304 | tf_op jit(solution)/shard_map/ppermute | solution.py:63
  384.5 92.8 %collective-permute-start.10 = (bf16[512,512]{1,0:T(8,128)(2,1)S(1)}, bf16[512,512]{1,0:T(8,128)(2,1)S(1)}, u32[]{:S(2)}, u32[]{:S(2)}) collective-permute-start(bf16[512,512]{1,0:T(8,128)(2,1)S(1)} %copy-done.12), channel_id=1, source_target_pairs={{0,12},{4,8},{8,4},{12,0},{1,13},{5,9},{9,5},{13,1},{2,14},{6,10},... | collective-permute-start | bytes 1572872 | tf_op jit(solution)/shard_map/ppermute | solution.py:64
  426.8 97.2 %collective-permute-start.9 = (bf16[512,512]{1,0:T(8,128)(2,1)S(1)}, bf16[512,512]{1,0:T(8,128)(2,1)S(1)}, u32[]{:S(2)}, u32[]{:S(2)}) collective-permute-start(bf16[512,512]{1,0:T(8,128)(2,1)S(1)} %copy-done.12), channel_id=1, source_target_pairs={{0,4},{4,0},{8,12},{12,8},{1,5},{5,1},{9,13},{13,9},{2,6},{6,2},{1... | collective-permute-start | bytes 1572872 | tf_op jit(solution)/shard_map/ppermute | solution.py:63
  426.8 50.6 %copy-start.13 = (bf16[256,512]{1,0:T(8,128)(2,1)S(1)}, bf16[256,512]{1,0:T(8,128)(2,1)}, u32[]{:S(2)}) copy-start(bf16[256,512]{1,0:T(8,128)(2,1)} %get-tuple-element.7) | copy-start | bytes 786436
  426.8 95.2 %collective-permute-start.7 = (bf16[256,512]{1,0:T(8,128)(2,1)S(1)}, bf16[256,512]{1,0:T(8,128)(2,1)S(1)}, u32[]{:S(2)}, u32[]{:S(2)}) collective-permute-start(bf16[256,512]{1,0:T(8,128)(2,1)S(1)} %copy-done.14), channel_id=1, source_target_pairs={{0,12},{4,8},{8,4},{12,0},{1,13},{5,9},{9,5},{13,1},{2,14},{6,10},... | collective-permute-start | bytes 786440 | tf_op jit(solution)/shard_map/ppermute | solution.py:64
  446.3 61.8 %collective-permute-start.14 = (bf16[768,512]{1,0:T(8,128)(2,1)S(1)}, bf16[768,512]{1,0:T(8,128)(2,1)S(1)}, u32[]{:S(2)}, u32[]{:S(2)}) collective-permute-start(bf16[768,512]{1,0:T(8,128)(2,1)S(1)} %collective-permute-done.13.far), channel_id=1, source_target_pairs={{0,4},{4,0},{8,12},{12,8},{1,5},{5,1},{9,13},{13,9},{2,6},{6,2},{1... | collective-permute-start | bytes 2359304 | tf_op jit(solution)/shard_map/ppermute | solution.py:65
  477.3 62.3 %collective-permute-start.6 = (bf16[256,512]{1,0:T(8,128)(2,1)S(1)}, bf16[256,512]{1,0:T(8,128)(2,1)S(1)}, u32[]{:S(2)}, u32[]{:S(2)}) collective-permute-start(bf16[256,512]{1,0:T(8,128)(2,1)S(1)} %copy-done.14), channel_id=1, source_target_pairs={{0,4},{4,0},{8,12},{12,8},{1,5},{5,1},{9,13},{13,9},{2,6},{6,2},{1... | collective-permute-start | bytes 786440 | tf_op jit(solution)/shard_map/ppermute | solution.py:63
  477.3 44.9 %collective-permute-start.1 = (bf16[256,512]{1,0:T(8,128)(2,1)S(1)}, bf16[256,512]{1,0:T(8,128)(2,1)S(1)}, u32[]{:S(2)}, u32[]{:S(2)}) collective-permute-start(bf16[256,512]{1,0:T(8,128)(2,1)S(1)} %copy-done.13), channel_id=1, source_target_pairs={{0,12},{4,8},{8,4},{12,0},{1,13},{5,9},{9,5},{13,1},{2,14},{6,10},... | collective-permute-start | bytes 786440 | tf_op jit(solution)/shard_map/ppermute | solution.py:64
  508.1 22.5 %collective-permute-start.11 = (bf16[512,512]{1,0:T(8,128)(2,1)S(1)}, bf16[512,512]{1,0:T(8,128)(2,1)S(1)}, u32[]{:S(2)}, u32[]{:S(2)}) collective-permute-start(bf16[512,512]{1,0:T(8,128)(2,1)S(1)} %collective-permute-done.10.far), channel_id=1, source_target_pairs={{0,4},{4,0},{8,12},{12,8},{1,5},{5,1},{9,13},{13,9},{2,6},{6,2},{1... | collective-permute-start | bytes 1572872 | tf_op jit(solution)/shard_map/ppermute | solution.py:65
  521.9 26.6 %collective-permute-start = (bf16[256,512]{1,0:T(8,128)(2,1)S(1)}, bf16[256,512]{1,0:T(8,128)(2,1)S(1)}, u32[]{:S(2)}, u32[]{:S(2)}) collective-permute-start(bf16[256,512]{1,0:T(8,128)(2,1)S(1)} %copy-done.13), channel_id=1, source_target_pairs={{0,4},{4,0},{8,12},{12,8},{1,5},{5,1},{9,13},{13,9},{2,6},{6,2},{1... | collective-permute-start | bytes 786440 | tf_op jit(solution)/shard_map/ppermute | solution.py:63
  522.3 19.6 %collective-permute-start.8 = (bf16[256,512]{1,0:T(8,128)(2,1)S(1)}, bf16[256,512]{1,0:T(8,128)(2,1)S(1)}, u32[]{:S(2)}, u32[]{:S(2)}) collective-permute-start(bf16[256,512]{1,0:T(8,128)(2,1)S(1)} %collective-permute-done.7.far), channel_id=1, source_target_pairs={{0,4},{4,0},{8,12},{12,8},{1,5},{5,1},{9,13},{13,9},{2,6},{6,2},{1... | collective-permute-start | bytes 786440 | tf_op jit(solution)/shard_map/ppermute | solution.py:65
  524.0 24.6 %collective-permute-start.2 = (bf16[256,512]{1,0:T(8,128)(2,1)S(1)}, bf16[256,512]{1,0:T(8,128)(2,1)S(1)}, u32[]{:S(2)}, u32[]{:S(2)}) collective-permute-start(bf16[256,512]{1,0:T(8,128)(2,1)S(1)} %collective-permute-done.1.far), channel_id=1, source_target_pairs={{0,4},{4,0},{8,12},{12,8},{1,5},{5,1},{9,13},{13,9},{2,6},{6,2},{1... | collective-permute-start | bytes 786440 | tf_op jit(solution)/shard_map/ppermute | solution.py:65
  (3 other events, 2.4 us)
where the time goes:
time: 561 us; the launch traced here: 555 us
  waiting for transfers between devices  354 us (63%)
  Pallas kernels  123 us (22%)
  starting transfers between devices  44.1 us (8%)
  local copies, waits for them, and re-layouts  34.3 us (6%)
    ppermute x11, waiting for transfers between devices, local(): mid = [lax.ppermute(x, 'col', with_near) for x in far]  143 us
    ppermute x11, waiting for transfers between devices, local(): far = [lax.ppermute(x, 'col', with_far) for x in parts]  130 us
    pallas_call x11, Pallas kernels, _group_product(): pl.pallas_call(_mm_kernel, grid=(size // bm,), out_shape=jax.ShapeDtypeSt...  123 us
    ppermute x11, waiting for transfers between devices, local(): near = [lax.ppermute(x, 'col', with_near) for x in parts]  62.8 us
    ppermute x3, waiting for transfers between devices, local(): lax.ppermute(b_own, 'row', [(p, (p - s) % side) for p in range(side)])  17.6 us
    ppermute x11, starting transfers between devices, local(): mid = [lax.ppermute(x, 'col', with_near) for x in far]  17 us
    ppermute x11, starting transfers between devices, local(): far = [lax.ppermute(x, 'col', with_far) for x in parts]  16.7 us
    dynamic_update_slice x4, local copies, waits for them, and re-layouts, local(): b = lax.dynamic_update_slice_in_dim(b, blk, (rel ^ rel // 2) * depth, 0)  12.9 us
  transfers between devices with their start and end apart: 36, of which 23 were waited for; matrix products, arithmetic and copies ran while one was open for 5% of the time, Pallas kernels for 21%

commit v1 on v0

v1 whole, which is shorter than its diff:
```python
import jax
import jax.numpy as jnp
from jax import lax
from jax.experimental import pallas as pl
from jax.experimental.pallas import tpu as pltpu
from jax.sharding import PartitionSpec as P


GROUPS = (256, 1024, 1024, 1024, 1024, 1024, 1024, 768, 512, 256, 128, 128)
BM = 256


def _mm_kernel(own, near, far, mid, b_ref, *rest):
    out_ref = rest[-1]
    lhs = jnp.concatenate([own[...], near[...], far[...], mid[...]], axis=1)
    out_ref[...] = jnp.dot(lhs, b_ref[...], preferred_element_type=jnp.float32).astype(out_ref.dtype)


def _group_product(own, near, far, mid, b, c, rows, cols, off, size):
    bm = BM if size > BM else BM // 2
    depth = own.shape[1]
    total = b.shape[0]
    piece = pl.BlockSpec((bm, depth), lambda i: (i, 0))
    whole = pl.BlockSpec((total, cols), lambda i: (0, 0), pipeline_mode=pl.Buffered(1))
    out = pl.BlockSpec((bm, cols), lambda i: (off // bm + i, 0))
    in_specs = [piece, piece, piece, piece, whole]
    args = [own, near, far, mid, b]
    alias = {}
    if c is not None:
        in_specs.append(pl.BlockSpec(memory_space=pl.ANY))
        args.append(c)
        alias = {5: 0}
    return pl.pallas_call(
        _mm_kernel,
        grid=(size // bm,),
        out_shape=jax.ShapeDtypeStruct((rows, cols), jnp.bfloat16),
        in_specs=in_specs,
        out_specs=out,
        input_output_aliases=alias,
        compiler_params=pltpu.CompilerParams(dimension_semantics=("arbitrary",), vmem_limit_bytes=20 * 2**20),
        cost_estimate=pl.CostEstimate(
            flops=2 * size * total * cols,
            bytes_accessed=size * (total + cols) * 2,
            transcendentals=0,
        ),
        name="group_product",
    )(*args)


def _stack_kernel(place_ref, *refs):
    sems = refs[-1]
    out_ref = refs[-2]
    depth = refs[0].shape[0]
    copies = [
        pltpu.make_async_copy(ref, out_ref.at[pl.ds(pl.multiple_of(place_ref[s] * depth, depth), depth)], sems.at[s])
        for s, ref in enumerate(refs[:-2])
    ]
    for copy in copies:
        copy.start()
    for copy in copies:
        copy.wait()


def _stack_blocks(places, blocks):
    count = len(blocks)
    depth, cols = blocks[0].shape
    return pl.pallas_call(
        _stack_kernel,
        out_shape=pltpu.VMEM((count * depth, cols), blocks[0].dtype),
        in_specs=[pl.BlockSpec(memory_space=pltpu.SMEM)] + [pl.BlockSpec(memory_space=pl.ANY)] * count,
        out_specs=pl.BlockSpec(memory_space=pltpu.VMEM),
        scratch_shapes=[pltpu.SemaphoreType.DMA((count,))],
        cost_estimate=pl.CostEstimate(flops=2**20, bytes_accessed=2 * count * depth * cols * 2, transcendentals=0),
        compiler_params=pltpu.CompilerParams(vmem_limit_bytes=12 * 2**20),
        name="stack_blocks",
    )(places, *blocks)


def solution(mesh):
    side = mesh.shape["row"]
    with_near = [(p, p ^ 1) for p in range(side)]
    with_far = [(p, side - 1 - p) for p in range(side)]

    def local(a, b_own):
        rows, _ = a.shape
        cols = b_own.shape[1]
        offs = [sum(GROUPS[:g]) for g in range(len(GROUPS))]
        row_pos, col_pos = lax.axis_index("row"), lax.axis_index("col")

        parts = [lax.slice_in_dim(a, o, o + s) for o, s in zip(offs, GROUPS)]
        near = [lax.ppermute(x, "col", with_near) for x in parts]
        far = [lax.ppermute(x, "col", with_far) for x in parts]
        mid = [lax.ppermute(x, "col", with_near) for x in far]

        blocks = [b_own] + [
            lax.ppermute(b_own, "row", [(p, (p - s) % side) for p in range(side)]) for s in range(1, side)
        ]
        rels = [lax.rem(row_pos + s, side) ^ col_pos for s in range(side)]
        b = _stack_blocks(jnp.stack([rel ^ (rel // 2) for rel in rels]), blocks)

        c = None
        for g, (off, size) in enumerate(zip(offs, GROUPS)):
            c = _group_product(parts[g], near[g], far[g], mid[g], b, c, rows, cols, off, size)
        return c

    return jax.shard_map(
        local, mesh=mesh, in_specs=(P(("dp", "row"), "col"), P("row", "col")),
        out_specs=P(("dp", "row"), "col"), check_vma=False,
    )
```

time: 561 us -> 558 us (level)
  waiting for transfers between devices: 354 us -> 402 us
  Pallas kernels: 123 us -> 92 us
  local copies, waits for them, and re-layouts: 34.3 us -> 20.5 us
    pallas_call x11 -> x12, Pallas kernels: 123 us -> 88.4 us  [_group_product(): pl.pallas_call(_mm_kernel, grid=(size // bm,), out_shape=jax.ShapeDtypeSt...]
    ppermute x11 -> x12, waiting for transfers between devices: 130 us -> 153 us  [local(): far = [lax.ppermute(x, 'col', with_far) for x in parts]]
    dynamic_update_slice x4 -> x0, local copies, waits for them, and re-layouts: 12.9 us -> none  [local(): b = lax.dynamic_update_slice_in_dim(b, blk, (rel ^ rel // 2) * depth, 0)]
    ppermute x3, waiting for transfers between devices: 17.6 us -> 30.1 us  [local(): lax.ppermute(b_own, 'row', [(p, (p - s) % side) for p in range(side)])]
    ppermute x11 -> x12, waiting for transfers between devices: 143 us -> 152 us  [local(): mid = [lax.ppermute(x, 'col', with_near) for x in far]]
    ppermute x11 -> x12, starting transfers between devices: 17 us -> 9.49 us  [local(): mid = [lax.ppermute(x, 'col', with_near) for x in far]]
    ppermute x11 -> x12, starting transfers between devices: 16.7 us -> 22 us  [local(): far = [lax.ppermute(x, 'col', with_far) for x in parts]]
    ppermute x11 -> x12, waiting for transfers between devices: 62.8 us -> 66.9 us  [local(): near = [lax.ppermute(x, 'col', with_near) for x in parts]]
  transfers between devices with their start and end apart: 36 -> 39, of which waited for: 23 -> 24; matrix products, arithmetic and copies ran while one was open for 5% -> 1% of each run, Pallas kernels for 21% -> 16%
where the time goes in v1:
time: 558 us; the launch traced here: 554 us
  waiting for transfers between devices  402 us (72%)
  Pallas kernels  92 us (16%)
  starting transfers between devices  39.8 us (7%)
  local copies, waits for them, and re-layouts  20.5 us (4%)
    ppermute x12, waiting for transfers between devices, local(): far = [lax.ppermute(x, 'col', with_far) for x in parts]  153 us
    ppermute x12, waiting for transfers between devices, local(): mid = [lax.ppermute(x, 'col', with_near) for x in far]  152 us
    pallas_call x12, Pallas kernels, _group_product(): pl.pallas_call(_mm_kernel, grid=(size // bm,), out_shape=jax.ShapeDtypeSt...  88.4 us
    ppermute x12, waiting for transfers between devices, local(): near = [lax.ppermute(x, 'col', with_near) for x in parts]  66.9 us
    ppermute x3, waiting for transfers between devices, local(): lax.ppermute(b_own, 'row', [(p, (p - s) % side) for p in range(side)])  30.1 us
    ppermute x12, starting transfers between devices, local(): far = [lax.ppermute(x, 'col', with_far) for x in parts]  22 us
  transfers between devices with their start and end apart: 39, of which 24 were waited for; matrix products, arithmetic and copies ran while one was open for 1% of the time, Pallas kernels for 16%

profile of v1, /device:TPU:28, one launch (start us, length us, event | category | flops | bytes accessed | tf_op | source)
XLA Modules:
  0.0 554.2 jit_solution(3130124969735000472)
XLA Ops:
  0.0 4.2 fusion.1
  7.1 3.0 collective-permute-start.37
  12.0 48.2 %collective-permute-done.37.far = bf16[256,512]{1,0:T(8,128)(2,1)S(1)} collective-permute-done((bf16[256,512]{1,0:T(8,128)(2,1)S(1)}, bf16[256,512]{1,0:T(8,128)(2,1)S(1)}, u32[]{:S(2)}, u32[]{:S(2)}) %collective-permute-start.37) | collective-permute-done | bytes 262176 | tf_op jit(solution)/shard_map/ppermute | solution.py:92
  60.1 3.1 collective-permute-start.38
  65.2 3.5 collective-permute-done.38.mid
  69.4 1.9 collective-permute-start.31
  73.1 24.2 %collective-permute-done.31.far = bf16[1024,512]{1,0:T(8,128)(2,1)S(1)} collective-permute-done((bf16[1024,512]{1,0:T(8,128)(2,1)S(1)}, bf16[1024,512]{1,0:T(8,128)(2,1)S(1)}, u32[]{:S(2)}, u32[]{:S(2)}) %collective-permute-start.31) | collective-permute-done | bytes 1048608 | tf_op jit(solution)/shard_map/ppermute | solution.py:92
  97.3 1.9 collective-permute-start.28
  99.2 20.6 %collective-permute-done.30.near = bf16[1024,512]{1,0:T(8,128)(2,1)S(1)} collective-permute-done((bf16[1024,512]{1,0:T(8,128)(2,1)S(1)}, bf16[1024,512]{1,0:T(8,128)(2,1)S(1)}, u32[]{:S(2)}, u32[]{:S(2)}) %collective-permute-start.30) | collective-permute-done | bytes 1048608 | tf_op jit(solution)/shard_map/ppermute | solution.py:91
  121.3 1.9 fusion.2
  124.7 29.8 %collective-permute-done.4.refs_2_ = bf16[512,2048]{1,0:T(8,128)(2,1)} collective-permute-done((bf16[512,2048]{1,0:T(8,128)(2,1)}, bf16[512,2048]{1,0:T(8,128)(2,1)}, u32[]{:S(2)}, u32[]{:S(2)}) %collective-permute-start.4) | collective-permute-done | bytes 2097184 | tf_op jit(solution)/shard_map/ppermute | solution.py:96
  158.6 1.6 copy-done.4
  160.2 3.6 stack_blocks.1.b_ref
  167.6 3.3 group_product.12.rest_0_
  171.0 2.1 collective-permute-start.22
  174.2 11.4 %group_product.13.rest_0_ = bf16[8192,2048]{1,0:T(8,128)(2,1)} custom-call(bf16[1024,512]{1,0:T(8,128)(2,1)S(1)} %copy-done.3, bf16[1024,512]{1,0:T(8,128)(2,1)S(1)} %copy-done.6, bf16[1024,512]{1,0:T(8,128)(2,1)} %collective-permute-done.34.far, bf16[1024,512]{1,0:T(8,128)(2,1)} %collective-permute-done.35.mid, ...), custom_call_target="tpu_custom_call", output_to_operand_aliasing={{}: (5, {})} | custom-call | flops 8589934592 | bytes 8388608 | tf_op jit(solution)/shard_map/group_product/pallas_call | solution.py:33
  185.6 23.6 %collective-permute-done.27.near = bf16[1024,512]{1,0:T(8,128)(2,1)S(1)} collective-permute-done((bf16[1024,512]{1,0:T(8,128)(2,1)}, bf16[1024,512]{1,0:T(8,128)(2,1)S(1)}, u32[]{:S(2)}, u32[]{:S(2)}) %collective-permute-start.27) | collective-permute-done | bytes 1048608 | tf_op jit(solution)/shard_map/ppermute | solution.py:91
  209.8 1.9 collective-permute-start.19
  211.7 20.6 %collective-permute-done.32.mid = bf16[1024,512]{1,0:T(8,128)(2,1)S(1)} collective-permute-done((bf16[1024,512]{1,0:T(8,128)(2,1)}, bf16[1024,512]{1,0:T(8,128)(2,1)S(1)}, u32[]{:S(2)}, u32[]{:S(2)}) %collective-permute-start.32) | collective-permute-done | bytes 1048608 | tf_op jit(solution)/shard_map/ppermute | solution.py:93
  232.4 10.3 %group_product.14.rest_0_ = bf16[8192,2048]{1,0:T(8,128)(2,1)} custom-call(bf16[1024,512]{1,0:T(8,128)(2,1)S(1)} %copy-done.1, bf16[1024,512]{1,0:T(8,128)(2,1)S(1)} %copy-done.10, bf16[1024,512]{1,0:T(8,128)(2,1)S(1)} %copy-done.8, bf16[1024,512]{1,0:T(8,128)(2,1)S(1)} %collective-permute-done.32.mid, ...), custom_call_target="tpu_custom_call", output_to_operand_aliasing={{}: (5, {})} | custom-call | flops 8589934592 | bytes 8388608 | tf_op jit(solution)/shard_map/group_product/pallas_call | solution.py:33
  242.7 12.1 %collective-permute-done.22.far = bf16[1024,512]{1,0:T(8,128)(2,1)S(1)} collective-permute-done((bf16[1024,512]{1,0:T(8,128)(2,1)S(1)}, bf16[1024,512]{1,0:T(8,128)(2,1)S(1)}, u32[]{:S(2)}, u32[]{:S(2)}) %collective-permute-start.22) | collective-permute-done | bytes 1048608 | tf_op jit(solution)/shard_map/ppermute | solution.py:92
  254.8 22.1 %collective-permute-done.29.mid = bf16[1024,512]{1,0:T(8,128)(2,1)S(1)} collective-permute-done((bf16[1024,512]{1,0:T(8,128)(2,1)}, bf16[1024,512]{1,0:T(8,128)(2,1)S(1)}, u32[]{:S(2)}, u32[]{:S(2)}) %collective-permute-start.29) | collective-permute-done | bytes 1048608 | tf_op jit(solution)/shard_map/ppermute | solution.py:93
  277.4 11.4 %group_product.15.rest_0_ = bf16[8192,2048]{1,0:T(8,128)(2,1)} custom-call(bf16[1024,512]{1,0:T(8,128)(2,1)} %get-tuple-element.9.own, bf16[1024,512]{1,0:T(8,128)(2,1)S(1)} %collective-permute-done.27.near, bf16[1024,512]{1,0:T(8,128)(2,1)} %collective-permute-done.28.far, ...), custom_call_target="tpu_custom_call", output_to_operand_aliasing={{}: (5, {})} | custom-call | flops 8589934592 | bytes 8388608 | tf_op jit(solution)/shard_map/group_product/pallas_call | solution.py:33
  288.8 11.0 %collective-permute-done.24.near = bf16[1024,512]{1,0:T(8,128)(2,1)S(1)} collective-permute-done((bf16[1024,512]{1,0:T(8,128)(2,1)S(1)}, bf16[1024,512]{1,0:T(8,128)(2,1)S(1)}, u32[]{:S(2)}, u32[]{:S(2)}) %collective-permute-start.24) | collective-permute-done | bytes 1048608 | tf_op jit(solution)/shard_map/ppermute | solution.py:91
  299.8 22.4 %collective-permute-done.19.far = bf16[1024,512]{1,0:T(8,128)(2,1)S(1)} collective-permute-done((bf16[1024,512]{1,0:T(8,128)(2,1)S(1)}, bf16[1024,512]{1,0:T(8,128)(2,1)S(1)}, u32[]{:S(2)}, u32[]{:S(2)}) %collective-permute-start.19) | collective-permute-done | bytes 1048608 | tf_op jit(solution)/shard_map/ppermute | solution.py:92
  322.3 1.9 collective-permute-start.16
  324.2 20.1 %collective-permute-done.26.mid = bf16[1024,512]{1,0:T(8,128)(2,1)S(1)} collective-permute-done((bf16[1024,512]{1,0:T(8,128)(2,1)S(1)}, bf16[1024,512]{1,0:T(8,128)(2,1)S(1)}, u32[]{:S(2)}, u32[]{:S(2)}) %collective-permute-start.26) | collective-permute-done | bytes 1048608 | tf_op jit(solution)/shard_map/ppermute | solution.py:93
  344.9 10.3 %group_product.16.rest_0_ = bf16[8192,2048]{1,0:T(8,128)(2,1)} custom-call(bf16[1024,512]{1,0:T(8,128)(2,1)S(1)} %get-tuple-element.10.own, bf16[1024,512]{1,0:T(8,128)(2,1)S(1)} %collective-permute-done.24.near, bf16[1024,512]{1,0:T(8,128)(2,1)S(1)} %collective-permute-done.25.far, ...), custom_call_target="tpu_custom_call", output_to_operand_aliasing={{}: (5, {})} | custom-call | flops 8589934592 | bytes 8388608 | tf_op jit(solution)/shard_map/group_product/pallas_call | solution.py:33
  355.2 11.6 %collective-permute-done.21.near = bf16[1024,512]{1,0:T(8,128)(2,1)S(1)} collective-permute-done((bf16[1024,512]{1,0:T(8,128)(2,1)S(1)}, bf16[1024,512]{1,0:T(8,128)(2,1)S(1)}, u32[]{:S(2)}, u32[]{:S(2)}) %collective-permute-start.21) | collective-permute-done | bytes 1048608 | tf_op jit(solution)/shard_map/ppermute | solution.py:91
  367.3 21.9 %collective-permute-done.23.mid = bf16[1024,512]{1,0:T(8,128)(2,1)S(1)} collective-permute-done((bf16[1024,512]{1,0:T(8,128)(2,1)S(1)}, bf16[1024,512]{1,0:T(8,128)(2,1)S(1)}, u32[]{:S(2)}, u32[]{:S(2)}) %collective-permute-start.23) | collective-permute-done | bytes 1048608 | tf_op jit(solution)/shard_map/ppermute | solution.py:93
  389.3 1.9 collective-permute-start.13
  391.2 10.3 %group_product.17.rest_0_ = bf16[8192,2048]{1,0:T(8,128)(2,1)} custom-call(bf16[1024,512]{1,0:T(8,128)(2,1)S(1)} %get-tuple-element.11.own, bf16[1024,512]{1,0:T(8,128)(2,1)S(1)} %collective-permute-done.21.near, bf16[1024,512]{1,0:T(8,128)(2,1)S(1)} %collective-permute-done.22.far, ...), custom_call_target="tpu_custom_call", output_to_operand_aliasing={{}: (5, {})} | custom-call | flops 8589934592 | bytes 8388608 | tf_op jit(solution)/shard_map/group_product/pallas_call | solution.py:33
  401.5 27.5 %collective-permute-done.16.far = bf16[768,512]{1,0:T(8,128)(2,1)S(1)} collective-permute-done((bf16[768,512]{1,0:T(8,128)(2,1)S(1)}, bf16[768,512]{1,0:T(8,128)(2,1)S(1)}, u32[]{:S(2)}, u32[]{:S(2)}) %collective-permute-start.16) | collective-permute-done | bytes 786464 | tf_op jit(solution)/shard_map/ppermute | solution.py:92
  429.0 2.0 collective-permute-start.10
  431.0 20.1 %collective-permute-done.20.mid = bf16[1024,512]{1,0:T(8,128)(2,1)S(1)} collective-permute-done((bf16[1024,512]{1,0:T(8,128)(2,1)S(1)}, bf16[1024,512]{1,0:T(8,128)(2,1)S(1)}, u32[]{:S(2)}, u32[]{:S(2)}) %collective-permute-start.20) | collective-permute-done | bytes 1048608 | tf_op jit(solution)/shard_map/ppermute | solution.py:93
  451.6 10.3 %group_product.18.rest_0_ = bf16[8192,2048]{1,0:T(8,128)(2,1)} custom-call(bf16[1024,512]{1,0:T(8,128)(2,1)S(1)} %get-tuple-element.12.own, bf16[1024,512]{1,0:T(8,128)(2,1)S(1)} %collective-permute-done.18.near, bf16[1024,512]{1,0:T(8,128)(2,1)S(1)} %collective-permute-done.19.far, ...), custom_call_target="tpu_custom_call", output_to_operand_aliasing={{}: (5, {})} | custom-call | flops 8589934592 | bytes 8388608 | tf_op jit(solution)/shard_map/group_product/pallas_call | solution.py:33
  461.9 17.7 %collective-permute-done.13.far = bf16[512,512]{1,0:T(8,128)(2,1)S(1)} collective-permute-done((bf16[512,512]{1,0:T(8,128)(2,1)S(1)}, bf16[512,512]{1,0:T(8,128)(2,1)S(1)}, u32[]{:S(2)}, u32[]{:S(2)}) %collective-permute-start.13) | collective-permute-done | bytes 524320 | tf_op jit(solution)/shard_map/ppermute | solution.py:92
  479.6 2.0 collective-permute-start.7
  481.6 31.3 %collective-permute-done.17.mid = bf16[768,512]{1,0:T(8,128)(2,1)S(1)} collective-permute-done((bf16[768,512]{1,0:T(8,128)(2,1)S(1)}, bf16[768,512]{1,0:T(8,128)(2,1)S(1)}, u32[]{:S(2)}, u32[]{:S(2)}) %collective-permute-start.17) | collective-permute-done | bytes 786464 | tf_op jit(solution)/shard_map/ppermute | solution.py:93
  513.4 8.0 %group_product.19.rest_0_ = bf16[8192,2048]{1,0:T(8,128)(2,1)} custom-call(bf16[768,512]{1,0:T(8,128)(2,1)S(1)} %slice.40.own, bf16[768,512]{1,0:T(8,128)(2,1)S(1)} %collective-permute-done.15.near, bf16[768,512]{1,0:T(8,128)(2,1)S(1)} %collective-permute-done.16.far, ...), custom_call_target="tpu_custom_call", output_to_operand_aliasing={{}: (5, {})} | custom-call | flops 6442450944 | bytes 6291456 | tf_op jit(solution)/shard_map/group_product/pallas_call | solution.py:33
  522.9 1.9 collective-permute-start.1
  524.8 7.7 %collective-permute-done.14.mid = bf16[512,512]{1,0:T(8,128)(2,1)S(1)} collective-permute-done((bf16[512,512]{1,0:T(8,128)(2,1)S(1)}, bf16[512,512]{1,0:T(8,128)(2,1)S(1)}, u32[]{:S(2)}, u32[]{:S(2)}) %collective-permute-start.14) | collective-permute-done | bytes 524320 | tf_op jit(solution)/shard_map/ppermute | solution.py:93
  533.1 5.6 %group_product.20.rest_0_ = bf16[8192,2048]{1,0:T(8,128)(2,1)} custom-call(bf16[512,512]{1,0:T(8,128)(2,1)S(1)} %slice.39.own, bf16[512,512]{1,0:T(8,128)(2,1)S(1)} %collective-permute-done.12.near, bf16[512,512]{1,0:T(8,128)(2,1)S(1)} %collective-permute-done.13.far, ...), custom_call_target="tpu_custom_call", output_to_operand_aliasing={{}: (5, {})} | custom-call | flops 4294967296 | bytes 4194304 | tf_op jit(solution)/shard_map/group_product/pallas_call | solution.py:33
  542.2 1.7 collective-permute-done.11.mid
  543.9 3.3 group_product.21.rest_0_
  547.3 2.3 collective-permute-done.8.mid
  549.5 2.1 group_product.22.rest_0_
  552.1 2.1 group_product.23
  (91 shorter events, 30.7 us)
Async XLA Ops:
  4.2 67.1 %copy-start = (bf16[1024,512]{1,0:T(8,128)(2,1)}, bf16[1024,512]{1,0:T(8,128)(2,1)S(1)}, u32[]{:S(2)}) copy-start(bf16[1024,512]{1,0:T(8,128)(2,1)S(1)} %get-tuple-element.8.own) | copy-start | bytes 3145732
  4.2 65.2 %collective-permute-start.34 = (bf16[1024,512]{1,0:T(8,128)(2,1)S(1)}, bf16[1024,512]{1,0:T(8,128)(2,1)}, u32[]{:S(2)}, u32[]{:S(2)}) collective-permute-start(bf16[1024,512]{1,0:T(8,128)(2,1)S(1)} %get-tuple-element.7.own), channel_id=1, source_target_pairs={{0,12},{4,8},{8,4},{12,0},{1,13},{5,9},{9,5},{13,1},{2,14},{6,10},... | collective-permute-start | bytes 3145736 | tf_op jit(solution)/shard_map/ppermute | solution.py:92
  4.4 66.9 %collective-permute-start.33 = (bf16[1024,512]{1,0:T(8,128)(2,1)S(1)}, bf16[1024,512]{1,0:T(8,128)(2,1)S(1)}, u32[]{:S(2)}, u32[]{:S(2)}) collective-permute-start(bf16[1024,512]{1,0:T(8,128)(2,1)S(1)} %get-tuple-element.7.own), channel_id=1, source_target_pairs={{0,4},{4,0},{8,12},{12,8},{1,5},{5,1},{9,13},{13,9},{2,6},{6,2},{1... | collective-permute-start | bytes 3145736 | tf_op jit(solution)/shard_map/ppermute | solution.py:91
  7.1 53.0 %collective-permute-start.37 = (bf16[256,512]{1,0:T(8,128)(2,1)S(1)}, bf16[256,512]{1,0:T(8,128)(2,1)S(1)}, u32[]{:S(2)}, u32[]{:S(2)}) collective-permute-start(bf16[256,512]{1,0:T(8,128)(2,1)S(1)} %get-tuple-element.5.own), channel_id=1, source_target_pairs={{0,12},{4,8},{8,4},{12,0},{1,13},{5,9},{9,5},{13,1},{2,14},{6,10},... | collective-permute-start | bytes 786440 | tf_op jit(solution)/shard_map/ppermute | solution.py:92
  10.1 53.8 %collective-permute-start.36 = (bf16[256,512]{1,0:T(8,128)(2,1)S(1)}, bf16[256,512]{1,0:T(8,128)(2,1)S(1)}, u32[]{:S(2)}, u32[]{:S(2)}) collective-permute-start(bf16[256,512]{1,0:T(8,128)(2,1)S(1)} %get-tuple-element.5.own), channel_id=1, source_target_pairs={{0,4},{4,0},{8,12},{12,8},{1,5},{5,1},{9,13},{13,9},{2,6},{6,2},{1... | collective-permute-start | bytes 786440 | tf_op jit(solution)/shard_map/ppermute | solution.py:91
  60.1 8.5 %collective-permute-start.38 = (bf16[256,512]{1,0:T(8,128)(2,1)S(1)}, bf16[256,512]{1,0:T(8,128)(2,1)S(1)}, u32[]{:S(2)}, u32[]{:S(2)}) collective-permute-start(bf16[256,512]{1,0:T(8,128)(2,1)S(1)} %collective-permute-done.37.far), channel_id=1, source_target_pairs={{0,4},{4,0},{8,12},{12,8},{1,5},{5,1},{9,13},{13,9},{2,6},{6,2},{1... | collective-permute-start | bytes 786440 | tf_op jit(solution)/shard_map/ppermute | solution.py:93
  63.9 59.3 %collective-permute-start.3 = (bf16[512,2048]{1,0:T(8,128)(2,1)}, bf16[512,2048]{1,0:T(8,128)(2,1)}, u32[]{:S(2)}, u32[]{:S(2)}) collective-permute-start(bf16[512,2048]{1,0:T(8,128)(2,1)} %refs_0_.1), channel_id=1, source_target_pairs={{0,3},{1,0},{2,1},{3,2},{4,7},{5,4},{6,5},{7,6},{8,11},{9,8},{10,9... | collective-permute-start | bytes 6291464 | tf_op jit(solution)/shard_map/ppermute | solution.py:96
  64.6 89.8 %collective-permute-start.4 = (bf16[512,2048]{1,0:T(8,128)(2,1)}, bf16[512,2048]{1,0:T(8,128)(2,1)}, u32[]{:S(2)}, u32[]{:S(2)}) collective-permute-start(bf16[512,2048]{1,0:T(8,128)(2,1)} %refs_0_.1), channel_id=1, source_target_pairs={{0,2},{1,3},{2,0},{3,1},{4,6},{5,7},{6,4},{7,5},{8,10},{9,11},{10,... | collective-permute-start | bytes 6291464 | tf_op jit(solution)/shard_map/ppermute | solution.py:96
  69.4 86.8 %collective-permute-start.5 = (bf16[512,2048]{1,0:T(8,128)(2,1)}, bf16[512,2048]{1,0:T(8,128)(2,1)}, u32[]{:S(2)}, u32[]{:S(2)}) collective-permute-start(bf16[512,2048]{1,0:T(8,128)(2,1)} %refs_0_.1), channel_id=1, source_target_pairs={{0,1},{1,2},{2,3},{3,0},{4,5},{5,6},{6,7},{7,4},{8,9},{9,10},{10,1... | collective-permute-start | bytes 6291464 | tf_op jit(solution)/shard_map/ppermute | solution.py:96
  69.4 27.9 %collective-permute-start.31 = (bf16[1024,512]{1,0:T(8,128)(2,1)S(1)}, bf16[1024,512]{1,0:T(8,128)(2,1)S(1)}, u32[]{:S(2)}, u32[]{:S(2)}) collective-permute-start(bf16[1024,512]{1,0:T(8,128)(2,1)S(1)} %get-tuple-element.8.own), channel_id=1, source_target_pairs={{0,12},{4,8},{8,4},{12,0},{1,13},{5,9},{9,5},{13,1},{2,14},{6,10},... | collective-permute-start | bytes 3145736 | tf_op jit(solution)/shard_map/ppermute | solution.py:92
  72.3 47.5 %collective-permute-start.30 = (bf16[1024,512]{1,0:T(8,128)(2,1)S(1)}, bf16[1024,512]{1,0:T(8,128)(2,1)S(1)}, u32[]{:S(2)}, u32[]{:S(2)}) collective-permute-start(bf16[1024,512]{1,0:T(8,128)(2,1)S(1)} %get-tuple-element.8.own), channel_id=1, source_target_pairs={{0,4},{4,0},{8,12},{12,8},{1,5},{5,1},{9,13},{13,9},{2,6},{6,2},{1... | collective-permute-start | bytes 3145736 | tf_op jit(solution)/shard_map/ppermute | solution.py:91
  97.3 22.5 %copy-start.7 = (bf16[1024,512]{1,0:T(8,128)(2,1)}, bf16[1024,512]{1,0:T(8,128)(2,1)S(1)}, u32[]{:S(2)}) copy-start(bf16[1024,512]{1,0:T(8,128)(2,1)S(1)} %collective-permute-done.31.far) | copy-start | bytes 3145732
  97.3 73.6 %collective-permute-start.28 = (bf16[1024,512]{1,0:T(8,128)(2,1)}, bf16[1024,512]{1,0:T(8,128)(2,1)}, u32[]{:S(2)}, u32[]{:S(2)}) collective-permute-start(bf16[1024,512]{1,0:T(8,128)(2,1)} %get-tuple-element.9.own), channel_id=1, source_target_pairs={{0,12},{4,8},{8,4},{12,0},{1,13},{5,9},{9,5},{13,1},{2,14},{6,10},... | collective-permute-start | bytes 3145736 | tf_op jit(solution)/shard_map/ppermute | solution.py:92
  120.8 52.3 %collective-permute-start.35 = (bf16[1024,512]{1,0:T(8,128)(2,1)}, bf16[1024,512]{1,0:T(8,128)(2,1)}, u32[]{:S(2)}, u32[]{:S(2)}) collective-permute-start(bf16[1024,512]{1,0:T(8,128)(2,1)} %collective-permute-done.34.far), channel_id=1, source_target_pairs={{0,4},{4,0},{8,12},{12,8},{1,5},{5,1},{9,13},{13,9},{2,6},{6,2},{1... | collective-permute-start | bytes 3145736 | tf_op jit(solution)/shard_map/ppermute | solution.py:93
  121.3 52.9 %copy-start.3 = (bf16[1024,512]{1,0:T(8,128)(2,1)S(1)}, bf16[1024,512]{1,0:T(8,128)(2,1)}, u32[]{:S(2)}) copy-start(bf16[1024,512]{1,0:T(8,128)(2,1)} %copy-done.2) | copy-start | bytes 3145732
  121.3 52.9 %copy-start.6 = (bf16[1024,512]{1,0:T(8,128)(2,1)S(1)}, bf16[1024,512]{1,0:T(8,128)(2,1)}, u32[]{:S(2)}) copy-start(bf16[1024,512]{1,0:T(8,128)(2,1)} %copy-done.5) | copy-start | bytes 3145732
  123.2 86.0 %collective-permute-start.27 = (bf16[1024,512]{1,0:T(8,128)(2,1)}, bf16[1024,512]{1,0:T(8,128)(2,1)S(1)}, u32[]{:S(2)}, u32[]{:S(2)}) collective-permute-start(bf16[1024,512]{1,0:T(8,128)(2,1)} %get-tuple-element.9.own), channel_id=1, source_target_pairs={{0,4},{4,0},{8,12},{12,8},{1,5},{5,1},{9,13},{13,9},{2,6},{6,2},{1... | collective-permute-start | bytes 3145736 | tf_op jit(solution)/shard_map/ppermute | solution.py:91
  154.5 55.3 %collective-permute-start.25 = (bf16[1024,512]{1,0:T(8,128)(2,1)S(1)}, bf16[1024,512]{1,0:T(8,128)(2,1)S(1)}, u32[]{:S(2)}, u32[]{:S(2)}) collective-permute-start(bf16[1024,512]{1,0:T(8,128)(2,1)S(1)} %get-tuple-element.10.own), channel_id=1, source_target_pairs={{0,12},{4,8},{8,4},{12,0},{1,13},{5,9},{9,5},{13,1},{2,14},{6,10},... | collective-permute-start | bytes 3145736 | tf_op jit(solution)/shard_map/ppermute | solution.py:92
  156.2 76.2 %collective-permute-start.32 = (bf16[1024,512]{1,0:T(8,128)(2,1)}, bf16[1024,512]{1,0:T(8,128)(2,1)S(1)}, u32[]{:S(2)}, u32[]{:S(2)}) collective-permute-start(bf16[1024,512]{1,0:T(8,128)(2,1)} %copy-done.7), channel_id=1, source_target_pairs={{0,4},{4,0},{8,12},{12,8},{1,5},{5,1},{9,13},{13,9},{2,6},{6,2},{1... | collective-permute-start | bytes 3145736 | tf_op jit(solution)/shard_map/ppermute | solution.py:93
  171.0 61.4 %copy-start.1 = (bf16[1024,512]{1,0:T(8,128)(2,1)S(1)}, bf16[1024,512]{1,0:T(8,128)(2,1)}, u32[]{:S(2)}) copy-start(bf16[1024,512]{1,0:T(8,128)(2,1)} %copy-done) | copy-start | bytes 3145732
  171.0 61.4 %copy-start.8 = (bf16[1024,512]{1,0:T(8,128)(2,1)S(1)}, bf16[1024,512]{1,0:T(8,128)(2,1)}, u32[]{:S(2)}) copy-start(bf16[1024,512]{1,0:T(8,128)(2,1)} %copy-done.7) | copy-start | bytes 3145732
  171.0 61.4 %copy-start.10 = (bf16[1024,512]{1,0:T(8,128)(2,1)S(1)}, bf16[1024,512]{1,0:T(8,128)(2,1)}, u32[]{:S(2)}) copy-start(bf16[1024,512]{1,0:T(8,128)(2,1)} %copy-done.9) | copy-start | bytes 3145732
  171.0 83.8 %collective-permute-start.22 = (bf16[1024,512]{1,0:T(8,128)(2,1)S(1)}, bf16[1024,512]{1,0:T(8,128)(2,1)S(1)}, u32[]{:S(2)}, u32[]{:S(2)}) collective-permute-start(bf16[1024,512]{1,0:T(8,128)(2,1)S(1)} %get-tuple-element.11.own), channel_id=1, source_target_pairs={{0,12},{4,8},{8,4},{12,0},{1,13},{5,9},{9,5},{13,1},{2,14},{6,10},... | collective-permute-start | bytes 3145736 | tf_op jit(solution)/shard_map/ppermute | solution.py:92
  173.1 103.9 %collective-permute-start.29 = (bf16[1024,512]{1,0:T(8,128)(2,1)}, bf16[1024,512]{1,0:T(8,128)(2,1)S(1)}, u32[]{:S(2)}, u32[]{:S(2)}) collective-permute-start(bf16[1024,512]{1,0:T(8,128)(2,1)} %collective-permute-done.28.far), channel_id=1, source_target_pairs={{0,4},{4,0},{8,12},{12,8},{1,5},{5,1},{9,13},{13,9},{2,6},{6,2},{1... | collective-permute-start | bytes 3145736 | tf_op jit(solution)/shard_map/ppermute | solution.py:93
  209.2 90.5 %collective-permute-start.24 = (bf16[1024,512]{1,0:T(8,128)(2,1)S(1)}, bf16[1024,512]{1,0:T(8,128)(2,1)S(1)}, u32[]{:S(2)}, u32[]{:S(2)}) collective-permute-start(bf16[1024,512]{1,0:T(8,128)(2,1)S(1)} %get-tuple-element.10.own), channel_id=1, source_target_pairs={{0,4},{4,0},{8,12},{12,8},{1,5},{5,1},{9,13},{13,9},{2,6},{6,2},{1... | collective-permute-start | bytes 3145736 | tf_op jit(solution)/shard_map/ppermute | solution.py:91
  209.8 112.5 %collective-permute-start.19 = (bf16[1024,512]{1,0:T(8,128)(2,1)S(1)}, bf16[1024,512]{1,0:T(8,128)(2,1)S(1)}, u32[]{:S(2)}, u32[]{:S(2)}) collective-permute-start(bf16[1024,512]{1,0:T(8,128)(2,1)S(1)} %get-tuple-element.12.own), channel_id=1, source_target_pairs={{0,12},{4,8},{8,4},{12,0},{1,13},{5,9},{9,5},{13,1},{2,14},{6,10},... | collective-permute-start | bytes 3145736 | tf_op jit(solution)/shard_map/ppermute | solution.py:92
  232.3 112.0 %collective-permute-start.26 = (bf16[1024,512]{1,0:T(8,128)(2,1)S(1)}, bf16[1024,512]{1,0:T(8,128)(2,1)S(1)}, u32[]{:S(2)}, u32[]{:S(2)}) collective-permute-start(bf16[1024,512]{1,0:T(8,128)(2,1)S(1)} %collective-permute-done.25.far), channel_id=1, source_target_pairs={{0,4},{4,0},{8,12},{12,8},{1,5},{5,1},{9,13},{13,9},{2,6},{6,2},{1... | collective-permute-start | bytes 3145736 | tf_op jit(solution)/shard_map/ppermute | solution.py:93
  254.8 112.0 %collective-permute-start.21 = (bf16[1024,512]{1,0:T(8,128)(2,1)S(1)}, bf16[1024,512]{1,0:T(8,128)(2,1)S(1)}, u32[]{:S(2)}, u32[]{:S(2)}) collective-permute-start(bf16[1024,512]{1,0:T(8,128)(2,1)S(1)} %get-tuple-element.11.own), channel_id=1, source_target_pairs={{0,4},{4,0},{8,12},{12,8},{1,5},{5,1},{9,13},{13,9},{2,6},{6,2},{1... | collective-permute-start | bytes 3145736 | tf_op jit(solution)/shard_map/ppermute | solution.py:91
  276.9 112.4 %collective-permute-start.23 = (bf16[1024,512]{1,0:T(8,128)(2,1)S(1)}, bf16[1024,512]{1,0:T(8,128)(2,1)S(1)}, u32[]{:S(2)}, u32[]{:S(2)}) collective-permute-start(bf16[1024,512]{1,0:T(8,128)(2,1)S(1)} %collective-permute-done.22.far), channel_id=1, source_target_pairs={{0,4},{4,0},{8,12},{12,8},{1,5},{5,1},{9,13},{13,9},{2,6},{6,2},{1... | collective-permute-start | bytes 3145736 | tf_op jit(solution)/shard_map/ppermute | solution.py:93
  299.8 129.3 %collective-permute-start.18 = (bf16[1024,512]{1,0:T(8,128)(2,1)S(1)}, bf16[1024,512]{1,0:T(8,128)(2,1)S(1)}, u32[]{:S(2)}, u32[]{:S(2)}) collective-permute-start(bf16[1024,512]{1,0:T(8,128)(2,1)S(1)} %get-tuple-element.12.own), channel_id=1, source_target_pairs={{0,4},{4,0},{8,12},{12,8},{1,5},{5,1},{9,13},{13,9},{2,6},{6,2},{1... | collective-permute-start | bytes 3145736 | tf_op jit(solution)/shard_map/ppermute | solution.py:91
  322.3 106.7 %collective-permute-start.16 = (bf16[768,512]{1,0:T(8,128)(2,1)S(1)}, bf16[768,512]{1,0:T(8,128)(2,1)S(1)}, u32[]{:S(2)}, u32[]{:S(2)}) collective-permute-start(bf16[768,512]{1,0:T(8,128)(2,1)S(1)} %slice.40.own), channel_id=1, source_target_pairs={{0,12},{4,8},{8,4},{12,0},{1,13},{5,9},{9,5},{13,1},{2,14},{6,10},... | collective-permute-start | bytes 2359304 | tf_op jit(solution)/shard_map/ppermute | solution.py:92
  344.3 106.7 %collective-permute-start.20 = (bf16[1024,512]{1,0:T(8,128)(2,1)S(1)}, bf16[1024,512]{1,0:T(8,128)(2,1)S(1)}, u32[]{:S(2)}, u32[]{:S(2)}) collective-permute-start(bf16[1024,512]{1,0:T(8,128)(2,1)S(1)} %collective-permute-done.19.far), channel_id=1, source_target_pairs={{0,4},{4,0},{8,12},{12,8},{1,5},{5,1},{9,13},{13,9},{2,6},{6,2},{1... | collective-permute-start | bytes 3145736 | tf_op jit(solution)/shard_map/ppermute | solution.py:93
  366.8 112.8 %collective-permute-start.15 = (bf16[768,512]{1,0:T(8,128)(2,1)S(1)}, bf16[768,512]{1,0:T(8,128)(2,1)S(1)}, u32[]{:S(2)}, u32[]{:S(2)}) collective-permute-start(bf16[768,512]{1,0:T(8,128)(2,1)S(1)} %slice.40.own), channel_id=1, source_target_pairs={{0,4},{4,0},{8,12},{12,8},{1,5},{5,1},{9,13},{13,9},{2,6},{6,2},{1... | collective-permute-start | bytes 2359304 | tf_op jit(solution)/shard_map/ppermute | solution.py:91
  389.3 90.3 %collective-permute-start.13 = (bf16[512,512]{1,0:T(8,128)(2,1)S(1)}, bf16[512,512]{1,0:T(8,128)(2,1)S(1)}, u32[]{:S(2)}, u32[]{:S(2)}) collective-permute-start(bf16[512,512]{1,0:T(8,128)(2,1)S(1)} %slice.39.own), channel_id=1, source_target_pairs={{0,12},{4,8},{8,4},{12,0},{1,13},{5,9},{9,5},{13,1},{2,14},{6,10},... | collective-permute-start | bytes 1572872 | tf_op jit(solution)/shard_map/ppermute | solution.py:92
  429.0 93.8 %collective-permute-start.12 = (bf16[512,512]{1,0:T(8,128)(2,1)S(1)}, bf16[512,512]{1,0:T(8,128)(2,1)S(1)}, u32[]{:S(2)}, u32[]{:S(2)}) collective-permute-start(bf16[512,512]{1,0:T(8,128)(2,1)S(1)} %slice.39.own), channel_id=1, source_target_pairs={{0,4},{4,0},{8,12},{12,8},{1,5},{5,1},{9,13},{13,9},{2,6},{6,2},{1... | collective-permute-start | bytes 1572872 | tf_op jit(solution)/shard_map/ppermute | solution.py:91
  429.0 50.6 %copy-start.14 = (bf16[128,512]{1,0:T(8,128)(2,1)S(1)}, bf16[128,512]{1,0:T(8,128)(2,1)}, u32[]{:S(2)}) copy-start(bf16[128,512]{1,0:T(8,128)(2,1)} %get-tuple-element.13.own) | copy-start | bytes 393220
  429.0 92.3 %collective-permute-start.10 = (bf16[256,512]{1,0:T(8,128)(2,1)S(1)}, bf16[256,512]{1,0:T(8,128)(2,1)S(1)}, u32[]{:S(2)}, u32[]{:S(2)}) collective-permute-start(bf16[256,512]{1,0:T(8,128)(2,1)S(1)} %get-tuple-element.6.own), channel_id=1, source_target_pairs={{0,12},{4,8},{8,4},{12,0},{1,13},{5,9},{9,5},{13,1},{2,14},{6,10},... | collective-permute-start | bytes 786440 | tf_op jit(solution)/shard_map/ppermute | solution.py:92
  451.1 61.8 %collective-permute-start.17 = (bf16[768,512]{1,0:T(8,128)(2,1)S(1)}, bf16[768,512]{1,0:T(8,128)(2,1)S(1)}, u32[]{:S(2)}, u32[]{:S(2)}) collective-permute-start(bf16[768,512]{1,0:T(8,128)(2,1)S(1)} %collective-permute-done.16.far), channel_id=1, source_target_pairs={{0,4},{4,0},{8,12},{12,8},{1,5},{5,1},{9,13},{13,9},{2,6},{6,2},{1... | collective-permute-start | bytes 2359304 | tf_op jit(solution)/shard_map/ppermute | solution.py:93
  479.6 61.1 %collective-permute-start.9 = (bf16[256,512]{1,0:T(8,128)(2,1)S(1)}, bf16[256,512]{1,0:T(8,128)(2,1)S(1)}, u32[]{:S(2)}, u32[]{:S(2)}) collective-permute-start(bf16[256,512]{1,0:T(8,128)(2,1)S(1)} %get-tuple-element.6.own), channel_id=1, source_target_pairs={{0,4},{4,0},{8,12},{12,8},{1,5},{5,1},{9,13},{13,9},{2,6},{6,2},{1... | collective-permute-start | bytes 786440 | tf_op jit(solution)/shard_map/ppermute | solution.py:91
  479.6 43.3 %copy-start.13 = (bf16[128,512]{1,0:T(8,128)(2,1)S(1)}, bf16[128,512]{1,0:T(8,128)(2,1)}, u32[]{:S(2)}) copy-start(bf16[128,512]{1,0:T(8,128)(2,1)} %get-tuple-element.14.own) | copy-start | bytes 393220
  479.6 59.1 %collective-permute-start.7 = (bf16[128,512]{1,0:T(8,128)(2,1)S(1)}, bf16[128,512]{1,0:T(8,128)(2,1)S(1)}, u32[]{:S(2)}, u32[]{:S(2)}) collective-permute-start(bf16[128,512]{1,0:T(8,128)(2,1)S(1)} %copy-done.14), channel_id=1, source_target_pairs={{0,12},{4,8},{8,4},{12,0},{1,13},{5,9},{9,5},{13,1},{2,14},{6,10},... | collective-permute-start | bytes 393224 | tf_op jit(solution)/shard_map/ppermute | solution.py:92
  512.9 19.7 %collective-permute-start.14 = (bf16[512,512]{1,0:T(8,128)(2,1)S(1)}, bf16[512,512]{1,0:T(8,128)(2,1)S(1)}, u32[]{:S(2)}, u32[]{:S(2)}) collective-permute-start(bf16[512,512]{1,0:T(8,128)(2,1)S(1)} %collective-permute-done.13.far), channel_id=1, source_target_pairs={{0,4},{4,0},{8,12},{12,8},{1,5},{5,1},{9,13},{13,9},{2,6},{6,2},{1... | collective-permute-start | bytes 1572872 | tf_op jit(solution)/shard_map/ppermute | solution.py:93
  521.4 25.9 %collective-permute-start.6 = (bf16[128,512]{1,0:T(8,128)(2,1)S(1)}, bf16[128,512]{1,0:T(8,128)(2,1)S(1)}, u32[]{:S(2)}, u32[]{:S(2)}) collective-permute-start(bf16[128,512]{1,0:T(8,128)(2,1)S(1)} %copy-done.14), channel_id=1, source_target_pairs={{0,4},{4,0},{8,12},{12,8},{1,5},{5,1},{9,13},{13,9},{2,6},{6,2},{1... | collective-permute-start | bytes 393224 | tf_op jit(solution)/shard_map/ppermute | solution.py:91
  522.9 17.3 %collective-permute-start.1 = (bf16[128,512]{1,0:T(8,128)(2,1)S(1)}, bf16[128,512]{1,0:T(8,128)(2,1)S(1)}, u32[]{:S(2)}, u32[]{:S(2)}) collective-permute-start(bf16[128,512]{1,0:T(8,128)(2,1)S(1)} %copy-done.13), channel_id=1, source_target_pairs={{0,12},{4,8},{8,4},{12,0},{1,13},{5,9},{9,5},{13,1},{2,14},{6,10},... | collective-permute-start | bytes 393224 | tf_op jit(solution)/shard_map/ppermute | solution.py:92
  532.5 11.4 %collective-permute-start.11 = (bf16[256,512]{1,0:T(8,128)(2,1)S(1)}, bf16[256,512]{1,0:T(8,128)(2,1)S(1)}, u32[]{:S(2)}, u32[]{:S(2)}) collective-permute-start(bf16[256,512]{1,0:T(8,128)(2,1)S(1)} %collective-permute-done.10.far), channel_id=1, source_target_pairs={{0,4},{4,0},{8,12},{12,8},{1,5},{5,1},{9,13},{13,9},{2,6},{6,2},{1... | collective-permute-start | bytes 786440 | tf_op jit(solution)/shard_map/ppermute | solution.py:93
  538.7 12.9 %collective-permute-start = (bf16[128,512]{1,0:T(8,128)(2,1)S(1)}, bf16[128,512]{1,0:T(8,128)(2,1)S(1)}, u32[]{:S(2)}, u32[]{:S(2)}) collective-permute-start(bf16[128,512]{1,0:T(8,128)(2,1)S(1)} %copy-done.13), channel_id=1, source_target_pairs={{0,4},{4,0},{8,12},{12,8},{1,5},{5,1},{9,13},{13,9},{2,6},{6,2},{1... | collective-permute-start | bytes 393224 | tf_op jit(solution)/shard_map/ppermute | solution.py:91
  540.2 9.3 %collective-permute-start.8 = (bf16[128,512]{1,0:T(8,128)(2,1)S(1)}, bf16[128,512]{1,0:T(8,128)(2,1)S(1)}, u32[]{:S(2)}, u32[]{:S(2)}) collective-permute-start(bf16[128,512]{1,0:T(8,128)(2,1)S(1)} %collective-permute-done.7.far), channel_id=1, source_target_pairs={{0,4},{4,0},{8,12},{12,8},{1,5},{5,1},{9,13},{13,9},{2,6},{6,2},{1... | collective-permute-start | bytes 393224 | tf_op jit(solution)/shard_map/ppermute | solution.py:93
  540.7 11.4 %collective-permute-start.2 = (bf16[128,512]{1,0:T(8,128)(2,1)S(1)}, bf16[128,512]{1,0:T(8,128)(2,1)S(1)}, u32[]{:S(2)}, u32[]{:S(2)}) collective-permute-start(bf16[128,512]{1,0:T(8,128)(2,1)S(1)} %collective-permute-done.1.far), channel_id=1, source_target_pairs={{0,4},{4,0},{8,12},{12,8},{1,5},{5,1},{9,13},{13,9},{2,6},{6,2},{1... | collective-permute-start | bytes 393224 | tf_op jit(solution)/shard_map/ppermute | solution.py:93
  (12 other events, 11.1 us)

commit v2 on v1

--- a/solution.py
+++ b/solution.py
@@ -1,3 +1,5 @@
+import functools
+
 import jax
 import jax.numpy as jnp
 from jax import lax
@@ -6,38 +8,47 @@
 from jax.sharding import PartitionSpec as P
 
 
-GROUPS = (256, 1024, 1024, 1024, 1024, 1024, 1024, 768, 512, 256, 128, 128)
+HALVES = 4
+GROUPS = (1024, 1024, 1024, 1024, 1024, 1024, 1024, 512, 256, 128, 128)
 BM = 256
 
 
-def _mm_kernel(own, near, far, mid, b_ref, *rest):
+def _mm_kernel(side, own, near, p2, p3, p4, p5, b_ref, *rest):
     out_ref = rest[-1]
-    lhs = jnp.concatenate([own[...], near[...], far[...], mid[...]], axis=1)
+    col_pos = lax.axis_index("col")
+    at_end = jnp.logical_or(col_pos == 0, col_pos == side - 1)
+
+    third = jnp.where(at_end, p3[...], p4[...])
+    fourth = jnp.where(at_end, p5[...], p2[...])
+    lhs = jnp.concatenate([own[...], near[...], third, fourth], axis=1)
     out_ref[...] = jnp.dot(lhs, b_ref[...], preferred_element_type=jnp.float32).astype(out_ref.dtype)
 
 
-def _group_product(own, near, far, mid, b, c, rows, cols, off, size):
+def _group_product(side, a, near, p2, p3, p4, p5, b, c, off, size):
     bm = BM if size > BM else BM // 2
-    depth = own.shape[1]
-    total = b.shape[0]
+    rows, depth = a.shape
+    total, cols = b.shape
+    base = off % p2.shape[0]
     piece = pl.BlockSpec((bm, depth), lambda i: (i, 0))
+    chunk = pl.BlockSpec((bm, depth), lambda i: (base // bm + i, 0))
+    full = pl.BlockSpec((bm, depth), lambda i: (off // bm + i, 0))
     whole = pl.BlockSpec((total, cols), lambda i: (0, 0), pipeline_mode=pl.Buffered(1))
     out = pl.BlockSpec((bm, cols), lambda i: (off // bm + i, 0))
-    in_specs = [piece, piece, piece, piece, whole]
-    args = [own, near, far, mid, b]
+    in_specs = [full, full, chunk, chunk, piece, piece, whole]
+    args = [a, near, p2, p3, p4, p5, b]
     alias = {}
     if c is not None:
         in_specs.append(pl.BlockSpec(memory_space=pl.ANY))
         args.append(c)
-        alias = {5: 0}
+        alias = {7: 0}
     return pl.pallas_call(
-        _mm_kernel,
+        functools.partial(_mm_kernel, side),
         grid=(size // bm,),
         out_shape=jax.ShapeDtypeStruct((rows, cols), jnp.bfloat16),
         in_specs=in_specs,
         out_specs=out,
         input_output_aliases=alias,
-        compiler_params=pltpu.CompilerParams(dimension_semantics=("arbitrary",), vmem_limit_bytes=20 * 2**20),
+        compiler_params=pltpu.CompilerParams(dimension_semantics=("arbitrary",), vmem_limit_bytes=22 * 2**20),
         cost_estimate=pl.CostEstimate(
             flops=2 * size * total * cols,
             bytes_accessed=size * (total + cols) * 2,
@@ -79,28 +90,29 @@
 def solution(mesh):
     side = mesh.shape["row"]
     with_near = [(p, p ^ 1) for p in range(side)]
-    with_far = [(p, side - 1 - p) for p in range(side)]
+    inner = [(p, side - 1 - p if 0 < p < side - 1 else p) for p in range(side)]
 
     def local(a, b_own):
         rows, _ = a.shape
-        cols = b_own.shape[1]
         offs = [sum(GROUPS[:g]) for g in range(len(GROUPS))]
         row_pos, col_pos = lax.axis_index("row"), lax.axis_index("col")
 
-        parts = [lax.slice_in_dim(a, o, o + s) for o, s in zip(offs, GROUPS)]
-        near = [lax.ppermute(x, "col", with_near) for x in parts]
-        far = [lax.ppermute(x, "col", with_far) for x in parts]
-        mid = [lax.ppermute(x, "col", with_near) for x in far]
+        near = lax.ppermute(a, "col", with_near)
+        step = rows // HALVES
+        p2 = [lax.ppermute(a[h * step : (h + 1) * step], "col", inner) for h in range(HALVES)]
+        p3 = [lax.ppermute(x, "col", with_near) for x in p2]
+        p4 = [lax.ppermute(near[o : o + s], "col", inner) for o, s in zip(offs, GROUPS)]
+        p5 = [lax.ppermute(x, "col", with_near) for x in p4]
 
         blocks = [b_own] + [
             lax.ppermute(b_own, "row", [(p, (p - s) % side) for p in range(side)]) for s in range(1, side)
         ]
-        rels = [lax.rem(row_pos + s, side) ^ col_pos for s in range(side)]
-        b = _stack_blocks(jnp.stack([rel ^ (rel // 2) for rel in rels]), blocks)
+        b = _stack_blocks(jnp.stack([lax.rem(row_pos + s, side) ^ col_pos for s in range(side)]), blocks)
 
         c = None
         for g, (off, size) in enumerate(zip(offs, GROUPS)):
-            c = _group_product(parts[g], near[g], far[g], mid[g], b, c, rows, cols, off, size)
+            h = off // step
+            c = _group_product(side, a, near, p2[h], p3[h], p4[g], p5[g], b, c, off, size)
         return c
 
     return jax.shard_map(

time: 558 us -> 558 us (level)
  waiting for transfers between devices: 402 us -> 353 us
  starting transfers between devices: 39.8 us -> 84.4 us
    ppermute x36 -> x31, waiting for transfers between devices: 372 us -> 275 us  [the longest x11 162 us: local(): p5 = [lax.ppermute(x, 'col', with_near) for x in p4]]
    ppermute x3, waiting for transfers between devices: 30.1 us -> 78.1 us  [local(): lax.ppermute(b_own, 'row', [(p, (p - s) % side) for p in range(side)])]
    ppermute x36 -> x31, starting transfers between devices: 39.2 us -> 81.9 us  [the longest x11 32.1 us: local(): p5 = [lax.ppermute(x, 'col', with_near) for x in p4]]
    unnamed x42 -> x36, local copies, waits for them, and re-layouts: 11.2 us -> 16.9 us
    pallas_call x12 -> x11, Pallas kernels: 88.4 us -> 92.2 us  [_group_product(): pl.pallas_call(functools.partial(_mm_kernel, side), grid=(size // bm,), o...]
  transfers between devices with their start and end apart: 39 -> 34, of which waited for: 24 -> 12; matrix products, arithmetic and copies ran while one was open for 1% -> 1% of each run, Pallas kernels for 16% -> 16%
where the time goes in v2:
time: 558 us; the launch traced here: 555 us
  waiting for transfers between devices  353 us (63%)
  Pallas kernels  93.4 us (17%)
  starting transfers between devices  84.4 us (15%)
  local copies, waits for them, and re-layouts  24.4 us (4%)
    ppermute x11, waiting for transfers between devices, local(): p5 = [lax.ppermute(x, 'col', with_near) for x in p4]  162 us
    pallas_call x11, Pallas kernels, _group_product(): pl.pallas_call(functools.partial(_mm_kernel, side), grid=(size // bm,), o...  92.2 us
    ppermute x1, waiting for transfers between devices, local(): near = lax.ppermute(a, 'col', with_near)  81.1 us
    ppermute x3, waiting for transfers between devices, local(): lax.ppermute(b_own, 'row', [(p, (p - s) % side) for p in range(side)])  78.1 us
    ppermute x11, starting transfers between devices, local(): p5 = [lax.ppermute(x, 'col', with_near) for x in p4]  32.1 us
    ppermute x4, waiting for transfers between devices, local(): p3 = [lax.ppermute(x, 'col', with_near) for x in p2]  31.6 us
    ppermute x11, starting transfers between devices, local(): lax.ppermute(near[o:o + s], 'col', inner)  30.9 us
    unnamed x36, local copies, waits for them, and re-layouts  16.9 us
  transfers between devices with their start and end apart: 34, of which 12 were waited for; matrix products, arithmetic and copies ran while one was open for 1% of the time, Pallas kernels for 16%

profile of v2, /device:TPU:28, one launch (start us, length us, event | category | flops | bytes accessed | tf_op | source)
XLA Modules:
  0.0 555.1 jit_solution(16560891682755247410)
XLA Ops:
  1.6 3.8 fusion.1
  5.4 2.0 collective-permute-start.28
  7.4 2.0 collective-permute-start.22
  9.4 37.3 %collective-permute-done.5.refs_1_ = bf16[512,2048]{1,0:T(8,128)(2,1)S(1)} collective-permute-done((bf16[512,2048]{1,0:T(8,128)(2,1)}, bf16[512,2048]{1,0:T(8,128)(2,1)S(1)}, u32[]{:S(2)}, u32[]{:S(2)}) %collective-permute-start.5) | collective-permute-done | bytes 2097184 | tf_op jit(solution)/shard_map/ppermute | solution.py:108
  49.4 40.8 %collective-permute-done.6.refs_2_ = bf16[512,2048]{1,0:T(8,128)(2,1)S(1)} collective-permute-done((bf16[512,2048]{1,0:T(8,128)(2,1)}, bf16[512,2048]{1,0:T(8,128)(2,1)S(1)}, u32[]{:S(2)}, u32[]{:S(2)}) %collective-permute-start.6) | collective-permute-done | bytes 2097184 | tf_op jit(solution)/shard_map/ppermute | solution.py:108
  90.2 1.4 copy-done.8
  93.2 9.2 %collective-permute-start.29 = (bf16[2048,512]{1,0:T(8,128)(2,1)}, bf16[2048,512]{1,0:T(8,128)(2,1)}, u32[]{:S(2)}, u32[]{:S(2)}) collective-permute-start(bf16[2048,512]{1,0:T(8,128)(2,1)} %collective-permute-done.28.p2), channel_id=1, source_target_pairs={{0,4},{4,0},{8,12},{12,8},{1,5},{5,1},{9,13},{13,9},{2,6},{6,2},{1... | collective-permute-start | bytes 6291464 | tf_op jit(solution)/shard_map/ppermute | solution.py:103
  102.4 81.1 %collective-permute-done.near = bf16[8192,512]{1,0:T(8,128)(2,1)S(1)} collective-permute-done((bf16[8192,512]{1,0:T(8,128)(2,1)}, bf16[8192,512]{1,0:T(8,128)(2,1)S(1)}, u32[]{:S(2)}, u32[]{:S(2)}) %collective-permute-start) | collective-permute-done | bytes 8388640 | tf_op jit(solution)/shard_map/ppermute | solution.py:100
  184.0 3.0 fusion
  187.0 1.8 copy-done
  190.1 1.6 collective-permute-start.32
  191.8 9.5 %collective-permute-start.30 = (bf16[1024,512]{1,0:T(8,128)(2,1)}, bf16[1024,512]{1,0:T(8,128)(2,1)}, u32[]{:S(2)}, u32[]{:S(2)}) collective-permute-start(bf16[1024,512]{1,0:T(8,128)(2,1)} %get-tuple-element.6), channel_id=1, source_target_pairs={{0,0},{4,8},{8,4},{12,12},{1,1},{5,9},{9,5},{13,13},{2,2},{6,10},{... | collective-permute-start | bytes 3145736 | tf_op jit(solution)/shard_map/ppermute | solution.py:104
  201.3 1.9 collective-permute-start.26
  203.2 15.4 %collective-permute-start.33 = (bf16[1024,512]{1,0:T(8,128)(2,1)}, bf16[1024,512]{1,0:T(8,128)(2,1)}, u32[]{:S(2)}, u32[]{:S(2)}) collective-permute-start(bf16[1024,512]{1,0:T(8,128)(2,1)} %collective-permute-done.32.p4), channel_id=1, source_target_pairs={{0,4},{4,0},{8,12},{12,8},{1,5},{5,1},{9,13},{13,9},{2,6},{6,2},{1... | collective-permute-start | bytes 3145736 | tf_op jit(solution)/shard_map/ppermute | solution.py:105
  218.6 10.0 %collective-permute-done.29.p3 = bf16[2048,512]{1,0:T(8,128)(2,1)} collective-permute-done((bf16[2048,512]{1,0:T(8,128)(2,1)}, bf16[2048,512]{1,0:T(8,128)(2,1)}, u32[]{:S(2)}, u32[]{:S(2)}) %collective-permute-start.29) | collective-permute-done | bytes 2097184 | tf_op jit(solution)/shard_map/ppermute | solution.py:103
  228.6 1.9 collective-permute-start.24
  230.5 10.6 %collective-permute-start.31 = (bf16[1024,512]{1,0:T(8,128)(2,1)}, bf16[1024,512]{1,0:T(8,128)(2,1)S(1)}, u32[]{:S(2)}, u32[]{:S(2)}) collective-permute-start(bf16[1024,512]{1,0:T(8,128)(2,1)} %collective-permute-done.30.p4), channel_id=1, source_target_pairs={{0,4},{4,0},{8,12},{12,8},{1,5},{5,1},{9,13},{13,9},{2,6},{6,2},{1... | collective-permute-start | bytes 3145736 | tf_op jit(solution)/shard_map/ppermute | solution.py:105
  241.2 1.7 copy-done.5
  242.9 1.7 copy-done.7
  244.6 1.6 copy-done.9
  246.2 1.6 copy-done.11
  248.9 2.2 copy-done.1
  251.9 21.7 %collective-permute-done.23.p3 = bf16[2048,512]{1,0:T(8,128)(2,1)} collective-permute-done((bf16[2048,512]{1,0:T(8,128)(2,1)}, bf16[2048,512]{1,0:T(8,128)(2,1)}, u32[]{:S(2)}, u32[]{:S(2)}) %collective-permute-start.23) | collective-permute-done | bytes 2097184 | tf_op jit(solution)/shard_map/ppermute | solution.py:103
  273.5 1.6 collective-permute-start.20
  275.2 2.0 collective-permute-start.18
  277.2 18.8 %collective-permute-done.33.p5 = bf16[1024,512]{1,0:T(8,128)(2,1)} collective-permute-done((bf16[1024,512]{1,0:T(8,128)(2,1)}, bf16[1024,512]{1,0:T(8,128)(2,1)}, u32[]{:S(2)}, u32[]{:S(2)}) %collective-permute-start.33) | collective-permute-done | bytes 1048608 | tf_op jit(solution)/shard_map/ppermute | solution.py:105
  296.5 11.6 %group_product.11.rest_0_ = bf16[8192,2048]{1,0:T(8,128)(2,1)} custom-call(bf16[8192,512]{1,0:T(8,128)(2,1)S(1)} %bitcast.5, bf16[8192,512]{1,0:T(8,128)(2,1)S(1)} %copy-done.1, bf16[2048,512]{1,0:T(8,128)(2,1)} %collective-permute-done.28.p2, bf16[2048,512]{1,0:T(8,128)(2,1)} %collective-permute-done.29.p3, bf16[1024,512]{1,0:T(8,128)(2,1)} %collective-permute-done.32.p4, ...), custom_call_target="tpu_custom_call" | custom-call | flops 8589934592 | bytes 8388608 | tf_op jit(solution)/shard_map/group_product/pallas_call | solution.py:44
  308.0 1.6 collective-permute-start.17
  309.7 8.7 %collective-permute-done.31.p5 = bf16[1024,512]{1,0:T(8,128)(2,1)S(1)} collective-permute-done((bf16[1024,512]{1,0:T(8,128)(2,1)}, bf16[1024,512]{1,0:T(8,128)(2,1)S(1)}, u32[]{:S(2)}, u32[]{:S(2)}) %collective-permute-start.31) | collective-permute-done | bytes 1048608 | tf_op jit(solution)/shard_map/ppermute | solution.py:105
  318.8 11.5 %group_product.12.rest_0_ = bf16[8192,2048]{1,0:T(8,128)(2,1)} custom-call(bf16[8192,512]{1,0:T(8,128)(2,1)S(1)} %bitcast.5, bf16[8192,512]{1,0:T(8,128)(2,1)S(1)} %copy-done.1, bf16[2048,512]{1,0:T(8,128)(2,1)} %collective-permute-done.28.p2, bf16[2048,512]{1,0:T(8,128)(2,1)} %collective-permute-done.29.p3, ...), custom_call_target="tpu_custom_call", output_to_operand_aliasing={{}: (7, {})} | custom-call | flops 8589934592 | bytes 8388608 | tf_op jit(solution)/shard_map/group_product/pallas_call | solution.py:44
  330.3 1.6 collective-permute-start.2
  331.9 9.5 %collective-permute-start.14 = (bf16[1024,512]{1,0:T(8,128)(2,1)}, bf16[1024,512]{1,0:T(8,128)(2,1)}, u32[]{:S(2)}, u32[]{:S(2)}) collective-permute-start(bf16[1024,512]{1,0:T(8,128)(2,1)} %get-tuple-element.11), channel_id=1, source_target_pairs={{0,0},{4,8},{8,4},{12,12},{1,1},{5,9},{9,5},{13,13},{2,2},{6,10},{... | collective-permute-start | bytes 3145736 | tf_op jit(solution)/shard_map/ppermute | solution.py:104
  341.4 11.5 %group_product.13.rest_0_ = bf16[8192,2048]{1,0:T(8,128)(2,1)} custom-call(bf16[8192,512]{1,0:T(8,128)(2,1)S(1)} %bitcast.5, bf16[8192,512]{1,0:T(8,128)(2,1)S(1)} %copy-done.1, bf16[2048,512]{1,0:T(8,128)(2,1)} %collective-permute-done.22.p2, bf16[2048,512]{1,0:T(8,128)(2,1)} %collective-permute-done.23.p3, ...), custom_call_target="tpu_custom_call", output_to_operand_aliasing={{}: (7, {})} | custom-call | flops 8589934592 | bytes 8388608 | tf_op jit(solution)/shard_map/group_product/pallas_call | solution.py:44
  352.9 55.5 %collective-permute-done.25.p5 = bf16[1024,512]{1,0:T(8,128)(2,1)} collective-permute-done((bf16[1024,512]{1,0:T(8,128)(2,1)S(1)}, bf16[1024,512]{1,0:T(8,128)(2,1)}, u32[]{:S(2)}, u32[]{:S(2)}) %collective-permute-start.25) | collective-permute-done | bytes 1048608 | tf_op jit(solution)/shard_map/ppermute | solution.py:105
  408.8 11.5 %group_product.14.rest_0_ = bf16[8192,2048]{1,0:T(8,128)(2,1)} custom-call(bf16[8192,512]{1,0:T(8,128)(2,1)S(1)} %bitcast.5, bf16[8192,512]{1,0:T(8,128)(2,1)S(1)} %copy-done.1, bf16[2048,512]{1,0:T(8,128)(2,1)} %collective-permute-done.22.p2, bf16[2048,512]{1,0:T(8,128)(2,1)} %collective-permute-done.23.p3, ...), custom_call_target="tpu_custom_call", output_to_operand_aliasing={{}: (7, {})} | custom-call | flops 8589934592 | bytes 8388608 | tf_op jit(solution)/shard_map/group_product/pallas_call | solution.py:44
  421.9 53.8 %collective-permute-done.21.p5 = bf16[1024,512]{1,0:T(8,128)(2,1)S(1)} collective-permute-done((bf16[1024,512]{1,0:T(8,128)(2,1)}, bf16[1024,512]{1,0:T(8,128)(2,1)S(1)}, u32[]{:S(2)}, u32[]{:S(2)}) %collective-permute-start.21) | collective-permute-done | bytes 1048608 | tf_op jit(solution)/shard_map/ppermute | solution.py:105
  478.3 11.3 %group_product.15.rest_0_ = bf16[8192,2048]{1,0:T(8,128)(2,1)} custom-call(bf16[8192,512]{1,0:T(8,128)(2,1)S(1)} %bitcast.5, bf16[8192,512]{1,0:T(8,128)(2,1)S(1)} %copy-done.1, bf16[2048,512]{1,0:T(8,128)(2,1)S(1)} %copy-done.3, bf16[2048,512]{1,0:T(8,128)(2,1)S(1)} %collective-permute-done.17.p3, ...), custom_call_target="tpu_custom_call", output_to_operand_aliasing={{}: (7, {})} | custom-call | flops 8589934592 | bytes 8388608 | tf_op jit(solution)/shard_map/group_product/pallas_call | solution.py:44
  490.3 7.8 %collective-permute-done.19.p5 = bf16[1024,512]{1,0:T(8,128)(2,1)S(1)} collective-permute-done((bf16[1024,512]{1,0:T(8,128)(2,1)S(1)}, bf16[1024,512]{1,0:T(8,128)(2,1)S(1)}, u32[]{:S(2)}, u32[]{:S(2)}) %collective-permute-start.19) | collective-permute-done | bytes 1048608 | tf_op jit(solution)/shard_map/ppermute | solution.py:105
  498.8 10.4 %group_product.16.rest_0_ = bf16[8192,2048]{1,0:T(8,128)(2,1)} custom-call(bf16[8192,512]{1,0:T(8,128)(2,1)S(1)} %bitcast.5, bf16[8192,512]{1,0:T(8,128)(2,1)S(1)} %copy-done.1, bf16[2048,512]{1,0:T(8,128)(2,1)S(1)} %copy-done.3, bf16[2048,512]{1,0:T(8,128)(2,1)S(1)} %collective-permute-done.17.p3, ...), custom_call_target="tpu_custom_call", output_to_operand_aliasing={{}: (7, {})} | custom-call | flops 8589934592 | bytes 8388608 | tf_op jit(solution)/shard_map/group_product/pallas_call | solution.py:44
  509.2 2.1 collective-permute-start.9
  511.4 2.0 collective-permute-start.11
  513.4 7.2 %collective-permute-done.15.p5 = bf16[1024,512]{1,0:T(8,128)(2,1)S(1)} collective-permute-done((bf16[1024,512]{1,0:T(8,128)(2,1)}, bf16[1024,512]{1,0:T(8,128)(2,1)S(1)}, u32[]{:S(2)}, u32[]{:S(2)}) %collective-permute-start.15) | collective-permute-done | bytes 1048608 | tf_op jit(solution)/shard_map/ppermute | solution.py:105
  520.6 11.3 %group_product.17.rest_0_ = bf16[8192,2048]{1,0:T(8,128)(2,1)} custom-call(bf16[8192,512]{1,0:T(8,128)(2,1)S(1)} %bitcast.5, bf16[8192,512]{1,0:T(8,128)(2,1)S(1)} %copy-done.1, bf16[2048,512]{1,0:T(8,128)(2,1)S(1)} %collective-permute-done.1.p2, bf16[2048,512]{1,0:T(8,128)(2,1)S(1)} %collective-permute-done.2.p3, ...), custom_call_target="tpu_custom_call", output_to_operand_aliasing={{}: (7, {})} | custom-call | flops 8589934592 | bytes 8388608 | tf_op jit(solution)/shard_map/group_product/pallas_call | solution.py:44
  531.9 10.0 %collective-permute-done.13.p5 = bf16[512,512]{1,0:T(8,128)(2,1)S(1)} collective-permute-done((bf16[512,512]{1,0:T(8,128)(2,1)S(1)}, bf16[512,512]{1,0:T(8,128)(2,1)S(1)}, u32[]{:S(2)}, u32[]{:S(2)}) %collective-permute-start.13) | collective-permute-done | bytes 524320 | tf_op jit(solution)/shard_map/ppermute | solution.py:105
  541.9 5.6 %group_product.18.rest_0_ = bf16[8192,2048]{1,0:T(8,128)(2,1)} custom-call(bf16[8192,512]{1,0:T(8,128)(2,1)S(1)} %bitcast.5, bf16[8192,512]{1,0:T(8,128)(2,1)S(1)} %copy-done.1, bf16[2048,512]{1,0:T(8,128)(2,1)S(1)} %collective-permute-done.1.p2, bf16[2048,512]{1,0:T(8,128)(2,1)S(1)} %collective-permute-done.2.p3, ...), custom_call_target="tpu_custom_call", output_to_operand_aliasing={{}: (7, {})} | custom-call | flops 4294967296 | bytes 4194304 | tf_op jit(solution)/shard_map/group_product/pallas_call | solution.py:44
  547.6 3.3 group_product.19.rest_0_
  550.9 2.1 group_product.20.rest_0_
  553.0 2.1 group_product.21
  (75 shorter events, 16.7 us)
Async XLA Ops:
  0.0 48.1 %copy-start.4 = (bf16[512,2048]{1,0:T(8,128)(2,1)S(1)}, bf16[512,2048]{1,0:T(8,128)(2,1)}, u32[]{:S(2)}) copy-start(bf16[512,2048]{1,0:T(8,128)(2,1)} %refs_0_.1) | copy-start | bytes 6291460
  0.0 183.5 %collective-permute-start = (bf16[8192,512]{1,0:T(8,128)(2,1)}, bf16[8192,512]{1,0:T(8,128)(2,1)S(1)}, u32[]{:S(2)}, u32[]{:S(2)}) collective-permute-start(bf16[8192,512]{1,0:T(8,128)(2,1)} %own.21), channel_id=1, source_target_pairs={{0,4},{4,0},{8,12},{12,8},{1,5},{5,1},{9,13},{13,9},{2,6},{6,2},{1... | collective-permute-start | bytes 25165832 | tf_op jit(solution)/shard_map/ppermute | solution.py:100
  0.5 46.3 %collective-permute-start.5 = (bf16[512,2048]{1,0:T(8,128)(2,1)}, bf16[512,2048]{1,0:T(8,128)(2,1)S(1)}, u32[]{:S(2)}, u32[]{:S(2)}) collective-permute-start(bf16[512,2048]{1,0:T(8,128)(2,1)} %refs_0_.1), channel_id=1, source_target_pairs={{0,3},{1,0},{2,1},{3,2},{4,7},{5,4},{6,5},{7,6},{8,11},{9,8},{10,9... | collective-permute-start | bytes 6291464 | tf_op jit(solution)/shard_map/ppermute | solution.py:108
  0.5 89.7 %collective-permute-start.6 = (bf16[512,2048]{1,0:T(8,128)(2,1)}, bf16[512,2048]{1,0:T(8,128)(2,1)S(1)}, u32[]{:S(2)}, u32[]{:S(2)}) collective-permute-start(bf16[512,2048]{1,0:T(8,128)(2,1)} %refs_0_.1), channel_id=1, source_target_pairs={{0,2},{1,3},{2,0},{3,1},{4,6},{5,7},{6,4},{7,5},{8,10},{9,11},{10,... | collective-permute-start | bytes 6291464 | tf_op jit(solution)/shard_map/ppermute | solution.py:108
  5.4 87.0 %collective-permute-start.28 = (bf16[2048,512]{1,0:T(8,128)(2,1)S(1)}, bf16[2048,512]{1,0:T(8,128)(2,1)}, u32[]{:S(2)}, u32[]{:S(2)}) collective-permute-start(bf16[2048,512]{1,0:T(8,128)(2,1)S(1)} %get-tuple-element.12), channel_id=1, source_target_pairs={{0,0},{4,8},{8,4},{12,12},{1,1},{5,9},{9,5},{13,13},{2,2},{6,10},{... | collective-permute-start | bytes 6291464 | tf_op jit(solution)/shard_map/ppermute | solution.py:102
  7.4 85.8 %collective-permute-start.22 = (bf16[2048,512]{1,0:T(8,128)(2,1)S(1)}, bf16[2048,512]{1,0:T(8,128)(2,1)}, u32[]{:S(2)}, u32[]{:S(2)}) collective-permute-start(bf16[2048,512]{1,0:T(8,128)(2,1)S(1)} %get-tuple-element.13), channel_id=1, source_target_pairs={{0,0},{4,8},{8,4},{12,12},{1,1},{5,9},{9,5},{13,13},{2,2},{6,10},{... | collective-permute-start | bytes 6291464 | tf_op jit(solution)/shard_map/ppermute | solution.py:102
  48.1 140.8 %collective-permute-start.7 = (bf16[512,2048]{1,0:T(8,128)(2,1)S(1)}, bf16[512,2048]{1,0:T(8,128)(2,1)S(1)}, u32[]{:S(2)}, u32[]{:S(2)}) collective-permute-start(bf16[512,2048]{1,0:T(8,128)(2,1)S(1)} %copy-done.4), channel_id=1, source_target_pairs={{0,1},{1,2},{2,3},{3,0},{4,5},{5,6},{6,7},{7,4},{8,9},{9,10},{10,1... | collective-permute-start | bytes 6291464 | tf_op jit(solution)/shard_map/ppermute | solution.py:108
  90.2 1.4 copy-start.8
  91.6 100.2 %collective-permute-start.16 = (bf16[2048,512]{1,0:T(8,128)(2,1)S(1)}, bf16[2048,512]{1,0:T(8,128)(2,1)S(1)}, u32[]{:S(2)}, u32[]{:S(2)}) collective-permute-start(bf16[2048,512]{1,0:T(8,128)(2,1)S(1)} %get-tuple-element.14), channel_id=1, source_target_pairs={{0,0},{4,8},{8,4},{12,12},{1,1},{5,9},{9,5},{13,13},{2,2},{6,10},{... | collective-permute-start | bytes 6291464 | tf_op jit(solution)/shard_map/ppermute | solution.py:102
  92.4 108.9 %collective-permute-start.1 = (bf16[2048,512]{1,0:T(8,128)(2,1)S(1)}, bf16[2048,512]{1,0:T(8,128)(2,1)S(1)}, u32[]{:S(2)}, u32[]{:S(2)}) collective-permute-start(bf16[2048,512]{1,0:T(8,128)(2,1)S(1)} %get-tuple-element.15), channel_id=1, source_target_pairs={{0,0},{4,8},{8,4},{12,12},{1,1},{5,9},{9,5},{13,13},{2,2},{6,10},{... | collective-permute-start | bytes 6291464 | tf_op jit(solution)/shard_map/ppermute | solution.py:102
  93.2 135.4 %collective-permute-start.29 = (bf16[2048,512]{1,0:T(8,128)(2,1)}, bf16[2048,512]{1,0:T(8,128)(2,1)}, u32[]{:S(2)}, u32[]{:S(2)}) collective-permute-start(bf16[2048,512]{1,0:T(8,128)(2,1)} %collective-permute-done.28.p2), channel_id=1, source_target_pairs={{0,4},{4,0},{8,12},{12,8},{1,5},{5,1},{9,13},{13,9},{2,6},{6,2},{1... | collective-permute-start | bytes 6291464 | tf_op jit(solution)/shard_map/ppermute | solution.py:103
  183.5 5.3 copy-start
  183.5 90.0 %collective-permute-start.23 = (bf16[2048,512]{1,0:T(8,128)(2,1)}, bf16[2048,512]{1,0:T(8,128)(2,1)}, u32[]{:S(2)}, u32[]{:S(2)}) collective-permute-start(bf16[2048,512]{1,0:T(8,128)(2,1)} %collective-permute-done.22.p2), channel_id=1, source_target_pairs={{0,4},{4,0},{8,12},{12,8},{1,5},{5,1},{9,13},{13,9},{2,6},{6,2},{1... | collective-permute-start | bytes 6291464 | tf_op jit(solution)/shard_map/ppermute | solution.py:103
  190.1 13.1 %collective-permute-start.32 = (bf16[1024,512]{1,0:T(8,128)(2,1)S(1)}, bf16[1024,512]{1,0:T(8,128)(2,1)}, u32[]{:S(2)}, u32[]{:S(2)}) collective-permute-start(bf16[1024,512]{1,0:T(8,128)(2,1)S(1)} %get-tuple-element.5), channel_id=1, source_target_pairs={{0,0},{4,8},{8,4},{12,12},{1,1},{5,9},{9,5},{13,13},{2,2},{6,10},{... | collective-permute-start | bytes 3145736 | tf_op jit(solution)/shard_map/ppermute | solution.py:104
  191.8 9.6 %copy-start.2 = (bf16[2048,512]{1,0:T(8,128)(2,1)}, bf16[2048,512]{1,0:T(8,128)(2,1)S(1)}, u32[]{:S(2)}) copy-start(bf16[2048,512]{1,0:T(8,128)(2,1)S(1)} %collective-permute-done.16.p2) | copy-start | bytes 6291460
  191.8 38.7 %collective-permute-start.30 = (bf16[1024,512]{1,0:T(8,128)(2,1)}, bf16[1024,512]{1,0:T(8,128)(2,1)}, u32[]{:S(2)}, u32[]{:S(2)}) collective-permute-start(bf16[1024,512]{1,0:T(8,128)(2,1)} %get-tuple-element.6), channel_id=1, source_target_pairs={{0,0},{4,8},{8,4},{12,12},{1,1},{5,9},{9,5},{13,13},{2,2},{6,10},{... | collective-permute-start | bytes 3145736 | tf_op jit(solution)/shard_map/ppermute | solution.py:104
  201.3 73.8 %collective-permute-start.26 = (bf16[1024,512]{1,0:T(8,128)(2,1)}, bf16[1024,512]{1,0:T(8,128)(2,1)S(1)}, u32[]{:S(2)}, u32[]{:S(2)}) collective-permute-start(bf16[1024,512]{1,0:T(8,128)(2,1)} %get-tuple-element.7), channel_id=1, source_target_pairs={{0,0},{4,8},{8,4},{12,12},{1,1},{5,9},{9,5},{13,13},{2,2},{6,10},{... | collective-permute-start | bytes 3145736 | tf_op jit(solution)/shard_map/ppermute | solution.py:104
  203.2 92.8 %collective-permute-start.33 = (bf16[1024,512]{1,0:T(8,128)(2,1)}, bf16[1024,512]{1,0:T(8,128)(2,1)}, u32[]{:S(2)}, u32[]{:S(2)}) collective-permute-start(bf16[1024,512]{1,0:T(8,128)(2,1)} %collective-permute-done.32.p4), channel_id=1, source_target_pairs={{0,4},{4,0},{8,12},{12,8},{1,5},{5,1},{9,13},{13,9},{2,6},{6,2},{1... | collective-permute-start | bytes 3145736 | tf_op jit(solution)/shard_map/ppermute | solution.py:105
  228.6 79.5 %collective-permute-start.24 = (bf16[1024,512]{1,0:T(8,128)(2,1)}, bf16[1024,512]{1,0:T(8,128)(2,1)S(1)}, u32[]{:S(2)}, u32[]{:S(2)}) collective-permute-start(bf16[1024,512]{1,0:T(8,128)(2,1)} %get-tuple-element.8), channel_id=1, source_target_pairs={{0,0},{4,8},{8,4},{12,12},{1,1},{5,9},{9,5},{13,13},{2,2},{6,10},{... | collective-permute-start | bytes 3145736 | tf_op jit(solution)/shard_map/ppermute | solution.py:104
  230.5 87.9 %collective-permute-start.31 = (bf16[1024,512]{1,0:T(8,128)(2,1)}, bf16[1024,512]{1,0:T(8,128)(2,1)S(1)}, u32[]{:S(2)}, u32[]{:S(2)}) collective-permute-start(bf16[1024,512]{1,0:T(8,128)(2,1)} %collective-permute-done.30.p4), channel_id=1, source_target_pairs={{0,4},{4,0},{8,12},{12,8},{1,5},{5,1},{9,13},{13,9},{2,6},{6,2},{1... | collective-permute-start | bytes 3145736 | tf_op jit(solution)/shard_map/ppermute | solution.py:105
  241.1 55.4 %slice-start = ((s8[8388608]{0:T(1024)(128)(4,1)}), s8[4194304]{0:T(1024)(128)(4,1)S(1)}, s32[]{:S(2)}) async-start(s8[8388608]{0:T(1024)(128)(4,1)} %bitcast.4), calls=%async_computation | async-start | bytes 8388608
  241.2 1.7 copy-start.5
  242.9 1.7 copy-start.7
  244.6 1.6 copy-start.9
  246.2 1.6 copy-start.11
  247.7 3.4 copy-start.1
  247.7 48.7 %slice-start.1 = ((s8[8388608]{0:T(1024)(128)(4,1)}), s8[4194304]{0:T(1024)(128)(4,1)S(1)}, s32[]{:S(2)}) async-start(s8[8388608]{0:T(1024)(128)(4,1)} %bitcast.4), calls=%async_computation.1 | async-start | bytes 8388608
  251.1 22.4 %copy-start.14 = (bf16[1024,512]{1,0:T(8,128)(2,1)S(1)}, bf16[1024,512]{1,0:T(8,128)(2,1)}, u32[]{:S(2)}) copy-start(bf16[1024,512]{1,0:T(8,128)(2,1)} %get-tuple-element.9) | copy-start | bytes 3145732
  273.5 56.8 %collective-permute-start.20 = (bf16[1024,512]{1,0:T(8,128)(2,1)S(1)}, bf16[1024,512]{1,0:T(8,128)(2,1)}, u32[]{:S(2)}, u32[]{:S(2)}) collective-permute-start(bf16[1024,512]{1,0:T(8,128)(2,1)S(1)} %copy-done.14), channel_id=1, source_target_pairs={{0,0},{4,8},{8,4},{12,12},{1,1},{5,9},{9,5},{13,13},{2,2},{6,10},{... | collective-permute-start | bytes 3145736 | tf_op jit(solution)/shard_map/ppermute | solution.py:104
  275.2 32.9 %copy-start.3 = (bf16[2048,512]{1,0:T(8,128)(2,1)S(1)}, bf16[2048,512]{1,0:T(8,128)(2,1)}, u32[]{:S(2)}) copy-start(bf16[2048,512]{1,0:T(8,128)(2,1)} %copy-done.2) | copy-start | bytes 6291460
  275.2 56.7 %collective-permute-start.18 = (bf16[1024,512]{1,0:T(8,128)(2,1)}, bf16[1024,512]{1,0:T(8,128)(2,1)S(1)}, u32[]{:S(2)}, u32[]{:S(2)}) collective-permute-start(bf16[1024,512]{1,0:T(8,128)(2,1)} %get-tuple-element.10), channel_id=1, source_target_pairs={{0,0},{4,8},{8,4},{12,12},{1,1},{5,9},{9,5},{13,13},{2,2},{6,10},{... | collective-permute-start | bytes 3145736 | tf_op jit(solution)/shard_map/ppermute | solution.py:104
  296.0 45.4 %collective-permute-start.27 = (bf16[1024,512]{1,0:T(8,128)(2,1)S(1)}, bf16[1024,512]{1,0:T(8,128)(2,1)}, u32[]{:S(2)}, u32[]{:S(2)}) collective-permute-start(bf16[1024,512]{1,0:T(8,128)(2,1)S(1)} %collective-permute-done.26.p4), channel_id=1, source_target_pairs={{0,4},{4,0},{8,12},{12,8},{1,5},{5,1},{9,13},{13,9},{2,6},{6,2},{1... | collective-permute-start | bytes 3145736 | tf_op jit(solution)/shard_map/ppermute | solution.py:105
  308.0 112.3 %collective-permute-start.17 = (bf16[2048,512]{1,0:T(8,128)(2,1)S(1)}, bf16[2048,512]{1,0:T(8,128)(2,1)S(1)}, u32[]{:S(2)}, u32[]{:S(2)}) collective-permute-start(bf16[2048,512]{1,0:T(8,128)(2,1)S(1)} %copy-done.3), channel_id=1, source_target_pairs={{0,4},{4,0},{8,12},{12,8},{1,5},{5,1},{9,13},{13,9},{2,6},{6,2},{1... | collective-permute-start | bytes 6291464 | tf_op jit(solution)/shard_map/ppermute | solution.py:103
  318.4 90.0 %collective-permute-start.25 = (bf16[1024,512]{1,0:T(8,128)(2,1)S(1)}, bf16[1024,512]{1,0:T(8,128)(2,1)}, u32[]{:S(2)}, u32[]{:S(2)}) collective-permute-start(bf16[1024,512]{1,0:T(8,128)(2,1)S(1)} %collective-permute-done.24.p4), channel_id=1, source_target_pairs={{0,4},{4,0},{8,12},{12,8},{1,5},{5,1},{9,13},{13,9},{2,6},{6,2},{1... | collective-permute-start | bytes 3145736 | tf_op jit(solution)/shard_map/ppermute | solution.py:105
  330.3 159.4 %collective-permute-start.2 = (bf16[2048,512]{1,0:T(8,128)(2,1)S(1)}, bf16[2048,512]{1,0:T(8,128)(2,1)S(1)}, u32[]{:S(2)}, u32[]{:S(2)}) collective-permute-start(bf16[2048,512]{1,0:T(8,128)(2,1)S(1)} %collective-permute-done.1.p2), channel_id=1, source_target_pairs={{0,4},{4,0},{8,12},{12,8},{1,5},{5,1},{9,13},{13,9},{2,6},{6,2},{1... | collective-permute-start | bytes 6291464 | tf_op jit(solution)/shard_map/ppermute | solution.py:103
  331.9 89.1 %collective-permute-start.14 = (bf16[1024,512]{1,0:T(8,128)(2,1)}, bf16[1024,512]{1,0:T(8,128)(2,1)}, u32[]{:S(2)}, u32[]{:S(2)}) collective-permute-start(bf16[1024,512]{1,0:T(8,128)(2,1)} %get-tuple-element.11), channel_id=1, source_target_pairs={{0,0},{4,8},{8,4},{12,12},{1,1},{5,9},{9,5},{13,13},{2,2},{6,10},{... | collective-permute-start | bytes 3145736 | tf_op jit(solution)/shard_map/ppermute | solution.py:104
  341.4 134.3 %collective-permute-start.21 = (bf16[1024,512]{1,0:T(8,128)(2,1)}, bf16[1024,512]{1,0:T(8,128)(2,1)S(1)}, u32[]{:S(2)}, u32[]{:S(2)}) collective-permute-start(bf16[1024,512]{1,0:T(8,128)(2,1)} %collective-permute-done.20.p4), channel_id=1, source_target_pairs={{0,4},{4,0},{8,12},{12,8},{1,5},{5,1},{9,13},{13,9},{2,6},{6,2},{1... | collective-permute-start | bytes 3145736 | tf_op jit(solution)/shard_map/ppermute | solution.py:105
  408.4 89.8 %collective-permute-start.19 = (bf16[1024,512]{1,0:T(8,128)(2,1)S(1)}, bf16[1024,512]{1,0:T(8,128)(2,1)S(1)}, u32[]{:S(2)}, u32[]{:S(2)}) collective-permute-start(bf16[1024,512]{1,0:T(8,128)(2,1)S(1)} %collective-permute-done.18.p4), channel_id=1, source_target_pairs={{0,4},{4,0},{8,12},{12,8},{1,5},{5,1},{9,13},{13,9},{2,6},{6,2},{1... | collective-permute-start | bytes 3145736 | tf_op jit(solution)/shard_map/ppermute | solution.py:105
  420.3 93.0 %collective-permute-start.12 = (bf16[512,512]{1,0:T(8,128)(2,1)S(1)}, bf16[512,512]{1,0:T(8,128)(2,1)S(1)}, u32[]{:S(2)}, u32[]{:S(2)}) collective-permute-start(bf16[512,512]{1,0:T(8,128)(2,1)S(1)} %slice.63), channel_id=1, source_target_pairs={{0,0},{4,8},{8,4},{12,12},{1,1},{5,9},{9,5},{13,13},{2,2},{6,10},{... | collective-permute-start | bytes 1572872 | tf_op jit(solution)/shard_map/ppermute | solution.py:104
  421.0 90.4 %collective-permute-start.10 = (bf16[256,512]{1,0:T(8,128)(2,1)S(1)}, bf16[256,512]{1,0:T(8,128)(2,1)S(1)}, u32[]{:S(2)}, u32[]{:S(2)}) collective-permute-start(bf16[256,512]{1,0:T(8,128)(2,1)S(1)} %slice.62), channel_id=1, source_target_pairs={{0,0},{4,8},{8,4},{12,12},{1,1},{5,9},{9,5},{13,13},{2,2},{6,10},{... | collective-permute-start | bytes 786440 | tf_op jit(solution)/shard_map/ppermute | solution.py:104
  476.6 44.0 %collective-permute-start.15 = (bf16[1024,512]{1,0:T(8,128)(2,1)}, bf16[1024,512]{1,0:T(8,128)(2,1)S(1)}, u32[]{:S(2)}, u32[]{:S(2)}) collective-permute-start(bf16[1024,512]{1,0:T(8,128)(2,1)} %collective-permute-done.14.p4), channel_id=1, source_target_pairs={{0,4},{4,0},{8,12},{12,8},{1,5},{5,1},{9,13},{13,9},{2,6},{6,2},{1... | collective-permute-start | bytes 3145736 | tf_op jit(solution)/shard_map/ppermute | solution.py:105
  478.3 11.4 %copy-start.15 = (bf16[128,512]{1,0:T(8,128)(2,1)S(1)}, bf16[128,512]{1,0:T(8,128)(2,1)}, u32[]{:S(2)}) copy-start(bf16[128,512]{1,0:T(8,128)(2,1)} %get-tuple-element.16) | copy-start | bytes 393220
  489.7 19.5 %collective-permute-start.8 = (bf16[128,512]{1,0:T(8,128)(2,1)S(1)}, bf16[128,512]{1,0:T(8,128)(2,1)S(1)}, u32[]{:S(2)}, u32[]{:S(2)}) collective-permute-start(bf16[128,512]{1,0:T(8,128)(2,1)S(1)} %copy-done.15), channel_id=1, source_target_pairs={{0,0},{4,8},{8,4},{12,12},{1,1},{5,9},{9,5},{13,13},{2,2},{6,10},{... | collective-permute-start | bytes 393224 | tf_op jit(solution)/shard_map/ppermute | solution.py:104
  498.1 13.2 %collective-permute-start.3 = (bf16[128,512]{1,0:T(8,128)(2,1)S(1)}, bf16[128,512]{1,0:T(8,128)(2,1)S(1)}, u32[]{:S(2)}, u32[]{:S(2)}) collective-permute-start(bf16[128,512]{1,0:T(8,128)(2,1)S(1)} %get-tuple-element.17), channel_id=1, source_target_pairs={{0,0},{4,8},{8,4},{12,12},{1,1},{5,9},{9,5},{13,13},{2,2},{6,10},{... | collective-permute-start | bytes 393224 | tf_op jit(solution)/shard_map/ppermute | solution.py:104
  509.2 41.8 %collective-permute-start.9 = (bf16[128,512]{1,0:T(8,128)(2,1)S(1)}, bf16[128,512]{1,0:T(8,128)(2,1)S(1)}, u32[]{:S(2)}, u32[]{:S(2)}) collective-permute-start(bf16[128,512]{1,0:T(8,128)(2,1)S(1)} %collective-permute-done.8.p4), channel_id=1, source_target_pairs={{0,4},{4,0},{8,12},{12,8},{1,5},{5,1},{9,13},{13,9},{2,6},{6,2},{1... | collective-permute-start | bytes 393224 | tf_op jit(solution)/shard_map/ppermute | solution.py:105
  511.3 41.7 %collective-permute-start.4 = (bf16[128,512]{1,0:T(8,128)(2,1)S(1)}, bf16[128,512]{1,0:T(8,128)(2,1)S(1)}, u32[]{:S(2)}, u32[]{:S(2)}) collective-permute-start(bf16[128,512]{1,0:T(8,128)(2,1)S(1)} %collective-permute-done.3.p4), channel_id=1, source_target_pairs={{0,4},{4,0},{8,12},{12,8},{1,5},{5,1},{9,13},{13,9},{2,6},{6,2},{1... | collective-permute-start | bytes 393224 | tf_op jit(solution)/shard_map/ppermute | solution.py:105
  511.4 36.2 %collective-permute-start.11 = (bf16[256,512]{1,0:T(8,128)(2,1)S(1)}, bf16[256,512]{1,0:T(8,128)(2,1)S(1)}, u32[]{:S(2)}, u32[]{:S(2)}) collective-permute-start(bf16[256,512]{1,0:T(8,128)(2,1)S(1)} %collective-permute-done.10.p4), channel_id=1, source_target_pairs={{0,4},{4,0},{8,12},{12,8},{1,5},{5,1},{9,13},{13,9},{2,6},{6,2},{1... | collective-permute-start | bytes 786440 | tf_op jit(solution)/shard_map/ppermute | solution.py:105
  513.3 28.6 %collective-permute-start.13 = (bf16[512,512]{1,0:T(8,128)(2,1)S(1)}, bf16[512,512]{1,0:T(8,128)(2,1)S(1)}, u32[]{:S(2)}, u32[]{:S(2)}) collective-permute-start(bf16[512,512]{1,0:T(8,128)(2,1)S(1)} %collective-permute-done.12.p4), channel_id=1, source_target_pairs={{0,4},{4,0},{8,12},{12,8},{1,5},{5,1},{9,13},{13,9},{2,6},{6,2},{1... | collective-permute-start | bytes 1572872 | tf_op jit(solution)/shard_map/ppermute | solution.py:105
  (4 other events, 4.8 us)

commit v3 on v2

--- a/solution.py
+++ b/solution.py
@@ -9,32 +9,63 @@
 
 
 HALVES = 4
-GROUPS = (1024, 1024, 1024, 1024, 1024, 1024, 1024, 512, 256, 128, 128)
+GROUPS = (1024, 1024, 1024, 1024, 1024, 1024, 1024)
+TAIL = (512, 256, 128, 128)
 BM = 256
+
+
+def _at_end(side):
+    col_pos = lax.axis_index("col")
+    return jnp.logical_or(col_pos == 0, col_pos == side - 1)
 
 
 def _mm_kernel(side, own, near, p2, p3, p4, p5, b_ref, *rest):
     out_ref = rest[-1]
-    col_pos = lax.axis_index("col")
-    at_end = jnp.logical_or(col_pos == 0, col_pos == side - 1)
-
+    at_end = _at_end(side)
     third = jnp.where(at_end, p3[...], p4[...])
     fourth = jnp.where(at_end, p5[...], p2[...])
     lhs = jnp.concatenate([own[...], near[...], third, fourth], axis=1)
     out_ref[...] = jnp.dot(lhs, b_ref[...], preferred_element_type=jnp.float32).astype(out_ref.dtype)
 
 
+def _early_kernel(side, own, near, p3, p4, b_ref, out_ref):
+    third = jnp.where(_at_end(side), p3[...], p4[...])
+    lhs = jnp.concatenate([own[...], near[...], third], axis=1)
+    out_ref[...] = jnp.dot(lhs, b_ref[: lhs.shape[1], :], preferred_element_type=jnp.float32)
+
+
+def _late_kernel(side, p2, p5, b_ref, early, c_in, out_ref):
+    fourth = jnp.where(_at_end(side), p5[...], p2[...])
+    depth = fourth.shape[1]
+    total = early[...] + jnp.dot(fourth, b_ref[-depth:, :], preferred_element_type=jnp.float32)
+    out_ref[...] = total.astype(out_ref.dtype)
+
+
+def _rows(bm, depth, off):
+    return pl.BlockSpec((bm, depth), lambda i: (off // bm + i, 0))
+
+
+def _kept(shape):
+    return pl.BlockSpec(shape, lambda i: (0, 0), pipeline_mode=pl.Buffered(1))
+
+
+def _params(vmem_mib):
+    return pltpu.CompilerParams(dimension_semantics=("arbitrary",), vmem_limit_bytes=vmem_mib * 2**20)
+
+
+def _cost(size, depth, cols):
+    return pl.CostEstimate(
+        flops=2 * size * depth * cols, bytes_accessed=2 * size * (depth + cols), transcendentals=0
+    )
+
+
 def _group_product(side, a, near, p2, p3, p4, p5, b, c, off, size):
-    bm = BM if size > BM else BM // 2
     rows, depth = a.shape
     total, cols = b.shape
-    base = off % p2.shape[0]
-    piece = pl.BlockSpec((bm, depth), lambda i: (i, 0))
-    chunk = pl.BlockSpec((bm, depth), lambda i: (base // bm + i, 0))
-    full = pl.BlockSpec((bm, depth), lambda i: (off // bm + i, 0))
-    whole = pl.BlockSpec((total, cols), lambda i: (0, 0), pipeline_mode=pl.Buffered(1))
-    out = pl.BlockSpec((bm, cols), lambda i: (off // bm + i, 0))
-    in_specs = [full, full, chunk, chunk, piece, piece, whole]
+    full = _rows(BM, depth, off)
+    chunk = _rows(BM, depth, off % p2.shape[0])
+    piece = _rows(BM, depth, 0)
+    in_specs = [full, full, chunk, chunk, piece, piece, _kept(b.shape)]
     args = [a, near, p2, p3, p4, p5, b]
     alias = {}
     if c is not None:
@@ -43,19 +74,52 @@
         alias = {7: 0}
     return pl.pallas_call(
         functools.partial(_mm_kernel, side),
+        grid=(size // BM,),
+        out_shape=jax.ShapeDtypeStruct((rows, cols), jnp.bfloat16),
+        in_specs=in_specs,
+        out_specs=_rows(BM, cols, off),
+        input_output_aliases=alias,
+        compiler_params=_params(16),
+        cost_estimate=_cost(size, total, cols),
+        name="group_product",
+    )(*args)
+
+
+def _early_product(side, a, near, p3, p4, b, off, size):
+    depth = a.shape[1]
+    cols = b.shape[1]
+    bm = min(BM, size)
+    full = _rows(bm, depth, off)
+    return pl.pallas_call(
+        functools.partial(_early_kernel, side),
+        grid=(size // bm,),
+        out_shape=pltpu.VMEM((size, cols), jnp.float32),
+        in_specs=[full, full, _rows(bm, depth, off % p3.shape[0]), _rows(bm, depth, 0), _kept(b.shape)],
+        out_specs=_rows(bm, cols, 0),
+        compiler_params=_params(20),
+        cost_estimate=_cost(size, 3 * depth, cols),
+        name="early_product",
+    )(a, near, p3, p4, b)
+
+
+def _late_product(side, p2, p5, b, early, c, off, size):
+    depth = p5.shape[1]
+    rows, cols = c.shape
+    bm = BM // 2
+    return pl.pallas_call(
+        functools.partial(_late_kernel, side),
         grid=(size // bm,),
         out_shape=jax.ShapeDtypeStruct((rows, cols), jnp.bfloat16),
-        in_specs=in_specs,
-        out_specs=out,
-        input_output_aliases=alias,
-        compiler_params=pltpu.CompilerParams(dimension_semantics=("arbitrary",), vmem_limit_bytes=22 * 2**20),
-        cost_estimate=pl.CostEstimate(
-            flops=2 * size * total * cols,
-            bytes_accessed=size * (total + cols) * 2,
-            transcendentals=0,
-        ),
-        name="group_product",
-    )(*args)
+        in_specs=[
+            _rows(bm, depth, off % p2.shape[0]), _rows(bm, depth, 0), _kept(b.shape), _rows(bm, cols, 0),
+            pl.BlockSpec(memory_space=pl.ANY),
+        ],
+        out_specs=_rows(bm, cols, off),
+        input_output_aliases={4: 0},
+        compiler_params=_params(16),
+        cost_estimate=_cost(size, depth, cols),
+        name="late_product",
+    )(p2, p5, b, early, c)
 
 
 def _stack_kernel(place_ref, *refs):
@@ -94,14 +158,15 @@
 
     def local(a, b_own):
         rows, _ = a.shape
-        offs = [sum(GROUPS[:g]) for g in range(len(GROUPS))]
+        sizes = GROUPS + TAIL
+        offs = [sum(sizes[:g]) for g in range(len(sizes))]
         row_pos, col_pos = lax.axis_index("row"), lax.axis_index("col")
 
         near = lax.ppermute(a, "col", with_near)
         step = rows // HALVES
         p2 = [lax.ppermute(a[h * step : (h + 1) * step], "col", inner) for h in range(HALVES)]
         p3 = [lax.ppermute(x, "col", with_near) for x in p2]
-        p4 = [lax.ppermute(near[o : o + s], "col", inner) for o, s in zip(offs, GROUPS)]
+        p4 = [lax.ppermute(near[o : o + s], "col", inner) for o, s in zip(offs, sizes)]
         p5 = [lax.ppermute(x, "col", with_near) for x in p4]
 
         blocks = [b_own] + [
@@ -109,10 +174,18 @@
         ]
         b = _stack_blocks(jnp.stack([lax.rem(row_pos + s, side) ^ col_pos for s in range(side)]), blocks)
 
+        main = len(GROUPS)
+        early = []
+        for g in range(main, len(sizes)):
+            early.append(_early_product(side, a, near, p3[offs[g] // step], p4[g], b, offs[g], sizes[g]))
+
         c = None
-        for g, (off, size) in enumerate(zip(offs, GROUPS)):
+        for g, (off, size) in enumerate(zip(offs, sizes)):
             h = off // step
-            c = _group_product(side, a, near, p2[h], p3[h], p4[g], p5[g], b, c, off, size)
+            if g < main:
+                c = _group_product(side, a, near, p2[h], p3[h], p4[g], p5[g], b, c, off, size)
+            else:
+                c = _late_product(side, p2[h], p5[g], b, early[g - main], c, off, size)
         return c
 
     return jax.shard_map(

time: 558 us -> 557 us (level)
  waiting for transfers between devices: 353 us -> 338 us
    ppermute x11, waiting for transfers between devices: 162 us -> 117 us  [local(): p5 = [lax.ppermute(x, 'col', with_near) for x in p4]]
    ppermute x4, waiting for transfers between devices: 31.6 us -> 69 us  [local(): p3 = [lax.ppermute(x, 'col', with_near) for x in p2]]
    ppermute x11, starting transfers between devices: 32.1 us -> 7.66 us  [local(): p5 = [lax.ppermute(x, 'col', with_near) for x in p4]]
    ppermute x11, starting transfers between devices: 30.9 us -> 51.5 us  [local(): lax.ppermute(near[o:o + s], 'col', inner)]
    ppermute x4, starting transfers between devices: 5.59 us -> 21.1 us  [local(): lax.ppermute(a[h * step:(h + 1) * step], 'col', inner)]
    ppermute x4, starting transfers between devices: 12.9 us -> 3.57 us  [local(): p3 = [lax.ppermute(x, 'col', with_near) for x in p2]]
    ppermute x1, waiting for transfers between devices: 81.1 us -> 72.4 us  [local(): near = lax.ppermute(a, 'col', with_near)]
    pallas_call x11 -> x15, Pallas kernels: 92.2 us -> 96.8 us  [the longest x7 77.8 us: _group_product(): pl.pallas_call(functools.partial(_mm_kernel, side), grid=(size // BM,), o...]
  transfers between devices with their start and end apart: 34 -> 34, of which waited for: 12 -> 11; matrix products, arithmetic and copies ran while one was open for 1% -> 2% of each run, Pallas kernels for 16% -> 17%
where the time goes in v3:
time: 557 us; the launch traced here: 551 us
  waiting for transfers between devices  338 us (61%)
  Pallas kernels  98 us (18%)
  starting transfers between devices  86.8 us (16%)
  local copies, waits for them, and re-layouts  28.1 us (5%)
    ppermute x11, waiting for transfers between devices, local(): p5 = [lax.ppermute(x, 'col', with_near) for x in p4]  117 us
    ppermute x3, waiting for transfers between devices, local(): lax.ppermute(b_own, 'row', [(p, (p - s) % side) for p in range(side)])  79.3 us
    pallas_call x7, Pallas kernels, _group_product(): pl.pallas_call(functools.partial(_mm_kernel, side), grid=(size // BM,), o...  77.8 us
    ppermute x1, waiting for transfers between devices, local(): near = lax.ppermute(a, 'col', with_near)  72.4 us
    ppermute x4, waiting for transfers between devices, local(): p3 = [lax.ppermute(x, 'col', with_near) for x in p2]  69 us
    ppermute x11, starting transfers between devices, local(): lax.ppermute(near[o:o + s], 'col', inner)  51.5 us
    ppermute x4, starting transfers between devices, local(): lax.ppermute(a[h * step:(h + 1) * step], 'col', inner)  21.1 us
    unnamed x44, local copies, waits for them, and re-layouts  19 us
  transfers between devices with their start and end apart: 34, of which 11 were waited for; matrix products, arithmetic and copies ran while one was open for 2% of the time, Pallas kernels for 17%

profile of v3, /device:TPU:28, one launch (start us, length us, event | category | flops | bytes accessed | tf_op | source)
XLA Modules:
  0.0 551.1 jit_solution(4991363331700003677)
XLA Ops:
  1.6 5.1 fusion.1
  8.3 38.5 %collective-permute-done.4.refs_1_ = bf16[512,2048]{1,0:T(8,128)(2,1)S(1)} collective-permute-done((bf16[512,2048]{1,0:T(8,128)(2,1)}, bf16[512,2048]{1,0:T(8,128)(2,1)S(1)}, u32[]{:S(2)}, u32[]{:S(2)}) %collective-permute-start.4) | collective-permute-done | bytes 2097184 | tf_op jit(solution)/shard_map/ppermute | solution.py:173
  49.4 40.8 %collective-permute-done.5.refs_2_ = bf16[512,2048]{1,0:T(8,128)(2,1)S(1)} collective-permute-done((bf16[512,2048]{1,0:T(8,128)(2,1)}, bf16[512,2048]{1,0:T(8,128)(2,1)S(1)}, u32[]{:S(2)}, u32[]{:S(2)}) %collective-permute-start.5) | collective-permute-done | bytes 2097184 | tf_op jit(solution)/shard_map/ppermute | solution.py:173
  91.6 17.2 %collective-permute-start.22 = (bf16[2048,512]{1,0:T(8,128)(2,1)}, bf16[2048,512]{1,0:T(8,128)(2,1)}, u32[]{:S(2)}, u32[]{:S(2)}) collective-permute-start(bf16[2048,512]{1,0:T(8,128)(2,1)} %get-tuple-element.13), channel_id=1, source_target_pairs={{0,0},{4,8},{8,4},{12,12},{1,1},{5,9},{9,5},{13,13},{2,2},{6,10},{... | collective-permute-start | bytes 6291464 | tf_op jit(solution)/shard_map/ppermute | solution.py:167
  108.8 2.3 collective-permute-start.16
  111.1 72.4 %collective-permute-done.1.near = bf16[8192,512]{1,0:T(8,128)(2,1)S(1)} collective-permute-done((bf16[8192,512]{1,0:T(8,128)(2,1)}, bf16[8192,512]{1,0:T(8,128)(2,1)S(1)}, u32[]{:S(2)}, u32[]{:S(2)}) %collective-permute-start.1) | collective-permute-done | bytes 8388640 | tf_op jit(solution)/shard_map/ppermute | solution.py:165
  184.0 3.2 fusion
  187.2 2.0 copy-done.19
  189.1 1.6 collective-permute-start.32
  192.3 9.6 %collective-permute-start.30 = (bf16[1024,512]{1,0:T(8,128)(2,1)}, bf16[1024,512]{1,0:T(8,128)(2,1)}, u32[]{:S(2)}, u32[]{:S(2)}) collective-permute-start(bf16[1024,512]{1,0:T(8,128)(2,1)} %get-tuple-element.6), channel_id=1, source_target_pairs={{0,0},{4,8},{8,4},{12,12},{1,1},{5,9},{9,5},{13,13},{2,2},{6,10},{... | collective-permute-start | bytes 3145736 | tf_op jit(solution)/shard_map/ppermute | solution.py:169
  201.8 26.6 %collective-permute-done.29.p3 = bf16[2048,512]{1,0:T(8,128)(2,1)S(1)} collective-permute-done((bf16[2048,512]{1,0:T(8,128)(2,1)S(1)}, bf16[2048,512]{1,0:T(8,128)(2,1)S(1)}, u32[]{:S(2)}, u32[]{:S(2)}) %collective-permute-start.29) | collective-permute-done | bytes 2097184 | tf_op jit(solution)/shard_map/ppermute | solution.py:168
  231.1 42.3 %collective-permute-done.7.p3 = bf16[2048,512]{1,0:T(8,128)(2,1)S(1)} collective-permute-done((bf16[2048,512]{1,0:T(8,128)(2,1)S(1)}, bf16[2048,512]{1,0:T(8,128)(2,1)S(1)}, u32[]{:S(2)}, u32[]{:S(2)}) %collective-permute-start.7) | collective-permute-done | bytes 2097184 | tf_op jit(solution)/shard_map/ppermute | solution.py:168
  275.4 9.5 %collective-permute-start.26 = (bf16[1024,512]{1,0:T(8,128)(2,1)}, bf16[1024,512]{1,0:T(8,128)(2,1)}, u32[]{:S(2)}, u32[]{:S(2)}) collective-permute-start(bf16[1024,512]{1,0:T(8,128)(2,1)} %get-tuple-element.7), channel_id=1, source_target_pairs={{0,0},{4,8},{8,4},{12,12},{1,1},{5,9},{9,5},{13,13},{2,2},{6,10},{... | collective-permute-start | bytes 3145736 | tf_op jit(solution)/shard_map/ppermute | solution.py:169
  285.8 5.4 collective-permute-start.12
  291.2 1.6 copy-done.14
  292.8 1.6 copy-done.16
  294.4 1.6 copy-done.18
  296.0 1.6 copy-done.20
  298.8 2.2 copy-done.2
  301.0 3.4 copy-done
  304.4 1.9 early_product.5.early
  307.3 1.9 early_product.4.early
  309.2 1.8 early_product.6.early
  311.0 10.0 %collective-permute-start.24 = (bf16[1024,512]{1,0:T(8,128)(2,1)}, bf16[1024,512]{1,0:T(8,128)(2,1)}, u32[]{:S(2)}, u32[]{:S(2)}) collective-permute-start(bf16[1024,512]{1,0:T(8,128)(2,1)} %get-tuple-element.8), channel_id=1, source_target_pairs={{0,0},{4,8},{8,4},{12,12},{1,1},{5,9},{9,5},{13,13},{2,2},{6,10},{... | collective-permute-start | bytes 3145736 | tf_op jit(solution)/shard_map/ppermute | solution.py:169
  321.0 1.8 collective-permute-start.31
  322.9 4.5 early_product.7.early
  328.3 12.6 %collective-permute-done.33.p5 = bf16[1024,512]{1,0:T(8,128)(2,1)} collective-permute-done((bf16[1024,512]{1,0:T(8,128)(2,1)}, bf16[1024,512]{1,0:T(8,128)(2,1)}, u32[]{:S(2)}, u32[]{:S(2)}) %collective-permute-start.33) | collective-permute-done | bytes 1048608 | tf_op jit(solution)/shard_map/ppermute | solution.py:170
  341.4 11.4 %group_product.7.rest_0_ = bf16[8192,2048]{1,0:T(8,128)(2,1)} custom-call(bf16[8192,512]{1,0:T(8,128)(2,1)S(1)} %copy-done, bf16[8192,512]{1,0:T(8,128)(2,1)S(1)} %copy-done.2, bf16[2048,512]{1,0:T(8,128)(2,1)S(1)} %copy-done.8, bf16[2048,512]{1,0:T(8,128)(2,1)S(1)} %copy-done.10, bf16[1024,512]{1,0:T(8,128)(2,1)} %collective-permute-done.32.p4, ...), custom_call_target="tpu_custom_call" | custom-call | flops 8589934592 | bytes 8388608 | tf_op jit(solution)/shard_map/group_product/pallas_call | solution.py:75
  352.8 1.6 collective-permute-start.17
  354.4 9.5 %collective-permute-start.18 = (bf16[1024,512]{1,0:T(8,128)(2,1)}, bf16[1024,512]{1,0:T(8,128)(2,1)}, u32[]{:S(2)}, u32[]{:S(2)}) collective-permute-start(bf16[1024,512]{1,0:T(8,128)(2,1)} %get-tuple-element.10), channel_id=1, source_target_pairs={{0,0},{4,8},{8,4},{12,12},{1,1},{5,9},{9,5},{13,13},{2,2},{6,10},{... | collective-permute-start | bytes 3145736 | tf_op jit(solution)/shard_map/ppermute | solution.py:169
  363.9 11.3 %group_product.8.rest_0_ = bf16[8192,2048]{1,0:T(8,128)(2,1)} custom-call(bf16[8192,512]{1,0:T(8,128)(2,1)S(1)} %copy-done, bf16[8192,512]{1,0:T(8,128)(2,1)S(1)} %copy-done.2, bf16[2048,512]{1,0:T(8,128)(2,1)S(1)} %copy-done.8, bf16[2048,512]{1,0:T(8,128)(2,1)S(1)} %copy-done.10, ...), custom_call_target="tpu_custom_call", output_to_operand_aliasing={{}: (7, {})} | custom-call | flops 8589934592 | bytes 8388608 | tf_op jit(solution)/shard_map/group_product/pallas_call | solution.py:75
  375.3 1.9 collective-permute-start.14
  377.1 8.6 %collective-permute-done.27.p5 = bf16[1024,512]{1,0:T(8,128)(2,1)S(1)} collective-permute-done((bf16[1024,512]{1,0:T(8,128)(2,1)}, bf16[1024,512]{1,0:T(8,128)(2,1)S(1)}, u32[]{:S(2)}, u32[]{:S(2)}) %collective-permute-start.27) | collective-permute-done | bytes 1048608 | tf_op jit(solution)/shard_map/ppermute | solution.py:170
  386.2 11.5 %group_product.9.rest_0_ = bf16[8192,2048]{1,0:T(8,128)(2,1)} custom-call(bf16[8192,512]{1,0:T(8,128)(2,1)S(1)} %copy-done, bf16[8192,512]{1,0:T(8,128)(2,1)S(1)} %copy-done.2, bf16[2048,512]{1,0:T(8,128)(2,1)} %collective-permute-done.22.p2, bf16[2048,512]{1,0:T(8,128)(2,1)} %collective-permute-done.23.p3, ...), custom_call_target="tpu_custom_call", output_to_operand_aliasing={{}: (7, {})} | custom-call | flops 8589934592 | bytes 8388608 | tf_op jit(solution)/shard_map/group_product/pallas_call | solution.py:75
  397.7 1.6 collective-permute-start.9
  399.3 53.9 %collective-permute-done.25.p5 = bf16[1024,512]{1,0:T(8,128)(2,1)S(1)} collective-permute-done((bf16[1024,512]{1,0:T(8,128)(2,1)}, bf16[1024,512]{1,0:T(8,128)(2,1)S(1)}, u32[]{:S(2)}, u32[]{:S(2)}) %collective-permute-start.25) | collective-permute-done | bytes 1048608 | tf_op jit(solution)/shard_map/ppermute | solution.py:170
  453.6 11.5 %group_product.10.rest_0_ = bf16[8192,2048]{1,0:T(8,128)(2,1)} custom-call(bf16[8192,512]{1,0:T(8,128)(2,1)S(1)} %copy-done, bf16[8192,512]{1,0:T(8,128)(2,1)S(1)} %copy-done.2, bf16[2048,512]{1,0:T(8,128)(2,1)} %collective-permute-done.22.p2, bf16[2048,512]{1,0:T(8,128)(2,1)} %collective-permute-done.23.p3, ...), custom_call_target="tpu_custom_call", output_to_operand_aliasing={{}: (7, {})} | custom-call | flops 8589934592 | bytes 8388608 | tf_op jit(solution)/shard_map/group_product/pallas_call | solution.py:75
  465.1 1.6 collective-permute-start.3
  467.2 8.5 %collective-permute-done.21.p5 = bf16[1024,512]{1,0:T(8,128)(2,1)S(1)} collective-permute-done((bf16[1024,512]{1,0:T(8,128)(2,1)S(1)}, bf16[1024,512]{1,0:T(8,128)(2,1)S(1)}, u32[]{:S(2)}, u32[]{:S(2)}) %collective-permute-start.21) | collective-permute-done | bytes 1048608 | tf_op jit(solution)/shard_map/ppermute | solution.py:170
  476.1 10.3 %group_product.11.rest_0_ = bf16[8192,2048]{1,0:T(8,128)(2,1)} custom-call(bf16[8192,512]{1,0:T(8,128)(2,1)S(1)} %copy-done, bf16[8192,512]{1,0:T(8,128)(2,1)S(1)} %copy-done.2, bf16[2048,512]{1,0:T(8,128)(2,1)S(1)} %copy-done.6, bf16[2048,512]{1,0:T(8,128)(2,1)S(1)} %collective-permute-done.17.p3, ...), custom_call_target="tpu_custom_call", output_to_operand_aliasing={{}: (7, {})} | custom-call | flops 8589934592 | bytes 8388608 | tf_op jit(solution)/shard_map/group_product/pallas_call | solution.py:75
  486.4 14.6 %collective-permute-done.19.p5 = bf16[1024,512]{1,0:T(8,128)(2,1)} collective-permute-done((bf16[1024,512]{1,0:T(8,128)(2,1)}, bf16[1024,512]{1,0:T(8,128)(2,1)}, u32[]{:S(2)}, u32[]{:S(2)}) %collective-permute-start.19) | collective-permute-done | bytes 1048608 | tf_op jit(solution)/shard_map/ppermute | solution.py:170
  501.5 11.4 %group_product.12.rest_0_ = bf16[8192,2048]{1,0:T(8,128)(2,1)} custom-call(bf16[8192,512]{1,0:T(8,128)(2,1)S(1)} %copy-done, bf16[8192,512]{1,0:T(8,128)(2,1)S(1)} %copy-done.2, bf16[2048,512]{1,0:T(8,128)(2,1)S(1)} %copy-done.6, bf16[2048,512]{1,0:T(8,128)(2,1)S(1)} %collective-permute-done.17.p3, ...), custom_call_target="tpu_custom_call", output_to_operand_aliasing={{}: (7, {})} | custom-call | flops 8589934592 | bytes 8388608 | tf_op jit(solution)/shard_map/group_product/pallas_call | solution.py:75
  512.9 18.9 %collective-permute-done.15.p5 = bf16[1024,512]{1,0:T(8,128)(2,1)S(1)} collective-permute-done((bf16[1024,512]{1,0:T(8,128)(2,1)S(1)}, bf16[1024,512]{1,0:T(8,128)(2,1)S(1)}, u32[]{:S(2)}, u32[]{:S(2)}) %collective-permute-start.15) | collective-permute-done | bytes 1048608 | tf_op jit(solution)/shard_map/ppermute | solution.py:170
  531.8 10.3 %group_product.13.c_in = bf16[8192,2048]{1,0:T(8,128)(2,1)} custom-call(bf16[8192,512]{1,0:T(8,128)(2,1)S(1)} %copy-done, bf16[8192,512]{1,0:T(8,128)(2,1)S(1)} %copy-done.2, bf16[2048,512]{1,0:T(8,128)(2,1)S(1)} %copy-done.4, bf16[2048,512]{1,0:T(8,128)(2,1)S(1)} %collective-permute-done.7.p3, ...), custom_call_target="tpu_custom_call", output_to_operand_aliasing={{}: (7, {})} | custom-call | flops 8589934592 | bytes 8388608 | tf_op jit(solution)/shard_map/group_product/pallas_call | solution.py:75
  542.2 2.9 late_product.4.c_in
  545.1 1.7 late_product.5.c_in
  546.8 2.1 late_product.6.c_in
  549.0 2.1 late_product.7
  (86 shorter events, 20.5 us)
Async XLA Ops:
  0.0 48.1 %copy-start.13 = (bf16[512,2048]{1,0:T(8,128)(2,1)S(1)}, bf16[512,2048]{1,0:T(8,128)(2,1)}, u32[]{:S(2)}) copy-start(bf16[512,2048]{1,0:T(8,128)(2,1)} %refs_0_.1) | copy-start | bytes 6291460
  0.0 183.5 %collective-permute-start.1 = (bf16[8192,512]{1,0:T(8,128)(2,1)}, bf16[8192,512]{1,0:T(8,128)(2,1)S(1)}, u32[]{:S(2)}, u32[]{:S(2)}) collective-permute-start(bf16[8192,512]{1,0:T(8,128)(2,1)} %own.21), channel_id=1, source_target_pairs={{0,4},{4,0},{8,12},{12,8},{1,5},{5,1},{9,13},{13,9},{2,6},{6,2},{1... | collective-permute-start | bytes 25165832 | tf_op jit(solution)/shard_map/ppermute | solution.py:165
  0.5 46.3 %collective-permute-start.4 = (bf16[512,2048]{1,0:T(8,128)(2,1)}, bf16[512,2048]{1,0:T(8,128)(2,1)S(1)}, u32[]{:S(2)}, u32[]{:S(2)}) collective-permute-start(bf16[512,2048]{1,0:T(8,128)(2,1)} %refs_0_.1), channel_id=1, source_target_pairs={{0,3},{1,0},{2,1},{3,2},{4,7},{5,4},{6,5},{7,6},{8,11},{9,8},{10,9... | collective-permute-start | bytes 6291464 | tf_op jit(solution)/shard_map/ppermute | solution.py:173
  0.5 89.7 %collective-permute-start.5 = (bf16[512,2048]{1,0:T(8,128)(2,1)}, bf16[512,2048]{1,0:T(8,128)(2,1)S(1)}, u32[]{:S(2)}, u32[]{:S(2)}) collective-permute-start(bf16[512,2048]{1,0:T(8,128)(2,1)} %refs_0_.1), channel_id=1, source_target_pairs={{0,2},{1,3},{2,0},{3,1},{4,6},{5,7},{6,4},{7,5},{8,10},{9,11},{10,... | collective-permute-start | bytes 6291464 | tf_op jit(solution)/shard_map/ppermute | solution.py:173
  6.7 102.1 %collective-permute-start.28 = (bf16[2048,512]{1,0:T(8,128)(2,1)S(1)}, bf16[2048,512]{1,0:T(8,128)(2,1)S(1)}, u32[]{:S(2)}, u32[]{:S(2)}) collective-permute-start(bf16[2048,512]{1,0:T(8,128)(2,1)S(1)} %get-tuple-element.12), channel_id=1, source_target_pairs={{0,0},{4,8},{8,4},{12,12},{1,1},{5,9},{9,5},{13,13},{2,2},{6,10},{... | collective-permute-start | bytes 6291464 | tf_op jit(solution)/shard_map/ppermute | solution.py:167
  7.5 103.6 %collective-permute-start = (bf16[2048,512]{1,0:T(8,128)(2,1)S(1)}, bf16[2048,512]{1,0:T(8,128)(2,1)S(1)}, u32[]{:S(2)}, u32[]{:S(2)}) collective-permute-start(bf16[2048,512]{1,0:T(8,128)(2,1)S(1)} %get-tuple-element.15), channel_id=1, source_target_pairs={{0,0},{4,8},{8,4},{12,12},{1,1},{5,9},{9,5},{13,13},{2,2},{6,10},{... | collective-permute-start | bytes 6291464 | tf_op jit(solution)/shard_map/ppermute | solution.py:167
  48.1 139.1 %collective-permute-start.6 = (bf16[512,2048]{1,0:T(8,128)(2,1)S(1)}, bf16[512,2048]{1,0:T(8,128)(2,1)S(1)}, u32[]{:S(2)}, u32[]{:S(2)}) collective-permute-start(bf16[512,2048]{1,0:T(8,128)(2,1)S(1)} %copy-done.13), channel_id=1, source_target_pairs={{0,1},{1,2},{2,3},{3,0},{4,5},{5,6},{6,7},{7,4},{8,9},{9,10},{10,1... | collective-permute-start | bytes 6291464 | tf_op jit(solution)/shard_map/ppermute | solution.py:173
  91.6 99.2 %collective-permute-start.22 = (bf16[2048,512]{1,0:T(8,128)(2,1)}, bf16[2048,512]{1,0:T(8,128)(2,1)}, u32[]{:S(2)}, u32[]{:S(2)}) collective-permute-start(bf16[2048,512]{1,0:T(8,128)(2,1)} %get-tuple-element.13), channel_id=1, source_target_pairs={{0,0},{4,8},{8,4},{12,12},{1,1},{5,9},{9,5},{13,13},{2,2},{6,10},{... | collective-permute-start | bytes 6291464 | tf_op jit(solution)/shard_map/ppermute | solution.py:167
  108.8 78.4 %copy-start.7 = (bf16[2048,512]{1,0:T(8,128)(2,1)}, bf16[2048,512]{1,0:T(8,128)(2,1)S(1)}, u32[]{:S(2)}) copy-start(bf16[2048,512]{1,0:T(8,128)(2,1)S(1)} %collective-permute-done.28.p2) | copy-start | bytes 6291460
  108.8 83.5 %collective-permute-start.16 = (bf16[2048,512]{1,0:T(8,128)(2,1)}, bf16[2048,512]{1,0:T(8,128)(2,1)S(1)}, u32[]{:S(2)}, u32[]{:S(2)}) collective-permute-start(bf16[2048,512]{1,0:T(8,128)(2,1)} %get-tuple-element.14), channel_id=1, source_target_pairs={{0,0},{4,8},{8,4},{12,12},{1,1},{5,9},{9,5},{13,13},{2,2},{6,10},{... | collective-permute-start | bytes 6291464 | tf_op jit(solution)/shard_map/ppermute | solution.py:167
  111.1 76.1 %copy-start.3 = (bf16[2048,512]{1,0:T(8,128)(2,1)}, bf16[2048,512]{1,0:T(8,128)(2,1)S(1)}, u32[]{:S(2)}) copy-start(bf16[2048,512]{1,0:T(8,128)(2,1)S(1)} %collective-permute-done.p2) | copy-start | bytes 6291460
  111.1 117.4 %collective-permute-start.29 = (bf16[2048,512]{1,0:T(8,128)(2,1)S(1)}, bf16[2048,512]{1,0:T(8,128)(2,1)S(1)}, u32[]{:S(2)}, u32[]{:S(2)}) collective-permute-start(bf16[2048,512]{1,0:T(8,128)(2,1)S(1)} %collective-permute-done.28.p2), channel_id=1, source_target_pairs={{0,4},{4,0},{8,12},{12,8},{1,5},{5,1},{9,13},{13,9},{2,6},{6,2},{1... | collective-permute-start | bytes 6291464 | tf_op jit(solution)/shard_map/ppermute | solution.py:168
  183.5 101.4 %copy-start.1 = (bf16[8192,512]{1,0:T(8,128)(2,1)}, bf16[8192,512]{1,0:T(8,128)(2,1)S(1)}, u32[]{:S(2)}) copy-start(bf16[8192,512]{1,0:T(8,128)(2,1)S(1)} %collective-permute-done.1.near) | copy-start | bytes 25165828
  183.5 89.9 %collective-permute-start.7 = (bf16[2048,512]{1,0:T(8,128)(2,1)S(1)}, bf16[2048,512]{1,0:T(8,128)(2,1)S(1)}, u32[]{:S(2)}, u32[]{:S(2)}) collective-permute-start(bf16[2048,512]{1,0:T(8,128)(2,1)S(1)} %collective-permute-done.p2), channel_id=1, source_target_pairs={{0,4},{4,0},{8,12},{12,8},{1,5},{5,1},{9,13},{13,9},{2,6},{6,2},{1... | collective-permute-start | bytes 6291464 | tf_op jit(solution)/shard_map/ppermute | solution.py:168
  187.2 2.0 copy-start.19
  189.1 95.8 %collective-permute-start.32 = (bf16[1024,512]{1,0:T(8,128)(2,1)S(1)}, bf16[1024,512]{1,0:T(8,128)(2,1)}, u32[]{:S(2)}, u32[]{:S(2)}) collective-permute-start(bf16[1024,512]{1,0:T(8,128)(2,1)S(1)} %get-tuple-element.5), channel_id=1, source_target_pairs={{0,0},{4,8},{8,4},{12,12},{1,1},{5,9},{9,5},{13,13},{2,2},{6,10},{... | collective-permute-start | bytes 3145736 | tf_op jit(solution)/shard_map/ppermute | solution.py:169
  190.8 162.0 %collective-permute-start.23 = (bf16[2048,512]{1,0:T(8,128)(2,1)}, bf16[2048,512]{1,0:T(8,128)(2,1)}, u32[]{:S(2)}, u32[]{:S(2)}) collective-permute-start(bf16[2048,512]{1,0:T(8,128)(2,1)} %collective-permute-done.22.p2), channel_id=1, source_target_pairs={{0,4},{4,0},{8,12},{12,8},{1,5},{5,1},{9,13},{13,9},{2,6},{6,2},{1... | collective-permute-start | bytes 6291464 | tf_op jit(solution)/shard_map/ppermute | solution.py:168
  192.3 93.5 %copy-start.5 = (bf16[2048,512]{1,0:T(8,128)(2,1)}, bf16[2048,512]{1,0:T(8,128)(2,1)S(1)}, u32[]{:S(2)}) copy-start(bf16[2048,512]{1,0:T(8,128)(2,1)S(1)} %collective-permute-done.16.p2) | copy-start | bytes 6291460
  192.3 128.8 %collective-permute-start.30 = (bf16[1024,512]{1,0:T(8,128)(2,1)}, bf16[1024,512]{1,0:T(8,128)(2,1)}, u32[]{:S(2)}, u32[]{:S(2)}) collective-permute-start(bf16[1024,512]{1,0:T(8,128)(2,1)} %get-tuple-element.6), channel_id=1, source_target_pairs={{0,0},{4,8},{8,4},{12,12},{1,1},{5,9},{9,5},{13,13},{2,2},{6,10},{... | collective-permute-start | bytes 3145736 | tf_op jit(solution)/shard_map/ppermute | solution.py:169
  229.8 45.0 %collective-permute-start.8 = (bf16[128,512]{1,0:T(8,128)(2,1)S(1)}, bf16[128,512]{1,0:T(8,128)(2,1)}, u32[]{:S(2)}, u32[]{:S(2)}) collective-permute-start(bf16[128,512]{1,0:T(8,128)(2,1)S(1)} %get-tuple-element.16), channel_id=1, source_target_pairs={{0,0},{4,8},{8,4},{12,12},{1,1},{5,9},{9,5},{13,13},{2,2},{6,10},{... | collective-permute-start | bytes 393224 | tf_op jit(solution)/shard_map/ppermute | solution.py:169
  273.4 2.0 collective-permute-start.2
  274.8 11.0 %collective-permute-start.10 = (bf16[256,512]{1,0:T(8,128)(2,1)S(1)}, bf16[256,512]{1,0:T(8,128)(2,1)S(1)}, u32[]{:S(2)}, u32[]{:S(2)}) collective-permute-start(bf16[256,512]{1,0:T(8,128)(2,1)S(1)} %slice.62), channel_id=1, source_target_pairs={{0,0},{4,8},{8,4},{12,12},{1,1},{5,9},{9,5},{13,13},{2,2},{6,10},{... | collective-permute-start | bytes 786440 | tf_op jit(solution)/shard_map/ppermute | solution.py:169
  275.4 52.0 %collective-permute-start.26 = (bf16[1024,512]{1,0:T(8,128)(2,1)}, bf16[1024,512]{1,0:T(8,128)(2,1)}, u32[]{:S(2)}, u32[]{:S(2)}) collective-permute-start(bf16[1024,512]{1,0:T(8,128)(2,1)} %get-tuple-element.7), channel_id=1, source_target_pairs={{0,0},{4,8},{8,4},{12,12},{1,1},{5,9},{9,5},{13,13},{2,2},{6,10},{... | collective-permute-start | bytes 3145736 | tf_op jit(solution)/shard_map/ppermute | solution.py:169
  284.9 56.0 %collective-permute-start.33 = (bf16[1024,512]{1,0:T(8,128)(2,1)}, bf16[1024,512]{1,0:T(8,128)(2,1)}, u32[]{:S(2)}, u32[]{:S(2)}) collective-permute-start(bf16[1024,512]{1,0:T(8,128)(2,1)} %collective-permute-done.32.p4), channel_id=1, source_target_pairs={{0,4},{4,0},{8,12},{12,8},{1,5},{5,1},{9,13},{13,9},{2,6},{6,2},{1... | collective-permute-start | bytes 3145736 | tf_op jit(solution)/shard_map/ppermute | solution.py:170
  285.8 25.2 %collective-permute-start.12 = (bf16[512,512]{1,0:T(8,128)(2,1)}, bf16[512,512]{1,0:T(8,128)(2,1)}, u32[]{:S(2)}, u32[]{:S(2)}) collective-permute-start(bf16[512,512]{1,0:T(8,128)(2,1)} %slice.63), channel_id=1, source_target_pairs={{0,0},{4,8},{8,4},{12,12},{1,1},{5,9},{9,5},{13,13},{2,2},{6,10},{... | collective-permute-start | bytes 1572872 | tf_op jit(solution)/shard_map/ppermute | solution.py:169
  297.6 3.4 copy-start.2
  301.0 3.4 copy-start
  311.0 16.4 %copy-start.21 = (bf16[1024,512]{1,0:T(8,128)(2,1)S(1)}, bf16[1024,512]{1,0:T(8,128)(2,1)}, u32[]{:S(2)}) copy-start(bf16[1024,512]{1,0:T(8,128)(2,1)} %get-tuple-element.9) | copy-start | bytes 3145732
  311.0 30.4 %copy-start.8 = (bf16[2048,512]{1,0:T(8,128)(2,1)S(1)}, bf16[2048,512]{1,0:T(8,128)(2,1)}, u32[]{:S(2)}) copy-start(bf16[2048,512]{1,0:T(8,128)(2,1)} %copy-done.7) | copy-start | bytes 6291460
  311.0 30.4 %copy-start.10 = (bf16[2048,512]{1,0:T(8,128)(2,1)S(1)}, bf16[2048,512]{1,0:T(8,128)(2,1)}, u32[]{:S(2)}) copy-start(bf16[2048,512]{1,0:T(8,128)(2,1)} %copy-done.9) | copy-start | bytes 6291460
  311.0 43.4 %collective-permute-start.24 = (bf16[1024,512]{1,0:T(8,128)(2,1)}, bf16[1024,512]{1,0:T(8,128)(2,1)}, u32[]{:S(2)}, u32[]{:S(2)}) collective-permute-start(bf16[1024,512]{1,0:T(8,128)(2,1)} %get-tuple-element.8), channel_id=1, source_target_pairs={{0,0},{4,8},{8,4},{12,12},{1,1},{5,9},{9,5},{13,13},{2,2},{6,10},{... | collective-permute-start | bytes 3145736 | tf_op jit(solution)/shard_map/ppermute | solution.py:169
  321.0 42.9 %collective-permute-start.31 = (bf16[1024,512]{1,0:T(8,128)(2,1)}, bf16[1024,512]{1,0:T(8,128)(2,1)S(1)}, u32[]{:S(2)}, u32[]{:S(2)}) collective-permute-start(bf16[1024,512]{1,0:T(8,128)(2,1)} %collective-permute-done.30.p4), channel_id=1, source_target_pairs={{0,4},{4,0},{8,12},{12,8},{1,5},{5,1},{9,13},{13,9},{2,6},{6,2},{1... | collective-permute-start | bytes 3145736 | tf_op jit(solution)/shard_map/ppermute | solution.py:170
  327.4 25.4 %copy-start.6 = (bf16[2048,512]{1,0:T(8,128)(2,1)S(1)}, bf16[2048,512]{1,0:T(8,128)(2,1)}, u32[]{:S(2)}) copy-start(bf16[2048,512]{1,0:T(8,128)(2,1)} %copy-done.5) | copy-start | bytes 6291460
  327.4 47.8 %collective-permute-start.20 = (bf16[1024,512]{1,0:T(8,128)(2,1)S(1)}, bf16[1024,512]{1,0:T(8,128)(2,1)S(1)}, u32[]{:S(2)}, u32[]{:S(2)}) collective-permute-start(bf16[1024,512]{1,0:T(8,128)(2,1)S(1)} %copy-done.21), channel_id=1, source_target_pairs={{0,0},{4,8},{8,4},{12,12},{1,1},{5,9},{9,5},{13,13},{2,2},{6,10},{... | collective-permute-start | bytes 3145736 | tf_op jit(solution)/shard_map/ppermute | solution.py:169
  340.9 44.8 %collective-permute-start.27 = (bf16[1024,512]{1,0:T(8,128)(2,1)}, bf16[1024,512]{1,0:T(8,128)(2,1)S(1)}, u32[]{:S(2)}, u32[]{:S(2)}) collective-permute-start(bf16[1024,512]{1,0:T(8,128)(2,1)} %collective-permute-done.26.p4), channel_id=1, source_target_pairs={{0,4},{4,0},{8,12},{12,8},{1,5},{5,1},{9,13},{13,9},{2,6},{6,2},{1... | collective-permute-start | bytes 3145736 | tf_op jit(solution)/shard_map/ppermute | solution.py:170
  352.8 112.3 %collective-permute-start.17 = (bf16[2048,512]{1,0:T(8,128)(2,1)S(1)}, bf16[2048,512]{1,0:T(8,128)(2,1)S(1)}, u32[]{:S(2)}, u32[]{:S(2)}) collective-permute-start(bf16[2048,512]{1,0:T(8,128)(2,1)S(1)} %copy-done.6), channel_id=1, source_target_pairs={{0,4},{4,0},{8,12},{12,8},{1,5},{5,1},{9,13},{13,9},{2,6},{6,2},{1... | collective-permute-start | bytes 6291464 | tf_op jit(solution)/shard_map/ppermute | solution.py:168
  354.4 43.3 %collective-permute-start.18 = (bf16[1024,512]{1,0:T(8,128)(2,1)}, bf16[1024,512]{1,0:T(8,128)(2,1)}, u32[]{:S(2)}, u32[]{:S(2)}) collective-permute-start(bf16[1024,512]{1,0:T(8,128)(2,1)} %get-tuple-element.10), channel_id=1, source_target_pairs={{0,0},{4,8},{8,4},{12,12},{1,1},{5,9},{9,5},{13,13},{2,2},{6,10},{... | collective-permute-start | bytes 3145736 | tf_op jit(solution)/shard_map/ppermute | solution.py:169
  363.9 89.3 %collective-permute-start.25 = (bf16[1024,512]{1,0:T(8,128)(2,1)}, bf16[1024,512]{1,0:T(8,128)(2,1)S(1)}, u32[]{:S(2)}, u32[]{:S(2)}) collective-permute-start(bf16[1024,512]{1,0:T(8,128)(2,1)} %collective-permute-done.24.p4), channel_id=1, source_target_pairs={{0,4},{4,0},{8,12},{12,8},{1,5},{5,1},{9,13},{13,9},{2,6},{6,2},{1... | collective-permute-start | bytes 3145736 | tf_op jit(solution)/shard_map/ppermute | solution.py:170
  375.3 91.5 %collective-permute-start.14 = (bf16[1024,512]{1,0:T(8,128)(2,1)}, bf16[1024,512]{1,0:T(8,128)(2,1)S(1)}, u32[]{:S(2)}, u32[]{:S(2)}) collective-permute-start(bf16[1024,512]{1,0:T(8,128)(2,1)} %get-tuple-element.11), channel_id=1, source_target_pairs={{0,0},{4,8},{8,4},{12,12},{1,1},{5,9},{9,5},{13,13},{2,2},{6,10},{... | collective-permute-start | bytes 3145736 | tf_op jit(solution)/shard_map/ppermute | solution.py:169
  385.8 89.9 %collective-permute-start.21 = (bf16[1024,512]{1,0:T(8,128)(2,1)S(1)}, bf16[1024,512]{1,0:T(8,128)(2,1)S(1)}, u32[]{:S(2)}, u32[]{:S(2)}) collective-permute-start(bf16[1024,512]{1,0:T(8,128)(2,1)S(1)} %collective-permute-done.20.p4), channel_id=1, source_target_pairs={{0,4},{4,0},{8,12},{12,8},{1,5},{5,1},{9,13},{13,9},{2,6},{6,2},{1... | collective-permute-start | bytes 3145736 | tf_op jit(solution)/shard_map/ppermute | solution.py:170
  397.7 149.1 %collective-permute-start.9 = (bf16[128,512]{1,0:T(8,128)(2,1)}, bf16[128,512]{1,0:T(8,128)(2,1)}, u32[]{:S(2)}, u32[]{:S(2)}) collective-permute-start(bf16[128,512]{1,0:T(8,128)(2,1)} %collective-permute-done.8.p4), channel_id=1, source_target_pairs={{0,4},{4,0},{8,12},{12,8},{1,5},{5,1},{9,13},{13,9},{2,6},{6,2},{1... | collective-permute-start | bytes 393224 | tf_op jit(solution)/shard_map/ppermute | solution.py:170
  453.2 47.9 %collective-permute-start.19 = (bf16[1024,512]{1,0:T(8,128)(2,1)}, bf16[1024,512]{1,0:T(8,128)(2,1)}, u32[]{:S(2)}, u32[]{:S(2)}) collective-permute-start(bf16[1024,512]{1,0:T(8,128)(2,1)} %collective-permute-done.18.p4), channel_id=1, source_target_pairs={{0,4},{4,0},{8,12},{12,8},{1,5},{5,1},{9,13},{13,9},{2,6},{6,2},{1... | collective-permute-start | bytes 3145736 | tf_op jit(solution)/shard_map/ppermute | solution.py:170
  465.1 83.8 %collective-permute-start.3 = (bf16[128,512]{1,0:T(8,128)(2,1)}, bf16[128,512]{1,0:T(8,128)(2,1)}, u32[]{:S(2)}, u32[]{:S(2)}) collective-permute-start(bf16[128,512]{1,0:T(8,128)(2,1)} %collective-permute-done.2.p4), channel_id=1, source_target_pairs={{0,4},{4,0},{8,12},{12,8},{1,5},{5,1},{9,13},{13,9},{2,6},{6,2},{1... | collective-permute-start | bytes 393224 | tf_op jit(solution)/shard_map/ppermute | solution.py:170
  466.7 78.4 %collective-permute-start.11 = (bf16[256,512]{1,0:T(8,128)(2,1)S(1)}, bf16[256,512]{1,0:T(8,128)(2,1)S(1)}, u32[]{:S(2)}, u32[]{:S(2)}) collective-permute-start(bf16[256,512]{1,0:T(8,128)(2,1)S(1)} %collective-permute-done.10.p4), channel_id=1, source_target_pairs={{0,4},{4,0},{8,12},{12,8},{1,5},{5,1},{9,13},{13,9},{2,6},{6,2},{1... | collective-permute-start | bytes 786440 | tf_op jit(solution)/shard_map/ppermute | solution.py:170
  475.7 56.2 %collective-permute-start.15 = (bf16[1024,512]{1,0:T(8,128)(2,1)S(1)}, bf16[1024,512]{1,0:T(8,128)(2,1)S(1)}, u32[]{:S(2)}, u32[]{:S(2)}) collective-permute-start(bf16[1024,512]{1,0:T(8,128)(2,1)S(1)} %collective-permute-done.14.p4), channel_id=1, source_target_pairs={{0,4},{4,0},{8,12},{12,8},{1,5},{5,1},{9,13},{13,9},{2,6},{6,2},{1... | collective-permute-start | bytes 3145736 | tf_op jit(solution)/shard_map/ppermute | solution.py:170
  486.4 45.4 %copy-start.4 = (bf16[2048,512]{1,0:T(8,128)(2,1)S(1)}, bf16[2048,512]{1,0:T(8,128)(2,1)}, u32[]{:S(2)}) copy-start(bf16[2048,512]{1,0:T(8,128)(2,1)} %copy-done.3) | copy-start | bytes 6291460
  501.0 41.1 %collective-permute-start.13 = (bf16[512,512]{1,0:T(8,128)(2,1)}, bf16[512,512]{1,0:T(8,128)(2,1)S(1)}, u32[]{:S(2)}, u32[]{:S(2)}) collective-permute-start(bf16[512,512]{1,0:T(8,128)(2,1)} %collective-permute-done.12.p4), channel_id=1, source_target_pairs={{0,4},{4,0},{8,12},{12,8},{1,5},{5,1},{9,13},{13,9},{2,6},{6,2},{1... | collective-permute-start | bytes 1572872 | tf_op jit(solution)/shard_map/ppermute | solution.py:170
  545.1 1.7 copy-start.12
  (8 other events, 11.4 us)

commit v4 on v3

--- a/solution.py
+++ b/solution.py
@@ -12,6 +12,7 @@
 GROUPS = (1024, 1024, 1024, 1024, 1024, 1024, 1024)
 TAIL = (512, 256, 128, 128)
 BM = 256
+LATE_STEPS = 1
 
 
 def _at_end(side):
@@ -28,15 +29,17 @@
     out_ref[...] = jnp.dot(lhs, b_ref[...], preferred_element_type=jnp.float32).astype(out_ref.dtype)
 
 
-def _early_kernel(side, own, near, p3, p4, b_ref, out_ref):
-    third = jnp.where(_at_end(side), p3[...], p4[...])
-    lhs = jnp.concatenate([own[...], near[...], third], axis=1)
-    out_ref[...] = jnp.dot(lhs, b_ref[: lhs.shape[1], :], preferred_element_type=jnp.float32)
+def _early_kernel(side, own, near, p2, p3, p4, b_ref, out_ref):
+    at_end = _at_end(side)
+    third = jnp.where(at_end, p3[...], p4[...])
+    fourth = jnp.where(at_end, jnp.zeros_like(p2), p2[...])
+    lhs = jnp.concatenate([own[...], near[...], third, fourth], axis=1)
+    out_ref[...] = jnp.dot(lhs, b_ref[...], preferred_element_type=jnp.float32)
 
 
-def _late_kernel(side, p2, p5, b_ref, early, c_in, out_ref):
-    fourth = jnp.where(_at_end(side), p5[...], p2[...])
-    depth = fourth.shape[1]
+def _late_kernel(side, p5, b_ref, early, c_in, out_ref):
+    depth = p5.shape[1]
+    fourth = jnp.where(_at_end(side), p5[...], jnp.zeros_like(p5))
     total = early[...] + jnp.dot(fourth, b_ref[-depth:, :], preferred_element_type=jnp.float32)
     out_ref[...] = total.astype(out_ref.dtype)
 
@@ -59,14 +62,13 @@
     )
 
 
-def _group_product(side, a, near, p2, p3, p4, p5, b, c, off, size):
-    rows, depth = a.shape
+def _group_product(side, own, near, p2, p3, p4, p5, b, c, rows, off, size):
+    depth = own.shape[1]
     total, cols = b.shape
-    full = _rows(BM, depth, off)
     chunk = _rows(BM, depth, off % p2.shape[0])
     piece = _rows(BM, depth, 0)
-    in_specs = [full, full, chunk, chunk, piece, piece, _kept(b.shape)]
-    args = [a, near, p2, p3, p4, p5, b]
+    in_specs = [chunk, piece, chunk, chunk, piece, piece, _kept(b.shape)]
+    args = [own, near, p2, p3, p4, p5, b]
     alias = {}
     if c is not None:
         in_specs.append(pl.BlockSpec(memory_space=pl.ANY))
@@ -79,47 +81,47 @@
         in_specs=in_specs,
         out_specs=_rows(BM, cols, off),
         input_output_aliases=alias,
-        compiler_params=_params(16),
+        compiler_params=_params(8),
         cost_estimate=_cost(size, total, cols),
         name="group_product",
     )(*args)
 
 
-def _early_product(side, a, near, p3, p4, b, off, size):
-    depth = a.shape[1]
-    cols = b.shape[1]
+def _early_product(side, own, near, p2, p3, p4, b, off, size):
+    depth = own.shape[1]
+    total, cols = b.shape
     bm = min(BM, size)
-    full = _rows(bm, depth, off)
+    chunk = _rows(bm, depth, off % p3.shape[0])
+    piece = _rows(bm, depth, 0)
     return pl.pallas_call(
         functools.partial(_early_kernel, side),
         grid=(size // bm,),
         out_shape=pltpu.VMEM((size, cols), jnp.float32),
-        in_specs=[full, full, _rows(bm, depth, off % p3.shape[0]), _rows(bm, depth, 0), _kept(b.shape)],
+        in_specs=[chunk, piece, chunk, chunk, piece, _kept(b.shape)],
         out_specs=_rows(bm, cols, 0),
-        compiler_params=_params(20),
-        cost_estimate=_cost(size, 3 * depth, cols),
+        compiler_params=_params(8),
+        cost_estimate=_cost(size, total, cols),
         name="early_product",
-    )(a, near, p3, p4, b)
+    )(own, near, p2, p3, p4, b)
 
 
-def _late_product(side, p2, p5, b, early, c, off, size):
+def _late_product(side, p5, b, early, c, off, size):
     depth = p5.shape[1]
     rows, cols = c.shape
-    bm = BM // 2
+    bm = min(BM, size) // LATE_STEPS
     return pl.pallas_call(
         functools.partial(_late_kernel, side),
         grid=(size // bm,),
         out_shape=jax.ShapeDtypeStruct((rows, cols), jnp.bfloat16),
         in_specs=[
-            _rows(bm, depth, off % p2.shape[0]), _rows(bm, depth, 0), _kept(b.shape), _rows(bm, cols, 0),
-            pl.BlockSpec(memory_space=pl.ANY),
+            _rows(bm, depth, 0), _kept(b.shape), _rows(bm, cols, 0), pl.BlockSpec(memory_space=pl.ANY),
         ],
         out_specs=_rows(bm, cols, off),
-        input_output_aliases={4: 0},
-        compiler_params=_params(16),
+        input_output_aliases={3: 0},
+        compiler_params=_params(8),
         cost_estimate=_cost(size, depth, cols),
         name="late_product",
-    )(p2, p5, b, early, c)
+    )(p5, b, early, c)
 
 
 def _stack_kernel(place_ref, *refs):
@@ -164,9 +166,11 @@
 
         near = lax.ppermute(a, "col", with_near)
         step = rows // HALVES
-        p2 = [lax.ppermute(a[h * step : (h + 1) * step], "col", inner) for h in range(HALVES)]
+        own = [a[h * step : (h + 1) * step] for h in range(HALVES)]
+        p2 = [lax.ppermute(x, "col", inner) for x in own]
         p3 = [lax.ppermute(x, "col", with_near) for x in p2]
-        p4 = [lax.ppermute(near[o : o + s], "col", inner) for o, s in zip(offs, sizes)]
+        near = [near[o : o + s] for o, s in zip(offs, sizes)]
+        p4 = [lax.ppermute(x, "col", inner) for x in near]
         p5 = [lax.ppermute(x, "col", with_near) for x in p4]
 
         blocks = [b_own] + [
@@ -175,17 +179,18 @@
         b = _stack_blocks(jnp.stack([lax.rem(row_pos + s, side) ^ col_pos for s in range(side)]), blocks)
 
         main = len(GROUPS)
-        early = []
+        early = {}
         for g in range(main, len(sizes)):
-            early.append(_early_product(side, a, near, p3[offs[g] // step], p4[g], b, offs[g], sizes[g]))
+            h = offs[g] // step
+            early[g] = _early_product(side, own[h], near[g], p2[h], p3[h], p4[g], b, offs[g], sizes[g])
 
         c = None
         for g, (off, size) in enumerate(zip(offs, sizes)):
             h = off // step
             if g < main:
-                c = _group_product(side, a, near, p2[h], p3[h], p4[g], p5[g], b, c, off, size)
+                c = _group_product(side, own[h], near[g], p2[h], p3[h], p4[g], p5[g], b, c, rows, off, size)
             else:
-                c = _late_product(side, p2[h], p5[g], b, early[g - main], c, off, size)
+                c = _late_product(side, p5[g], b, early[g], c, off, size)
         return c
 
     return jax.shard_map(

time: 557 us -> 552 us (level)
  starting transfers between devices: 86.8 us -> 70 us
  local copies, waits for them, and re-layouts: 28.1 us -> 37.7 us
  waiting for transfers between devices: 338 us -> 345 us
    ppermute x15, starting transfers between devices: 72.6 us -> 35.8 us  [the longest x11 31.5 us: local(): p4 = [lax.ppermute(x, 'col', inner) for x in near]]
    ppermute x11, starting transfers between devices: 7.66 us -> 23.3 us  [local(): p5 = [lax.ppermute(x, 'col', with_near) for x in p4]]
    ppermute x1, waiting for transfers between devices: 72.4 us -> 79.8 us  [local(): near = lax.ppermute(a, 'col', with_near)]
    ppermute x11, waiting for transfers between devices: 117 us -> 124 us  [local(): p5 = [lax.ppermute(x, 'col', with_near) for x in p4]]
    ppermute x4, waiting for transfers between devices: 69 us -> 62.5 us  [local(): p3 = [lax.ppermute(x, 'col', with_near) for x in p2]]
    unnamed x44 -> x74, local copies, waits for them, and re-layouts: 19 us -> 24.3 us
  transfers between devices with their start and end apart: 34 -> 34, of which waited for: 11 -> 12; matrix products, arithmetic and copies ran while one was open for 2% -> 2% of each run, Pallas kernels for 17% -> 17%
where the time goes in v4:
time: 552 us; the launch traced here: 549 us
  waiting for transfers between devices  345 us (62%)
  Pallas kernels  95.1 us (17%)
  starting transfers between devices  70 us (13%)
  local copies, waits for them, and re-layouts  37.7 us (7%)
    ppermute x11, waiting for transfers between devices, local(): p5 = [lax.ppermute(x, 'col', with_near) for x in p4]  124 us
    ppermute x1, waiting for transfers between devices, local(): near = lax.ppermute(a, 'col', with_near)  79.8 us
    ppermute x3, waiting for transfers between devices, local(): lax.ppermute(b_own, 'row', [(p, (p - s) % side) for p in range(side)])  79.2 us
    pallas_call x7, Pallas kernels, _group_product(): pl.pallas_call(functools.partial(_mm_kernel, side), grid=(size // BM,), o...  76.8 us
    ppermute x4, waiting for transfers between devices, local(): p3 = [lax.ppermute(x, 'col', with_near) for x in p2]  62.5 us
    ppermute x11, starting transfers between devices, local(): p4 = [lax.ppermute(x, 'col', inner) for x in near]  31.5 us
    unnamed x74, local copies, waits for them, and re-layouts  24.3 us
    ppermute x11, starting transfers between devices, local(): p5 = [lax.ppermute(x, 'col', with_near) for x in p4]  23.3 us
  transfers between devices with their start and end apart: 34, of which 12 were waited for; matrix products, arithmetic and copies ran while one was open for 2% of the time, Pallas kernels for 17%

profile of v4, /device:TPU:28, one launch (start us, length us, event | category | flops | bytes accessed | tf_op | source)
XLA Modules:
  0.0 548.8 jit_solution(9777881728133776505)
XLA Ops:
  1.6 3.8 fusion.1
  6.2 1.4 copy-done.4
  8.4 38.4 %collective-permute-done.3.refs_1_ = bf16[512,2048]{1,0:T(8,128)(2,1)S(1)} collective-permute-done((bf16[512,2048]{1,0:T(8,128)(2,1)}, bf16[512,2048]{1,0:T(8,128)(2,1)S(1)}, u32[]{:S(2)}, u32[]{:S(2)}) %collective-permute-start.3) | collective-permute-done | bytes 2097184 | tf_op jit(solution)/shard_map/ppermute | solution.py:177
  48.0 1.3 collective-permute-start.5
  49.4 40.8 %collective-permute-done.4.refs_2_ = bf16[512,2048]{1,0:T(8,128)(2,1)S(1)} collective-permute-done((bf16[512,2048]{1,0:T(8,128)(2,1)}, bf16[512,2048]{1,0:T(8,128)(2,1)S(1)}, u32[]{:S(2)}, u32[]{:S(2)}) %collective-permute-start.4) | collective-permute-done | bytes 2097184 | tf_op jit(solution)/shard_map/ppermute | solution.py:177
  91.5 2.0 collective-permute-start.22
  93.5 1.3 copy-done.8
  97.0 5.4 collective-permute-start.29
  102.3 1.4 copy-done.10
  103.7 79.8 %collective-permute-done = bf16[8192,512]{1,0:T(8,128)(2,1)S(1)} collective-permute-done((bf16[8192,512]{1,0:T(8,128)(2,1)}, bf16[8192,512]{1,0:T(8,128)(2,1)S(1)}, u32[]{:S(2)}, u32[]{:S(2)}) %collective-permute-start) | collective-permute-done | bytes 8388640 | tf_op jit(solution)/shard_map/ppermute | solution.py:167
  183.5 3.4 copy-done.36
  187.4 5.8 %fusion = (bf16[1024,512]{1,0:T(8,128)(2,1)S(1)}, bf16[1024,512]{1,0:T(8,128)(2,1)}, bf16[1024,512]{1,0:T(8,128)(2,1)}, bf16[1024,512]{1,0:T(8,128)(2,1)}, bf16[...) fusion(bf16[8192,512]{1,0:T(8,128)(2,1)} %copy-done.36), kind=kLoop, calls=%fused_computation.1 | loop fusion | bytes 14680064 | tf_op jit(solution)/shard_map/slice | solution.py:172
  193.2 1.4 copy-done.26
  194.6 1.7 collective-permute-start.32
  196.3 9.5 %collective-permute-start.30 = (bf16[1024,512]{1,0:T(8,128)(2,1)}, bf16[1024,512]{1,0:T(8,128)(2,1)}, u32[]{:S(2)}, u32[]{:S(2)}) collective-permute-start(bf16[1024,512]{1,0:T(8,128)(2,1)} %get-tuple-element.6.near), channel_id=1, source_target_pairs={{0,0},{4,8},{8,4},{12,12},{1,1},{5,9},{9,5},{13,13},{2,2},{6,10},{... | collective-permute-start | bytes 3145736 | tf_op jit(solution)/shard_map/ppermute | solution.py:173
  208.1 20.4 %collective-permute-done.29.p3 = bf16[2048,512]{1,0:T(8,128)(2,1)S(1)} collective-permute-done((bf16[2048,512]{1,0:T(8,128)(2,1)S(1)}, bf16[2048,512]{1,0:T(8,128)(2,1)S(1)}, u32[]{:S(2)}, u32[]{:S(2)}) %collective-permute-start.29) | collective-permute-done | bytes 2097184 | tf_op jit(solution)/shard_map/ppermute | solution.py:171
  228.5 1.3 copy-done.12
  231.2 42.2 %collective-permute-done.7.p3 = bf16[2048,512]{1,0:T(8,128)(2,1)S(1)} collective-permute-done((bf16[2048,512]{1,0:T(8,128)(2,1)S(1)}, bf16[2048,512]{1,0:T(8,128)(2,1)S(1)}, u32[]{:S(2)}, u32[]{:S(2)}) %collective-permute-start.7) | collective-permute-done | bytes 2097184 | tf_op jit(solution)/shard_map/ppermute | solution.py:171
  276.1 9.5 %collective-permute-start.26 = (bf16[1024,512]{1,0:T(8,128)(2,1)}, bf16[1024,512]{1,0:T(8,128)(2,1)}, u32[]{:S(2)}, u32[]{:S(2)}) collective-permute-start(bf16[1024,512]{1,0:T(8,128)(2,1)} %get-tuple-element.7.near), channel_id=1, source_target_pairs={{0,0},{4,8},{8,4},{12,12},{1,1},{5,9},{9,5},{13,13},{2,2},{6,10},{... | collective-permute-start | bytes 3145736 | tf_op jit(solution)/shard_map/ppermute | solution.py:173
  285.6 3.1 collective-permute-start.33
  288.7 1.8 slice.63.near
  291.2 5.4 collective-permute-start.12
  296.7 1.6 copy-done.21
  298.3 1.6 copy-done.23
  299.9 1.6 copy-done.25
  301.4 1.6 copy-done.27
  307.8 2.3 early_product.6.early
  311.1 13.9 %collective-permute-start.31 = (bf16[1024,512]{1,0:T(8,128)(2,1)}, bf16[1024,512]{1,0:T(8,128)(2,1)S(1)}, u32[]{:S(2)}, u32[]{:S(2)}) collective-permute-start(bf16[1024,512]{1,0:T(8,128)(2,1)} %collective-permute-done.30.p4), channel_id=1, source_target_pairs={{0,4},{4,0},{8,12},{12,8},{1,5},{5,1},{9,13},{13,9},{2,6},{6,2},{1... | collective-permute-start | bytes 3145736 | tf_op jit(solution)/shard_map/ppermute | solution.py:174
  325.0 5.7 %early_product.7.early = f32[512,2048]{1,0:T(8,128)S(1)} custom-call(bf16[2048,512]{1,0:T(8,128)(2,1)S(1)} %get-tuple-element.14.own, bf16[512,512]{1,0:T(8,128)(2,1)} %slice.63.near, bf16[2048,512]{1,0:T(8,128)(2,1)S(1)} %copy-done.1, bf16[2048,512]{1,0:T(8,128)(2,1)S(1)} %copy-done.3, bf16[512,512]{1,0:T(8,128)(2,1)} %collective-permute-done.12.p4, ...), custom_call_target="tpu_custom_call" | custom-call | flops 4294967296 | bytes 4194304 | tf_op jit(solution)/shard_map/early_product/pallas_call | solution.py:96
  331.6 9.3 %collective-permute-done.33.p5 = bf16[1024,512]{1,0:T(8,128)(2,1)} collective-permute-done((bf16[1024,512]{1,0:T(8,128)(2,1)}, bf16[1024,512]{1,0:T(8,128)(2,1)}, u32[]{:S(2)}, u32[]{:S(2)}) %collective-permute-start.33) | collective-permute-done | bytes 1048608 | tf_op jit(solution)/shard_map/ppermute | solution.py:174
  341.4 11.4 %group_product.7.rest_0_ = bf16[8192,2048]{1,0:T(8,128)(2,1)} custom-call(bf16[2048,512]{1,0:T(8,128)(2,1)S(1)} %copy-done.5, bf16[1024,512]{1,0:T(8,128)(2,1)S(1)} %get-tuple-element.5.near, bf16[2048,512]{1,0:T(8,128)(2,1)S(1)} %copy-done.11, bf16[2048,512]{1,0:T(8,128)(2,1)S(1)} %copy-done.13, bf16[1024,512]{1,0:T(8,128)(2,1)} %collective-permute-done.32.p4, ...), custom_call_target="tpu_custom_call" | custom-call | flops 8589934592 | bytes 8388608 | tf_op jit(solution)/shard_map/group_product/pallas_call | solution.py:77
  352.8 1.6 collective-permute-start.17
  355.5 7.8 %collective-permute-done.31.p5 = bf16[1024,512]{1,0:T(8,128)(2,1)S(1)} collective-permute-done((bf16[1024,512]{1,0:T(8,128)(2,1)}, bf16[1024,512]{1,0:T(8,128)(2,1)S(1)}, u32[]{:S(2)}, u32[]{:S(2)}) %collective-permute-start.31) | collective-permute-done | bytes 1048608 | tf_op jit(solution)/shard_map/ppermute | solution.py:174
  363.8 11.4 %group_product.8.rest_0_ = bf16[8192,2048]{1,0:T(8,128)(2,1)} custom-call(bf16[2048,512]{1,0:T(8,128)(2,1)S(1)} %copy-done.5, bf16[1024,512]{1,0:T(8,128)(2,1)} %get-tuple-element.6.near, bf16[2048,512]{1,0:T(8,128)(2,1)S(1)} %copy-done.11, bf16[2048,512]{1,0:T(8,128)(2,1)S(1)} %copy-done.13, ...), custom_call_target="tpu_custom_call", output_to_operand_aliasing={{}: (7, {})} | custom-call | flops 8589934592 | bytes 8388608 | tf_op jit(solution)/shard_map/group_product/pallas_call | solution.py:77
  375.9 9.9 %collective-permute-done.27.p5 = bf16[1024,512]{1,0:T(8,128)(2,1)S(1)} collective-permute-done((bf16[1024,512]{1,0:T(8,128)(2,1)}, bf16[1024,512]{1,0:T(8,128)(2,1)S(1)}, u32[]{:S(2)}, u32[]{:S(2)}) %collective-permute-start.27) | collective-permute-done | bytes 1048608 | tf_op jit(solution)/shard_map/ppermute | solution.py:174
  386.2 11.6 %group_product.9.rest_0_ = bf16[8192,2048]{1,0:T(8,128)(2,1)} custom-call(bf16[2048,512]{1,0:T(8,128)(2,1)S(1)} %copy-done.9, bf16[1024,512]{1,0:T(8,128)(2,1)} %get-tuple-element.7.near, bf16[2048,512]{1,0:T(8,128)(2,1)} %collective-permute-done.22.p2, bf16[2048,512]{1,0:T(8,128)(2,1)} %collective-permute-done.23.p3, ...), custom_call_target="tpu_custom_call", output_to_operand_aliasing={{}: (7, {})} | custom-call | flops 8589934592 | bytes 8388608 | tf_op jit(solution)/shard_map/group_product/pallas_call | solution.py:77
  397.8 1.6 collective-permute-start.9
  399.5 53.7 %collective-permute-done.25.p5 = bf16[1024,512]{1,0:T(8,128)(2,1)S(1)} collective-permute-done((bf16[1024,512]{1,0:T(8,128)(2,1)S(1)}, bf16[1024,512]{1,0:T(8,128)(2,1)S(1)}, u32[]{:S(2)}, u32[]{:S(2)}) %collective-permute-start.25) | collective-permute-done | bytes 1048608 | tf_op jit(solution)/shard_map/ppermute | solution.py:174
  453.6 11.4 %group_product.10.rest_0_ = bf16[8192,2048]{1,0:T(8,128)(2,1)} custom-call(bf16[2048,512]{1,0:T(8,128)(2,1)S(1)} %copy-done.9, bf16[1024,512]{1,0:T(8,128)(2,1)S(1)} %copy-done.19, bf16[2048,512]{1,0:T(8,128)(2,1)} %collective-permute-done.22.p2, bf16[2048,512]{1,0:T(8,128)(2,1)} %collective-permute-done.23.p3, ...), custom_call_target="tpu_custom_call", output_to_operand_aliasing={{}: (7, {})} | custom-call | flops 8589934592 | bytes 8388608 | tf_op jit(solution)/shard_map/group_product/pallas_call | solution.py:77
  465.1 1.6 collective-permute-start.2
  467.1 8.6 %collective-permute-done.21.p5 = bf16[1024,512]{1,0:T(8,128)(2,1)S(1)} collective-permute-done((bf16[1024,512]{1,0:T(8,128)(2,1)S(1)}, bf16[1024,512]{1,0:T(8,128)(2,1)S(1)}, u32[]{:S(2)}, u32[]{:S(2)}) %collective-permute-start.21) | collective-permute-done | bytes 1048608 | tf_op jit(solution)/shard_map/ppermute | solution.py:174
  476.1 10.3 %group_product.11.rest_0_ = bf16[8192,2048]{1,0:T(8,128)(2,1)} custom-call(bf16[2048,512]{1,0:T(8,128)(2,1)S(1)} %copy-done.7, bf16[1024,512]{1,0:T(8,128)(2,1)S(1)} %copy-done.18, bf16[2048,512]{1,0:T(8,128)(2,1)S(1)} %copy-done.15, bf16[2048,512]{1,0:T(8,128)(2,1)S(1)} %collective-permute-done.17.p3, ...), custom_call_target="tpu_custom_call", output_to_operand_aliasing={{}: (7, {})} | custom-call | flops 8589934592 | bytes 8388608 | tf_op jit(solution)/shard_map/group_product/pallas_call | solution.py:77
  486.4 14.5 %collective-permute-done.19.p5 = bf16[1024,512]{1,0:T(8,128)(2,1)S(1)} collective-permute-done((bf16[1024,512]{1,0:T(8,128)(2,1)S(1)}, bf16[1024,512]{1,0:T(8,128)(2,1)S(1)}, u32[]{:S(2)}, u32[]{:S(2)}) %collective-permute-start.19) | collective-permute-done | bytes 1048608 | tf_op jit(solution)/shard_map/ppermute | solution.py:174
  501.4 10.3 %group_product.12.rest_0_ = bf16[8192,2048]{1,0:T(8,128)(2,1)} custom-call(bf16[2048,512]{1,0:T(8,128)(2,1)S(1)} %copy-done.7, bf16[1024,512]{1,0:T(8,128)(2,1)S(1)} %copy-done.17, bf16[2048,512]{1,0:T(8,128)(2,1)S(1)} %copy-done.15, bf16[2048,512]{1,0:T(8,128)(2,1)S(1)} %collective-permute-done.17.p3, ...), custom_call_target="tpu_custom_call", output_to_operand_aliasing={{}: (7, {})} | custom-call | flops 8589934592 | bytes 8388608 | tf_op jit(solution)/shard_map/group_product/pallas_call | solution.py:77
  511.7 20.1 %collective-permute-done.15.p5 = bf16[1024,512]{1,0:T(8,128)(2,1)S(1)} collective-permute-done((bf16[1024,512]{1,0:T(8,128)(2,1)S(1)}, bf16[1024,512]{1,0:T(8,128)(2,1)S(1)}, u32[]{:S(2)}, u32[]{:S(2)}) %collective-permute-start.15) | collective-permute-done | bytes 1048608 | tf_op jit(solution)/shard_map/ppermute | solution.py:174
  531.8 10.3 %group_product.13.c_in = bf16[8192,2048]{1,0:T(8,128)(2,1)} custom-call(bf16[2048,512]{1,0:T(8,128)(2,1)S(1)} %get-tuple-element.14.own, bf16[1024,512]{1,0:T(8,128)(2,1)S(1)} %copy-done.16, bf16[2048,512]{1,0:T(8,128)(2,1)S(1)} %copy-done.1, bf16[2048,512]{1,0:T(8,128)(2,1)S(1)} %copy-done.3, ...), custom_call_target="tpu_custom_call", output_to_operand_aliasing={{}: (7, {})} | custom-call | flops 8589934592 | bytes 8388608 | tf_op jit(solution)/shard_map/group_product/pallas_call | solution.py:77
  542.2 2.4 late_product.4.c_in
  544.6 1.7 late_product.5.c_in
  (116 shorter events, 29.5 us)
Async XLA Ops:
  0.0 48.0 %copy-start.20 = (bf16[512,2048]{1,0:T(8,128)(2,1)S(1)}, bf16[512,2048]{1,0:T(8,128)(2,1)}, u32[]{:S(2)}) copy-start(bf16[512,2048]{1,0:T(8,128)(2,1)} %refs_0_.1) | copy-start | bytes 6291460
  0.0 183.5 %collective-permute-start = (bf16[8192,512]{1,0:T(8,128)(2,1)}, bf16[8192,512]{1,0:T(8,128)(2,1)S(1)}, u32[]{:S(2)}, u32[]{:S(2)}) collective-permute-start(bf16[8192,512]{1,0:T(8,128)(2,1)} %param.2), channel_id=1, source_target_pairs={{0,4},{4,0},{8,12},{12,8},{1,5},{5,1},{9,13},{13,9},{2,6},{6,2},{1... | collective-permute-start | bytes 25165832 | tf_op jit(solution)/shard_map/ppermute | solution.py:167
  0.5 46.3 %collective-permute-start.3 = (bf16[512,2048]{1,0:T(8,128)(2,1)}, bf16[512,2048]{1,0:T(8,128)(2,1)S(1)}, u32[]{:S(2)}, u32[]{:S(2)}) collective-permute-start(bf16[512,2048]{1,0:T(8,128)(2,1)} %refs_0_.1), channel_id=1, source_target_pairs={{0,3},{1,0},{2,1},{3,2},{4,7},{5,4},{6,5},{7,6},{8,11},{9,8},{10,9... | collective-permute-start | bytes 6291464 | tf_op jit(solution)/shard_map/ppermute | solution.py:177
  0.5 89.8 %collective-permute-start.4 = (bf16[512,2048]{1,0:T(8,128)(2,1)}, bf16[512,2048]{1,0:T(8,128)(2,1)S(1)}, u32[]{:S(2)}, u32[]{:S(2)}) collective-permute-start(bf16[512,2048]{1,0:T(8,128)(2,1)} %refs_0_.1), channel_id=1, source_target_pairs={{0,2},{1,3},{2,0},{3,1},{4,6},{5,7},{6,4},{7,5},{8,10},{9,11},{10,... | collective-permute-start | bytes 6291464 | tf_op jit(solution)/shard_map/ppermute | solution.py:177
  5.4 89.4 %collective-permute-start.28 = (bf16[2048,512]{1,0:T(8,128)(2,1)S(1)}, bf16[2048,512]{1,0:T(8,128)(2,1)S(1)}, u32[]{:S(2)}, u32[]{:S(2)}) collective-permute-start(bf16[2048,512]{1,0:T(8,128)(2,1)S(1)} %get-tuple-element.12.own), channel_id=1, source_target_pairs={{0,0},{4,8},{8,4},{12,12},{1,1},{5,9},{9,5},{13,13},{2,2},{6,10},{... | collective-permute-start | bytes 6291464 | tf_op jit(solution)/shard_map/ppermute | solution.py:170
  7.6 89.4 %collective-permute-start.6 = (bf16[2048,512]{1,0:T(8,128)(2,1)S(1)}, bf16[2048,512]{1,0:T(8,128)(2,1)S(1)}, u32[]{:S(2)}, u32[]{:S(2)}) collective-permute-start(bf16[2048,512]{1,0:T(8,128)(2,1)S(1)} %get-tuple-element.14.own), channel_id=1, source_target_pairs={{0,0},{4,8},{8,4},{12,12},{1,1},{5,9},{9,5},{13,13},{2,2},{6,10},{... | collective-permute-start | bytes 6291464 | tf_op jit(solution)/shard_map/ppermute | solution.py:170
  48.0 145.2 %collective-permute-start.5 = (bf16[512,2048]{1,0:T(8,128)(2,1)S(1)}, bf16[512,2048]{1,0:T(8,128)(2,1)S(1)}, u32[]{:S(2)}, u32[]{:S(2)}) collective-permute-start(bf16[512,2048]{1,0:T(8,128)(2,1)S(1)} %copy-done.20), channel_id=1, source_target_pairs={{0,1},{1,2},{2,3},{3,0},{4,5},{5,6},{6,7},{7,4},{8,9},{9,10},{10,1... | collective-permute-start | bytes 6291464 | tf_op jit(solution)/shard_map/ppermute | solution.py:177
  91.5 104.8 %collective-permute-start.22 = (bf16[2048,512]{1,0:T(8,128)(2,1)S(1)}, bf16[2048,512]{1,0:T(8,128)(2,1)}, u32[]{:S(2)}, u32[]{:S(2)}) collective-permute-start(bf16[2048,512]{1,0:T(8,128)(2,1)S(1)} %get-tuple-element.15.own), channel_id=1, source_target_pairs={{0,0},{4,8},{8,4},{12,12},{1,1},{5,9},{9,5},{13,13},{2,2},{6,10},{... | collective-permute-start | bytes 6291464 | tf_op jit(solution)/shard_map/ppermute | solution.py:170
  94.8 111.9 %collective-permute-start.16 = (bf16[2048,512]{1,0:T(8,128)(2,1)S(1)}, bf16[2048,512]{1,0:T(8,128)(2,1)S(1)}, u32[]{:S(2)}, u32[]{:S(2)}) collective-permute-start(bf16[2048,512]{1,0:T(8,128)(2,1)S(1)} %get-tuple-element.13.own), channel_id=1, source_target_pairs={{0,0},{4,8},{8,4},{12,12},{1,1},{5,9},{9,5},{13,13},{2,2},{6,10},{... | collective-permute-start | bytes 6291464 | tf_op jit(solution)/shard_map/ppermute | solution.py:170
  97.0 96.3 %copy-start = (bf16[2048,512]{1,0:T(8,128)(2,1)}, bf16[2048,512]{1,0:T(8,128)(2,1)S(1)}, u32[]{:S(2)}) copy-start(bf16[2048,512]{1,0:T(8,128)(2,1)S(1)} %collective-permute-done.6.p2) | copy-start | bytes 6291460
  97.0 131.5 %collective-permute-start.29 = (bf16[2048,512]{1,0:T(8,128)(2,1)S(1)}, bf16[2048,512]{1,0:T(8,128)(2,1)S(1)}, u32[]{:S(2)}, u32[]{:S(2)}) collective-permute-start(bf16[2048,512]{1,0:T(8,128)(2,1)S(1)} %collective-permute-done.28.p2), channel_id=1, source_target_pairs={{0,4},{4,0},{8,12},{12,8},{1,5},{5,1},{9,13},{13,9},{2,6},{6,2},{1... | collective-permute-start | bytes 6291464 | tf_op jit(solution)/shard_map/ppermute | solution.py:171
  186.9 86.5 %collective-permute-start.7 = (bf16[2048,512]{1,0:T(8,128)(2,1)S(1)}, bf16[2048,512]{1,0:T(8,128)(2,1)S(1)}, u32[]{:S(2)}, u32[]{:S(2)}) collective-permute-start(bf16[2048,512]{1,0:T(8,128)(2,1)S(1)} %collective-permute-done.6.p2), channel_id=1, source_target_pairs={{0,4},{4,0},{8,12},{12,8},{1,5},{5,1},{9,13},{13,9},{2,6},{6,2},{1... | collective-permute-start | bytes 6291464 | tf_op jit(solution)/shard_map/ppermute | solution.py:171
  194.6 91.0 %collective-permute-start.32 = (bf16[1024,512]{1,0:T(8,128)(2,1)S(1)}, bf16[1024,512]{1,0:T(8,128)(2,1)}, u32[]{:S(2)}, u32[]{:S(2)}) collective-permute-start(bf16[1024,512]{1,0:T(8,128)(2,1)S(1)} %get-tuple-element.5.near), channel_id=1, source_target_pairs={{0,0},{4,8},{8,4},{12,12},{1,1},{5,9},{9,5},{13,13},{2,2},{6,10},{... | collective-permute-start | bytes 3145736 | tf_op jit(solution)/shard_map/ppermute | solution.py:173
  196.3 114.8 %collective-permute-start.30 = (bf16[1024,512]{1,0:T(8,128)(2,1)}, bf16[1024,512]{1,0:T(8,128)(2,1)}, u32[]{:S(2)}, u32[]{:S(2)}) collective-permute-start(bf16[1024,512]{1,0:T(8,128)(2,1)} %get-tuple-element.6.near), channel_id=1, source_target_pairs={{0,0},{4,8},{8,4},{12,12},{1,1},{5,9},{9,5},{13,13},{2,2},{6,10},{... | collective-permute-start | bytes 3145736 | tf_op jit(solution)/shard_map/ppermute | solution.py:173
  206.8 66.7 %copy-start.14 = (bf16[2048,512]{1,0:T(8,128)(2,1)}, bf16[2048,512]{1,0:T(8,128)(2,1)S(1)}, u32[]{:S(2)}) copy-start(bf16[2048,512]{1,0:T(8,128)(2,1)S(1)} %collective-permute-done.16.p2) | copy-start | bytes 6291460
  206.8 68.6 %collective-permute-start.8 = (bf16[128,512]{1,0:T(8,128)(2,1)S(1)}, bf16[128,512]{1,0:T(8,128)(2,1)S(1)}, u32[]{:S(2)}, u32[]{:S(2)}) collective-permute-start(bf16[128,512]{1,0:T(8,128)(2,1)S(1)} %get-tuple-element.16.near), channel_id=1, source_target_pairs={{0,0},{4,8},{8,4},{12,12},{1,1},{5,9},{9,5},{13,13},{2,2},{6,10},{... | collective-permute-start | bytes 393224 | tf_op jit(solution)/shard_map/ppermute | solution.py:173
  229.8 123.0 %collective-permute-start.23 = (bf16[2048,512]{1,0:T(8,128)(2,1)}, bf16[2048,512]{1,0:T(8,128)(2,1)}, u32[]{:S(2)}, u32[]{:S(2)}) collective-permute-start(bf16[2048,512]{1,0:T(8,128)(2,1)} %collective-permute-done.22.p2), channel_id=1, source_target_pairs={{0,4},{4,0},{8,12},{12,8},{1,5},{5,1},{9,13},{13,9},{2,6},{6,2},{1... | collective-permute-start | bytes 6291464 | tf_op jit(solution)/shard_map/ppermute | solution.py:171
  274.7 15.8 %collective-permute-start.10 = (bf16[256,512]{1,0:T(8,128)(2,1)S(1)}, bf16[256,512]{1,0:T(8,128)(2,1)S(1)}, u32[]{:S(2)}, u32[]{:S(2)}) collective-permute-start(bf16[256,512]{1,0:T(8,128)(2,1)S(1)} %slice.62.near), channel_id=1, source_target_pairs={{0,0},{4,8},{8,4},{12,12},{1,1},{5,9},{9,5},{13,13},{2,2},{6,10},{... | collective-permute-start | bytes 786440 | tf_op jit(solution)/shard_map/ppermute | solution.py:173
  275.4 15.1 %copy-start.32 = (bf16[128,512]{1,0:T(8,128)(2,1)}, bf16[128,512]{1,0:T(8,128)(2,1)S(1)}, u32[]{:S(2)}) copy-start(bf16[128,512]{1,0:T(8,128)(2,1)S(1)} %collective-permute-done.8.p4) | copy-start | bytes 393220
  275.4 0.7 collective-permute-start.1
  276.1 20.5 %copy-start.34 = (bf16[128,512]{1,0:T(8,128)(2,1)}, bf16[128,512]{1,0:T(8,128)(2,1)S(1)}, u32[]{:S(2)}) copy-start(bf16[128,512]{1,0:T(8,128)(2,1)S(1)} %collective-permute-done.1.p4) | copy-start | bytes 393220
  276.1 54.6 %collective-permute-start.26 = (bf16[1024,512]{1,0:T(8,128)(2,1)}, bf16[1024,512]{1,0:T(8,128)(2,1)}, u32[]{:S(2)}, u32[]{:S(2)}) collective-permute-start(bf16[1024,512]{1,0:T(8,128)(2,1)} %get-tuple-element.7.near), channel_id=1, source_target_pairs={{0,0},{4,8},{8,4},{12,12},{1,1},{5,9},{9,5},{13,13},{2,2},{6,10},{... | collective-permute-start | bytes 3145736 | tf_op jit(solution)/shard_map/ppermute | solution.py:173
  285.6 55.4 %collective-permute-start.33 = (bf16[1024,512]{1,0:T(8,128)(2,1)}, bf16[1024,512]{1,0:T(8,128)(2,1)}, u32[]{:S(2)}, u32[]{:S(2)}) collective-permute-start(bf16[1024,512]{1,0:T(8,128)(2,1)} %collective-permute-done.32.p4), channel_id=1, source_target_pairs={{0,4},{4,0},{8,12},{12,8},{1,5},{5,1},{9,13},{13,9},{2,6},{6,2},{1... | collective-permute-start | bytes 3145736 | tf_op jit(solution)/shard_map/ppermute | solution.py:174
  291.2 18.9 %collective-permute-start.12 = (bf16[512,512]{1,0:T(8,128)(2,1)}, bf16[512,512]{1,0:T(8,128)(2,1)}, u32[]{:S(2)}, u32[]{:S(2)}) collective-permute-start(bf16[512,512]{1,0:T(8,128)(2,1)} %slice.63.near), channel_id=1, source_target_pairs={{0,0},{4,8},{8,4},{12,12},{1,1},{5,9},{9,5},{13,13},{2,2},{6,10},{... | collective-permute-start | bytes 1572872 | tf_op jit(solution)/shard_map/ppermute | solution.py:173
  310.2 20.5 %copy-start.18 = (bf16[1024,512]{1,0:T(8,128)(2,1)S(1)}, bf16[1024,512]{1,0:T(8,128)(2,1)}, u32[]{:S(2)}) copy-start(bf16[1024,512]{1,0:T(8,128)(2,1)} %get-tuple-element.9.near) | copy-start | bytes 3145732
  310.2 31.2 %copy-start.5 = (bf16[2048,512]{1,0:T(8,128)(2,1)S(1)}, bf16[2048,512]{1,0:T(8,128)(2,1)}, u32[]{:S(2)}) copy-start(bf16[2048,512]{1,0:T(8,128)(2,1)} %copy-done.4) | copy-start | bytes 6291460
  310.2 31.2 %copy-start.11 = (bf16[2048,512]{1,0:T(8,128)(2,1)S(1)}, bf16[2048,512]{1,0:T(8,128)(2,1)}, u32[]{:S(2)}) copy-start(bf16[2048,512]{1,0:T(8,128)(2,1)} %copy-done.10) | copy-start | bytes 6291460
  310.2 31.2 %copy-start.13 = (bf16[2048,512]{1,0:T(8,128)(2,1)S(1)}, bf16[2048,512]{1,0:T(8,128)(2,1)}, u32[]{:S(2)}) copy-start(bf16[2048,512]{1,0:T(8,128)(2,1)} %copy-done.12) | copy-start | bytes 6291460
  310.2 44.2 %collective-permute-start.24 = (bf16[1024,512]{1,0:T(8,128)(2,1)S(1)}, bf16[1024,512]{1,0:T(8,128)(2,1)S(1)}, u32[]{:S(2)}, u32[]{:S(2)}) collective-permute-start(bf16[1024,512]{1,0:T(8,128)(2,1)S(1)} %copy-done.19), channel_id=1, source_target_pairs={{0,0},{4,8},{8,4},{12,12},{1,1},{5,9},{9,5},{13,13},{2,2},{6,10},{... | collective-permute-start | bytes 3145736 | tf_op jit(solution)/shard_map/ppermute | solution.py:173
  311.1 52.2 %collective-permute-start.31 = (bf16[1024,512]{1,0:T(8,128)(2,1)}, bf16[1024,512]{1,0:T(8,128)(2,1)S(1)}, u32[]{:S(2)}, u32[]{:S(2)}) collective-permute-start(bf16[1024,512]{1,0:T(8,128)(2,1)} %collective-permute-done.30.p4), channel_id=1, source_target_pairs={{0,4},{4,0},{8,12},{12,8},{1,5},{5,1},{9,13},{13,9},{2,6},{6,2},{1... | collective-permute-start | bytes 3145736 | tf_op jit(solution)/shard_map/ppermute | solution.py:174
  330.7 22.1 %copy-start.15 = (bf16[2048,512]{1,0:T(8,128)(2,1)S(1)}, bf16[2048,512]{1,0:T(8,128)(2,1)}, u32[]{:S(2)}) copy-start(bf16[2048,512]{1,0:T(8,128)(2,1)} %copy-done.14) | copy-start | bytes 6291460
  330.7 23.7 %copy-start.17 = (bf16[1024,512]{1,0:T(8,128)(2,1)S(1)}, bf16[1024,512]{1,0:T(8,128)(2,1)}, u32[]{:S(2)}) copy-start(bf16[1024,512]{1,0:T(8,128)(2,1)} %get-tuple-element.10.near) | copy-start | bytes 3145732
  330.8 44.4 %collective-permute-start.20 = (bf16[1024,512]{1,0:T(8,128)(2,1)S(1)}, bf16[1024,512]{1,0:T(8,128)(2,1)S(1)}, u32[]{:S(2)}, u32[]{:S(2)}) collective-permute-start(bf16[1024,512]{1,0:T(8,128)(2,1)S(1)} %copy-done.18), channel_id=1, source_target_pairs={{0,0},{4,8},{8,4},{12,12},{1,1},{5,9},{9,5},{13,13},{2,2},{6,10},{... | collective-permute-start | bytes 3145736 | tf_op jit(solution)/shard_map/ppermute | solution.py:173
  340.9 44.8 %collective-permute-start.27 = (bf16[1024,512]{1,0:T(8,128)(2,1)}, bf16[1024,512]{1,0:T(8,128)(2,1)S(1)}, u32[]{:S(2)}, u32[]{:S(2)}) collective-permute-start(bf16[1024,512]{1,0:T(8,128)(2,1)} %collective-permute-done.26.p4), channel_id=1, source_target_pairs={{0,4},{4,0},{8,12},{12,8},{1,5},{5,1},{9,13},{13,9},{2,6},{6,2},{1... | collective-permute-start | bytes 3145736 | tf_op jit(solution)/shard_map/ppermute | solution.py:174
  352.8 112.2 %collective-permute-start.17 = (bf16[2048,512]{1,0:T(8,128)(2,1)S(1)}, bf16[2048,512]{1,0:T(8,128)(2,1)S(1)}, u32[]{:S(2)}, u32[]{:S(2)}) collective-permute-start(bf16[2048,512]{1,0:T(8,128)(2,1)S(1)} %copy-done.15), channel_id=1, source_target_pairs={{0,4},{4,0},{8,12},{12,8},{1,5},{5,1},{9,13},{13,9},{2,6},{6,2},{1... | collective-permute-start | bytes 6291464 | tf_op jit(solution)/shard_map/ppermute | solution.py:171
  354.5 20.7 %copy-start.16 = (bf16[1024,512]{1,0:T(8,128)(2,1)S(1)}, bf16[1024,512]{1,0:T(8,128)(2,1)}, u32[]{:S(2)}) copy-start(bf16[1024,512]{1,0:T(8,128)(2,1)} %get-tuple-element.11.near) | copy-start | bytes 3145732
  354.5 31.8 %copy-start.9 = (bf16[2048,512]{1,0:T(8,128)(2,1)S(1)}, bf16[2048,512]{1,0:T(8,128)(2,1)}, u32[]{:S(2)}) copy-start(bf16[2048,512]{1,0:T(8,128)(2,1)} %copy-done.8) | copy-start | bytes 6291460
  354.5 43.4 %collective-permute-start.18 = (bf16[1024,512]{1,0:T(8,128)(2,1)S(1)}, bf16[1024,512]{1,0:T(8,128)(2,1)S(1)}, u32[]{:S(2)}, u32[]{:S(2)}) collective-permute-start(bf16[1024,512]{1,0:T(8,128)(2,1)S(1)} %copy-done.17), channel_id=1, source_target_pairs={{0,0},{4,8},{8,4},{12,12},{1,1},{5,9},{9,5},{13,13},{2,2},{6,10},{... | collective-permute-start | bytes 3145736 | tf_op jit(solution)/shard_map/ppermute | solution.py:173
  363.3 89.9 %collective-permute-start.25 = (bf16[1024,512]{1,0:T(8,128)(2,1)S(1)}, bf16[1024,512]{1,0:T(8,128)(2,1)S(1)}, u32[]{:S(2)}, u32[]{:S(2)}) collective-permute-start(bf16[1024,512]{1,0:T(8,128)(2,1)S(1)} %collective-permute-done.24.p4), channel_id=1, source_target_pairs={{0,4},{4,0},{8,12},{12,8},{1,5},{5,1},{9,13},{13,9},{2,6},{6,2},{1... | collective-permute-start | bytes 3145736 | tf_op jit(solution)/shard_map/ppermute | solution.py:174
  375.2 91.5 %collective-permute-start.14 = (bf16[1024,512]{1,0:T(8,128)(2,1)S(1)}, bf16[1024,512]{1,0:T(8,128)(2,1)S(1)}, u32[]{:S(2)}, u32[]{:S(2)}) collective-permute-start(bf16[1024,512]{1,0:T(8,128)(2,1)S(1)} %copy-done.16), channel_id=1, source_target_pairs={{0,0},{4,8},{8,4},{12,12},{1,1},{5,9},{9,5},{13,13},{2,2},{6,10},{... | collective-permute-start | bytes 3145736 | tf_op jit(solution)/shard_map/ppermute | solution.py:173
  385.8 89.9 %collective-permute-start.21 = (bf16[1024,512]{1,0:T(8,128)(2,1)S(1)}, bf16[1024,512]{1,0:T(8,128)(2,1)S(1)}, u32[]{:S(2)}, u32[]{:S(2)}) collective-permute-start(bf16[1024,512]{1,0:T(8,128)(2,1)S(1)} %collective-permute-done.20.p4), channel_id=1, source_target_pairs={{0,4},{4,0},{8,12},{12,8},{1,5},{5,1},{9,13},{13,9},{2,6},{6,2},{1... | collective-permute-start | bytes 3145736 | tf_op jit(solution)/shard_map/ppermute | solution.py:174
  397.8 78.3 %copy-start.7 = (bf16[2048,512]{1,0:T(8,128)(2,1)S(1)}, bf16[2048,512]{1,0:T(8,128)(2,1)}, u32[]{:S(2)}) copy-start(bf16[2048,512]{1,0:T(8,128)(2,1)} %copy-done.6) | copy-start | bytes 6291460
  397.8 148.4 %collective-permute-start.9 = (bf16[128,512]{1,0:T(8,128)(2,1)S(1)}, bf16[128,512]{1,0:T(8,128)(2,1)S(1)}, u32[]{:S(2)}, u32[]{:S(2)}) collective-permute-start(bf16[128,512]{1,0:T(8,128)(2,1)S(1)} %copy-done.33), channel_id=1, source_target_pairs={{0,4},{4,0},{8,12},{12,8},{1,5},{5,1},{9,13},{13,9},{2,6},{6,2},{1... | collective-permute-start | bytes 393224 | tf_op jit(solution)/shard_map/ppermute | solution.py:174
  453.2 47.8 %collective-permute-start.19 = (bf16[1024,512]{1,0:T(8,128)(2,1)S(1)}, bf16[1024,512]{1,0:T(8,128)(2,1)S(1)}, u32[]{:S(2)}, u32[]{:S(2)}) collective-permute-start(bf16[1024,512]{1,0:T(8,128)(2,1)S(1)} %collective-permute-done.18.p4), channel_id=1, source_target_pairs={{0,4},{4,0},{8,12},{12,8},{1,5},{5,1},{9,13},{13,9},{2,6},{6,2},{1... | collective-permute-start | bytes 3145736 | tf_op jit(solution)/shard_map/ppermute | solution.py:174
  465.1 82.5 %collective-permute-start.2 = (bf16[128,512]{1,0:T(8,128)(2,1)S(1)}, bf16[128,512]{1,0:T(8,128)(2,1)S(1)}, u32[]{:S(2)}, u32[]{:S(2)}) collective-permute-start(bf16[128,512]{1,0:T(8,128)(2,1)S(1)} %copy-done.35), channel_id=1, source_target_pairs={{0,4},{4,0},{8,12},{12,8},{1,5},{5,1},{9,13},{13,9},{2,6},{6,2},{1... | collective-permute-start | bytes 393224 | tf_op jit(solution)/shard_map/ppermute | solution.py:174
  466.6 77.9 %collective-permute-start.11 = (bf16[256,512]{1,0:T(8,128)(2,1)S(1)}, bf16[256,512]{1,0:T(8,128)(2,1)S(1)}, u32[]{:S(2)}, u32[]{:S(2)}) collective-permute-start(bf16[256,512]{1,0:T(8,128)(2,1)S(1)} %copy-done.31), channel_id=1, source_target_pairs={{0,4},{4,0},{8,12},{12,8},{1,5},{5,1},{9,13},{13,9},{2,6},{6,2},{1... | collective-permute-start | bytes 786440 | tf_op jit(solution)/shard_map/ppermute | solution.py:174
  475.7 56.2 %collective-permute-start.15 = (bf16[1024,512]{1,0:T(8,128)(2,1)S(1)}, bf16[1024,512]{1,0:T(8,128)(2,1)S(1)}, u32[]{:S(2)}, u32[]{:S(2)}) collective-permute-start(bf16[1024,512]{1,0:T(8,128)(2,1)S(1)} %collective-permute-done.14.p4), channel_id=1, source_target_pairs={{0,4},{4,0},{8,12},{12,8},{1,5},{5,1},{9,13},{13,9},{2,6},{6,2},{1... | collective-permute-start | bytes 3145736 | tf_op jit(solution)/shard_map/ppermute | solution.py:174
  500.9 41.2 %collective-permute-start.13 = (bf16[512,512]{1,0:T(8,128)(2,1)}, bf16[512,512]{1,0:T(8,128)(2,1)S(1)}, u32[]{:S(2)}, u32[]{:S(2)}) collective-permute-start(bf16[512,512]{1,0:T(8,128)(2,1)} %collective-permute-done.12.p4), channel_id=1, source_target_pairs={{0,4},{4,0},{8,12},{12,8},{1,5},{5,1},{9,13},{13,9},{2,6},{6,2},{1... | collective-permute-start | bytes 1572872 | tf_op jit(solution)/shard_map/ppermute | solution.py:174
  (23 other events, 36.4 us)

commit v5 on v4

--- a/solution.py
+++ b/solution.py
@@ -9,7 +9,7 @@
 
 
 HALVES = 4
-GROUPS = (1024, 1024, 1024, 1024, 1024, 1024, 1024)
+GROUPS = (2048, 2048, 2048, 1024)
 TAIL = (512, 256, 128, 128)
 BM = 256
 LATE_STEPS = 1
@@ -67,7 +67,8 @@
     total, cols = b.shape
     chunk = _rows(BM, depth, off % p2.shape[0])
     piece = _rows(BM, depth, 0)
-    in_specs = [chunk, piece, chunk, chunk, piece, piece, _kept(b.shape)]
+    full = _rows(BM, depth, off)
+    in_specs = [full, full, chunk, chunk, piece, piece, _kept(b.shape)]
     args = [own, near, p2, p3, p4, p5, b]
     alias = {}
     if c is not None:
@@ -91,13 +92,14 @@
     depth = own.shape[1]
     total, cols = b.shape
     bm = min(BM, size)
+    full = _rows(bm, depth, off)
     chunk = _rows(bm, depth, off % p3.shape[0])
     piece = _rows(bm, depth, 0)
     return pl.pallas_call(
         functools.partial(_early_kernel, side),
         grid=(size // bm,),
         out_shape=pltpu.VMEM((size, cols), jnp.float32),
-        in_specs=[chunk, piece, chunk, chunk, piece, _kept(b.shape)],
+        in_specs=[full, full, chunk, chunk, piece, _kept(b.shape)],
         out_specs=_rows(bm, cols, 0),
         compiler_params=_params(8),
         cost_estimate=_cost(size, total, cols),
@@ -166,11 +168,9 @@
 
         near = lax.ppermute(a, "col", with_near)
         step = rows // HALVES
-        own = [a[h * step : (h + 1) * step] for h in range(HALVES)]
-        p2 = [lax.ppermute(x, "col", inner) for x in own]
+        p2 = [lax.ppermute(a[h * step : (h + 1) * step], "col", inner) for h in range(HALVES)]
         p3 = [lax.ppermute(x, "col", with_near) for x in p2]
-        near = [near[o : o + s] for o, s in zip(offs, sizes)]
-        p4 = [lax.ppermute(x, "col", inner) for x in near]
+        p4 = [lax.ppermute(near[o : o + s], "col", inner) for o, s in zip(offs, sizes)]
         p5 = [lax.ppermute(x, "col", with_near) for x in p4]
 
         blocks = [b_own] + [
@@ -182,13 +182,13 @@
         early = {}
         for g in range(main, len(sizes)):
             h = offs[g] // step
-            early[g] = _early_product(side, own[h], near[g], p2[h], p3[h], p4[g], b, offs[g], sizes[g])
+            early[g] = _early_product(side, a, near, p2[h], p3[h], p4[g], b, offs[g], sizes[g])
 
         c = None
         for g, (off, size) in enumerate(zip(offs, sizes)):
             h = off // step
             if g < main:
-                c = _group_product(side, own[h], near[g], p2[h], p3[h], p4[g], p5[g], b, c, rows, off, size)
+                c = _group_product(side, a, near, p2[h], p3[h], p4[g], p5[g], b, c, rows, off, size)
             else:
                 c = _late_product(side, p5[g], b, early[g], c, off, size)
         return c

time: 552 us -> 740 us (1.34)
  starting transfers between devices: 70 us -> 303 us
  waiting for transfers between devices: 345 us -> 311 us
  local copies, waits for them, and re-layouts: 37.7 us -> 28.2 us
    ppermute x4, starting transfers between devices: 7.9 us -> 155 us  [local(): p3 = [lax.ppermute(x, 'col', with_near) for x in p2]]
    ppermute x1, waiting for transfers between devices: 79.8 us -> 173 us  [local(): near = lax.ppermute(a, 'col', with_near)]
    ppermute x3, waiting for transfers between devices: 79.2 us -> 0.01 us  [local(): lax.ppermute(b_own, 'row', [(p, (p - s) % side) for p in range(side)])]
    ppermute x11 -> x8, starting transfers between devices: 23.3 us -> 82.7 us  [local(): p5 = [lax.ppermute(x, 'col', with_near) for x in p4]]
    ppermute x4, waiting for transfers between devices: 62.5 us -> 34.5 us  [local(): p3 = [lax.ppermute(x, 'col', with_near) for x in p2]]
    ppermute x15 -> x12, starting transfers between devices: 35.8 us -> 63.8 us  [the longest x8 42.1 us: local(): lax.ppermute(near[o:o + s], 'col', inner)]
    ppermute x11 -> x8, waiting for transfers between devices: 124 us -> 103 us  [local(): p5 = [lax.ppermute(x, 'col', with_near) for x in p4]]
    unnamed x74 -> x32, local copies, waits for them, and re-layouts: 24.3 us -> 18.6 us
  transfers between devices with their start and end apart: 34 -> 28, of which waited for: 12 -> 6; matrix products, arithmetic and copies ran while one was open for 2% -> 1% of each run, Pallas kernels for 17% -> 12%
where the time goes in v5:
time: 740 us; the launch traced here: 733 us
  waiting for transfers between devices  311 us (42%)
  starting transfers between devices  303 us (41%)
  Pallas kernels  90.3 us (12%)
  local copies, waits for them, and re-layouts  28.2 us (4%)
    ppermute x1, waiting for transfers between devices, local(): near = lax.ppermute(a, 'col', with_near)  173 us
    ppermute x4, starting transfers between devices, local(): p3 = [lax.ppermute(x, 'col', with_near) for x in p2]  155 us
    ppermute x8, waiting for transfers between devices, local(): p5 = [lax.ppermute(x, 'col', with_near) for x in p4]  103 us
    ppermute x8, starting transfers between devices, local(): p5 = [lax.ppermute(x, 'col', with_near) for x in p4]  82.7 us
    pallas_call x4, Pallas kernels, _group_product(): pl.pallas_call(functools.partial(_mm_kernel, side), grid=(size // BM,), o...  73.1 us
    ppermute x8, starting transfers between devices, local(): lax.ppermute(near[o:o + s], 'col', inner)  42.1 us
    ppermute x4, waiting for transfers between devices, local(): p3 = [lax.ppermute(x, 'col', with_near) for x in p2]  34.5 us
    ppermute x4, starting transfers between devices, local(): lax.ppermute(a[h * step:(h + 1) * step], 'col', inner)  21.7 us
  transfers between devices with their start and end apart: 28, of which 6 were waited for; matrix products, arithmetic and copies ran while one was open for 1% of the time, Pallas kernels for 12%

profile of v5, /device:TPU:28, one launch (start us, length us, event | category | flops | bytes accessed | tf_op | source)
XLA Modules:
  0.0 732.6 jit_solution(14895059572489618737)
XLA Ops:
  0.5 1.2 collective-permute-start.4
  1.6 5.2 fusion.1
  6.8 2.2 collective-permute-start.6
  9.1 173.3 %collective-permute-done.near = bf16[8192,512]{1,0:T(8,128)(2,1)S(1)} collective-permute-done((bf16[8192,512]{1,0:T(8,128)(2,1)}, bf16[8192,512]{1,0:T(8,128)(2,1)S(1)}, u32[]{:S(2)}, u32[]{:S(2)}) %collective-permute-start) | collective-permute-done | bytes 8388640 | tf_op jit(solution)/shard_map/ppermute | solution.py:169
  182.4 17.9 %collective-permute-start.24 = (bf16[2048,512]{1,0:T(8,128)(2,1)}, bf16[2048,512]{1,0:T(8,128)(2,1)}, u32[]{:S(2)}, u32[]{:S(2)}) collective-permute-start(bf16[2048,512]{1,0:T(8,128)(2,1)} %get-tuple-element.8), channel_id=1, source_target_pairs={{0,0},{4,8},{8,4},{12,12},{1,1},{5,9},{9,5},{13,13},{2,2},{6,10},{... | collective-permute-start | bytes 6291464 | tf_op jit(solution)/shard_map/ppermute | solution.py:171
  200.3 2.4 fusion
  202.8 1.3 copy-done.10
  204.9 1.3 copy-done.12
  207.0 1.4 copy-done.14
  208.4 2.0 collective-permute-start.26
  210.5 17.2 %collective-permute-start.22 = (bf16[2048,512]{1,0:T(8,128)(2,1)}, bf16[2048,512]{1,0:T(8,128)(2,1)}, u32[]{:S(2)}, u32[]{:S(2)}) collective-permute-start(bf16[2048,512]{1,0:T(8,128)(2,1)} %get-tuple-element.6), channel_id=1, source_target_pairs={{0,0},{4,8},{8,4},{12,12},{1,1},{5,9},{9,5},{13,13},{2,2},{6,10},{... | collective-permute-start | bytes 6291464 | tf_op jit(solution)/shard_map/ppermute | solution.py:173
  227.7 50.7 %collective-permute-start.25 = (bf16[2048,512]{1,0:T(8,128)(2,1)}, bf16[2048,512]{1,0:T(8,128)(2,1)}, u32[]{:S(2)}, u32[]{:S(2)}) collective-permute-start(bf16[2048,512]{1,0:T(8,128)(2,1)} %collective-permute-done.24.p2), channel_id=1, source_target_pairs={{0,4},{4,0},{8,12},{12,8},{1,5},{5,1},{9,13},{13,9},{2,6},{6,2},{1... | collective-permute-start | bytes 6291464 | tf_op jit(solution)/shard_map/ppermute | solution.py:172
  278.4 17.3 %collective-permute-start.18 = (bf16[2048,512]{1,0:T(8,128)(2,1)}, bf16[2048,512]{1,0:T(8,128)(2,1)}, u32[]{:S(2)}, u32[]{:S(2)}) collective-permute-start(bf16[2048,512]{1,0:T(8,128)(2,1)} %get-tuple-element.7), channel_id=1, source_target_pairs={{0,0},{4,8},{8,4},{12,12},{1,1},{5,9},{9,5},{13,13},{2,2},{6,10},{... | collective-permute-start | bytes 6291464 | tf_op jit(solution)/shard_map/ppermute | solution.py:173
  295.7 72.7 %collective-permute-start.27 = (bf16[2048,512]{1,0:T(8,128)(2,1)}, bf16[2048,512]{1,0:T(8,128)(2,1)}, u32[]{:S(2)}, u32[]{:S(2)}) collective-permute-start(bf16[2048,512]{1,0:T(8,128)(2,1)} %collective-permute-done.26.p4), channel_id=1, source_target_pairs={{0,4},{4,0},{8,12},{12,8},{1,5},{5,1},{9,13},{13,9},{2,6},{6,2},{1... | collective-permute-start | bytes 6291464 | tf_op jit(solution)/shard_map/ppermute | solution.py:174
  368.4 1.4 copy-done.3
  372.8 1.7 collective-permute-start.12
  374.5 1.6 copy-done.5
  376.1 1.6 copy-done.11
  377.7 1.6 copy-done.13
  379.3 1.6 copy-done.15
  380.9 1.2 stack_blocks.1.b_ref
  382.1 2.2 copy-done.2
  386.3 3.4 copy-done
  389.6 1.3 early_product.5.early
  390.9 1.3 early_product.4.early
  392.5 102.0 %collective-permute-start.21 = (bf16[2048,512]{1,0:T(8,128)(2,1)S(1)}, bf16[2048,512]{1,0:T(8,128)(2,1)S(1)}, u32[]{:S(2)}, u32[]{:S(2)}) collective-permute-start(bf16[2048,512]{1,0:T(8,128)(2,1)S(1)} %copy-done.9), channel_id=1, source_target_pairs={{0,4},{4,0},{8,12},{12,8},{1,5},{5,1},{9,13},{13,9},{2,6},{6,2},{1... | collective-permute-start | bytes 6291464 | tf_op jit(solution)/shard_map/ppermute | solution.py:172
  494.5 2.3 early_product.6.early
  496.9 4.7 early_product.7.early
  501.6 2.1 collective-permute-start.17
  503.6 1.9 collective-permute-start.14
  505.5 1.9 collective-permute-start.19
  507.4 21.0 %group_product.4.rest_0_ = bf16[8192,2048]{1,0:T(8,128)(2,1)} custom-call(bf16[8192,512]{1,0:T(8,128)(2,1)S(1)} %copy-done, bf16[8192,512]{1,0:T(8,128)(2,1)S(1)} %copy-done.2, bf16[2048,512]{1,0:T(8,128)(2,1)} %collective-permute-done.24.p2, bf16[2048,512]{1,0:T(8,128)(2,1)} %collective-permute-done.25.p3, bf16[2048,512]{1,0:T(8,128)(2,1)} %collective-permute-done.26.p4, ...), custom_call_target="tpu_custom_call" | custom-call | flops 17179869184 | bytes 16777216 | tf_op jit(solution)/shard_map/group_product/pallas_call | solution.py:78
  528.4 12.5 %collective-permute-done.21.p3 = bf16[2048,512]{1,0:T(8,128)(2,1)S(1)} collective-permute-done((bf16[2048,512]{1,0:T(8,128)(2,1)S(1)}, bf16[2048,512]{1,0:T(8,128)(2,1)S(1)}, u32[]{:S(2)}, u32[]{:S(2)}) %collective-permute-start.21) | collective-permute-done | bytes 2097184 | tf_op jit(solution)/shard_map/ppermute | solution.py:172
  541.0 2.0 collective-permute-start.9
  543.0 43.0 %collective-permute-done.23.p5 = bf16[2048,512]{1,0:T(8,128)(2,1)} collective-permute-done((bf16[2048,512]{1,0:T(8,128)(2,1)}, bf16[2048,512]{1,0:T(8,128)(2,1)}, u32[]{:S(2)}, u32[]{:S(2)}) %collective-permute-start.23) | collective-permute-done | bytes 2097184 | tf_op jit(solution)/shard_map/ppermute | solution.py:174
  586.0 2.0 collective-permute-start.2
  588.0 20.8 %group_product.5.rest_0_ = bf16[8192,2048]{1,0:T(8,128)(2,1)} custom-call(bf16[8192,512]{1,0:T(8,128)(2,1)S(1)} %copy-done, bf16[8192,512]{1,0:T(8,128)(2,1)S(1)} %copy-done.2, bf16[2048,512]{1,0:T(8,128)(2,1)S(1)} %copy-done.9, bf16[2048,512]{1,0:T(8,128)(2,1)S(1)} %collective-permute-done.21.p3, ...), custom_call_target="tpu_custom_call", output_to_operand_aliasing={{}: (7, {})} | custom-call | flops 17179869184 | bytes 16777216 | tf_op jit(solution)/shard_map/group_product/pallas_call | solution.py:78
  608.9 22.0 %collective-permute-done.17.p3 = bf16[2048,512]{1,0:T(8,128)(2,1)S(1)} collective-permute-done((bf16[2048,512]{1,0:T(8,128)(2,1)S(1)}, bf16[2048,512]{1,0:T(8,128)(2,1)S(1)}, u32[]{:S(2)}, u32[]{:S(2)}) %collective-permute-start.17) | collective-permute-done | bytes 2097184 | tf_op jit(solution)/shard_map/ppermute | solution.py:172
  630.9 2.0 collective-permute-start.11
  632.9 43.0 %collective-permute-done.19.p5 = bf16[2048,512]{1,0:T(8,128)(2,1)} collective-permute-done((bf16[2048,512]{1,0:T(8,128)(2,1)}, bf16[2048,512]{1,0:T(8,128)(2,1)}, u32[]{:S(2)}, u32[]{:S(2)}) %collective-permute-start.19) | collective-permute-done | bytes 2097184 | tf_op jit(solution)/shard_map/ppermute | solution.py:174
  675.9 2.0 collective-permute-start.15
  677.9 20.9 %group_product.6.rest_0_ = bf16[8192,2048]{1,0:T(8,128)(2,1)} custom-call(bf16[8192,512]{1,0:T(8,128)(2,1)S(1)} %copy-done, bf16[8192,512]{1,0:T(8,128)(2,1)S(1)} %copy-done.2, bf16[2048,512]{1,0:T(8,128)(2,1)S(1)} %copy-done.7, bf16[2048,512]{1,0:T(8,128)(2,1)S(1)} %collective-permute-done.17.p3, ...), custom_call_target="tpu_custom_call", output_to_operand_aliasing={{}: (7, {})} | custom-call | flops 17179869184 | bytes 16777216 | tf_op jit(solution)/shard_map/group_product/pallas_call | solution.py:78
  698.8 16.9 %collective-permute-done.15.p5 = bf16[1024,512]{1,0:T(8,128)(2,1)S(1)} collective-permute-done((bf16[1024,512]{1,0:T(8,128)(2,1)S(1)}, bf16[1024,512]{1,0:T(8,128)(2,1)S(1)}, u32[]{:S(2)}, u32[]{:S(2)}) %collective-permute-start.15) | collective-permute-done | bytes 1048608 | tf_op jit(solution)/shard_map/ppermute | solution.py:174
  715.7 10.3 %group_product.7.c_in = bf16[8192,2048]{1,0:T(8,128)(2,1)} custom-call(bf16[8192,512]{1,0:T(8,128)(2,1)S(1)} %copy-done, bf16[8192,512]{1,0:T(8,128)(2,1)S(1)} %copy-done.2, bf16[2048,512]{1,0:T(8,128)(2,1)S(1)} %collective-permute-done.6.p2, bf16[2048,512]{1,0:T(8,128)(2,1)S(1)} %copy-done.4, ...), custom_call_target="tpu_custom_call", output_to_operand_aliasing={{}: (7, {})} | custom-call | flops 8589934592 | bytes 8388608 | tf_op jit(solution)/shard_map/group_product/pallas_call | solution.py:78
  726.0 2.4 late_product.4.c_in
  728.4 1.7 late_product.5.c_in
  730.1 1.2 late_product.6.c_in
  731.4 1.2 late_product.7
  (60 shorter events, 7.4 us)
Async XLA Ops:
  0.0 182.4 %collective-permute-start = (bf16[8192,512]{1,0:T(8,128)(2,1)}, bf16[8192,512]{1,0:T(8,128)(2,1)S(1)}, u32[]{:S(2)}, u32[]{:S(2)}) collective-permute-start(bf16[8192,512]{1,0:T(8,128)(2,1)} %own.15), channel_id=1, source_target_pairs={{0,4},{4,0},{8,12},{12,8},{1,5},{5,1},{9,13},{13,9},{2,6},{6,2},{1... | collective-permute-start | bytes 25165832 | tf_op jit(solution)/shard_map/ppermute | solution.py:169
  0.5 202.3 %collective-permute-start.3 = (bf16[512,2048]{1,0:T(8,128)(2,1)}, bf16[512,2048]{1,0:T(8,128)(2,1)S(1)}, u32[]{:S(2)}, u32[]{:S(2)}) collective-permute-start(bf16[512,2048]{1,0:T(8,128)(2,1)} %refs_0_.1), channel_id=1, source_target_pairs={{0,3},{1,0},{2,1},{3,2},{4,7},{5,4},{6,5},{7,6},{8,11},{9,8},{10,9... | collective-permute-start | bytes 6291464 | tf_op jit(solution)/shard_map/ppermute | solution.py:177
  0.5 204.4 %collective-permute-start.4 = (bf16[512,2048]{1,0:T(8,128)(2,1)}, bf16[512,2048]{1,0:T(8,128)(2,1)S(1)}, u32[]{:S(2)}, u32[]{:S(2)}) collective-permute-start(bf16[512,2048]{1,0:T(8,128)(2,1)} %refs_0_.1), channel_id=1, source_target_pairs={{0,2},{1,3},{2,0},{3,1},{4,6},{5,7},{6,4},{7,5},{8,10},{9,11},{10,... | collective-permute-start | bytes 6291464 | tf_op jit(solution)/shard_map/ppermute | solution.py:177
  1.6 205.4 %collective-permute-start.5 = (bf16[512,2048]{1,0:T(8,128)(2,1)}, bf16[512,2048]{1,0:T(8,128)(2,1)S(1)}, u32[]{:S(2)}, u32[]{:S(2)}) collective-permute-start(bf16[512,2048]{1,0:T(8,128)(2,1)} %refs_0_.1), channel_id=1, source_target_pairs={{0,1},{1,2},{2,3},{3,0},{4,5},{5,6},{6,7},{7,4},{8,9},{9,10},{10,1... | collective-permute-start | bytes 6291464 | tf_op jit(solution)/shard_map/ppermute | solution.py:177
  6.8 203.6 %collective-permute-start.6 = (bf16[2048,512]{1,0:T(8,128)(2,1)}, bf16[2048,512]{1,0:T(8,128)(2,1)S(1)}, u32[]{:S(2)}, u32[]{:S(2)}) collective-permute-start(bf16[2048,512]{1,0:T(8,128)(2,1)} %get-tuple-element.11), channel_id=1, source_target_pairs={{0,0},{4,8},{8,4},{12,12},{1,1},{5,9},{9,5},{13,13},{2,2},{6,10},{... | collective-permute-start | bytes 6291464 | tf_op jit(solution)/shard_map/ppermute | solution.py:171
  182.4 189.5 %copy-start.1 = (bf16[8192,512]{1,0:T(8,128)(2,1)}, bf16[8192,512]{1,0:T(8,128)(2,1)S(1)}, u32[]{:S(2)}) copy-start(bf16[8192,512]{1,0:T(8,128)(2,1)S(1)} %collective-permute-done.near) | copy-start | bytes 25165828
  182.4 28.0 %collective-permute-start.24 = (bf16[2048,512]{1,0:T(8,128)(2,1)}, bf16[2048,512]{1,0:T(8,128)(2,1)}, u32[]{:S(2)}, u32[]{:S(2)}) collective-permute-start(bf16[2048,512]{1,0:T(8,128)(2,1)} %get-tuple-element.8), channel_id=1, source_target_pairs={{0,0},{4,8},{8,4},{12,12},{1,1},{5,9},{9,5},{13,13},{2,2},{6,10},{... | collective-permute-start | bytes 6291464 | tf_op jit(solution)/shard_map/ppermute | solution.py:171
  202.8 1.3 copy-start.10
  204.1 23.6 %collective-permute-start.20 = (bf16[2048,512]{1,0:T(8,128)(2,1)S(1)}, bf16[2048,512]{1,0:T(8,128)(2,1)S(1)}, u32[]{:S(2)}, u32[]{:S(2)}) collective-permute-start(bf16[2048,512]{1,0:T(8,128)(2,1)S(1)} %get-tuple-element.9), channel_id=1, source_target_pairs={{0,0},{4,8},{8,4},{12,12},{1,1},{5,9},{9,5},{13,13},{2,2},{6,10},{... | collective-permute-start | bytes 6291464 | tf_op jit(solution)/shard_map/ppermute | solution.py:171
  204.9 1.3 copy-start.12
  206.2 72.2 %collective-permute-start.16 = (bf16[2048,512]{1,0:T(8,128)(2,1)S(1)}, bf16[2048,512]{1,0:T(8,128)(2,1)S(1)}, u32[]{:S(2)}, u32[]{:S(2)}) collective-permute-start(bf16[2048,512]{1,0:T(8,128)(2,1)S(1)} %get-tuple-element.10), channel_id=1, source_target_pairs={{0,0},{4,8},{8,4},{12,12},{1,1},{5,9},{9,5},{13,13},{2,2},{6,10},{... | collective-permute-start | bytes 6291464 | tf_op jit(solution)/shard_map/ppermute | solution.py:171
  207.0 1.4 copy-start.14
  208.4 87.3 %collective-permute-start.26 = (bf16[2048,512]{1,0:T(8,128)(2,1)S(1)}, bf16[2048,512]{1,0:T(8,128)(2,1)}, u32[]{:S(2)}, u32[]{:S(2)}) collective-permute-start(bf16[2048,512]{1,0:T(8,128)(2,1)S(1)} %get-tuple-element.5), channel_id=1, source_target_pairs={{0,0},{4,8},{8,4},{12,12},{1,1},{5,9},{9,5},{13,13},{2,2},{6,10},{... | collective-permute-start | bytes 6291464 | tf_op jit(solution)/shard_map/ppermute | solution.py:173
  210.4 158.0 %collective-permute-start.7 = (bf16[2048,512]{1,0:T(8,128)(2,1)S(1)}, bf16[2048,512]{1,0:T(8,128)(2,1)S(1)}, u32[]{:S(2)}, u32[]{:S(2)}) collective-permute-start(bf16[2048,512]{1,0:T(8,128)(2,1)S(1)} %collective-permute-done.6.p2), channel_id=1, source_target_pairs={{0,4},{4,0},{8,12},{12,8},{1,5},{5,1},{9,13},{13,9},{2,6},{6,2},{1... | collective-permute-start | bytes 6291464 | tf_op jit(solution)/shard_map/ppermute | solution.py:172
  210.5 284.0 %collective-permute-start.22 = (bf16[2048,512]{1,0:T(8,128)(2,1)}, bf16[2048,512]{1,0:T(8,128)(2,1)}, u32[]{:S(2)}, u32[]{:S(2)}) collective-permute-start(bf16[2048,512]{1,0:T(8,128)(2,1)} %get-tuple-element.6), channel_id=1, source_target_pairs={{0,0},{4,8},{8,4},{12,12},{1,1},{5,9},{9,5},{13,13},{2,2},{6,10},{... | collective-permute-start | bytes 6291464 | tf_op jit(solution)/shard_map/ppermute | solution.py:173
  227.7 145.1 %copy-start.8 = (bf16[2048,512]{1,0:T(8,128)(2,1)}, bf16[2048,512]{1,0:T(8,128)(2,1)S(1)}, u32[]{:S(2)}) copy-start(bf16[2048,512]{1,0:T(8,128)(2,1)S(1)} %collective-permute-done.20.p2) | copy-start | bytes 6291460
  227.7 273.9 %collective-permute-start.25 = (bf16[2048,512]{1,0:T(8,128)(2,1)}, bf16[2048,512]{1,0:T(8,128)(2,1)}, u32[]{:S(2)}, u32[]{:S(2)}) collective-permute-start(bf16[2048,512]{1,0:T(8,128)(2,1)} %collective-permute-done.24.p2), channel_id=1, source_target_pairs={{0,4},{4,0},{8,12},{12,8},{1,5},{5,1},{9,13},{13,9},{2,6},{6,2},{1... | collective-permute-start | bytes 6291464 | tf_op jit(solution)/shard_map/ppermute | solution.py:172
  278.4 94.4 %copy-start.6 = (bf16[2048,512]{1,0:T(8,128)(2,1)}, bf16[2048,512]{1,0:T(8,128)(2,1)S(1)}, u32[]{:S(2)}) copy-start(bf16[2048,512]{1,0:T(8,128)(2,1)S(1)} %collective-permute-done.16.p2) | copy-start | bytes 6291460
  278.4 225.2 %collective-permute-start.18 = (bf16[2048,512]{1,0:T(8,128)(2,1)}, bf16[2048,512]{1,0:T(8,128)(2,1)}, u32[]{:S(2)}, u32[]{:S(2)}) collective-permute-start(bf16[2048,512]{1,0:T(8,128)(2,1)} %get-tuple-element.7), channel_id=1, source_target_pairs={{0,0},{4,8},{8,4},{12,12},{1,1},{5,9},{9,5},{13,13},{2,2},{6,10},{... | collective-permute-start | bytes 6291464 | tf_op jit(solution)/shard_map/ppermute | solution.py:173
  295.7 209.8 %collective-permute-start.27 = (bf16[2048,512]{1,0:T(8,128)(2,1)}, bf16[2048,512]{1,0:T(8,128)(2,1)}, u32[]{:S(2)}, u32[]{:S(2)}) collective-permute-start(bf16[2048,512]{1,0:T(8,128)(2,1)} %collective-permute-done.26.p4), channel_id=1, source_target_pairs={{0,4},{4,0},{8,12},{12,8},{1,5},{5,1},{9,13},{13,9},{2,6},{6,2},{1... | collective-permute-start | bytes 6291464 | tf_op jit(solution)/shard_map/ppermute | solution.py:174
  368.4 1.4 copy-start.3
  369.8 0.7 collective-permute-start.8
  370.5 0.7 collective-permute-start.1
  371.2 1.5 collective-permute-start.10
  372.8 19.4 %collective-permute-start.12 = (bf16[512,512]{1,0:T(8,128)(2,1)}, bf16[512,512]{1,0:T(8,128)(2,1)S(1)}, u32[]{:S(2)}, u32[]{:S(2)}) collective-permute-start(bf16[512,512]{1,0:T(8,128)(2,1)} %slice.51), channel_id=1, source_target_pairs={{0,0},{4,8},{8,4},{12,12},{1,1},{5,9},{9,5},{13,13},{2,2},{6,10},{... | collective-permute-start | bytes 1572872 | tf_op jit(solution)/shard_map/ppermute | solution.py:173
  374.5 1.6 copy-start.5
  376.1 1.6 copy-start.11
  377.7 1.6 copy-start.13
  379.3 1.6 copy-start.15
  380.9 3.4 copy-start.2
  384.3 2.0 copy-start.4
  386.3 3.4 copy-start
  390.9 1.6 copy-start.9
  392.5 148.5 %collective-permute-start.21 = (bf16[2048,512]{1,0:T(8,128)(2,1)S(1)}, bf16[2048,512]{1,0:T(8,128)(2,1)S(1)}, u32[]{:S(2)}, u32[]{:S(2)}) collective-permute-start(bf16[2048,512]{1,0:T(8,128)(2,1)S(1)} %copy-done.9), channel_id=1, source_target_pairs={{0,4},{4,0},{8,12},{12,8},{1,5},{5,1},{9,13},{13,9},{2,6},{6,2},{1... | collective-permute-start | bytes 6291464 | tf_op jit(solution)/shard_map/ppermute | solution.py:172
  494.5 91.5 %collective-permute-start.23 = (bf16[2048,512]{1,0:T(8,128)(2,1)}, bf16[2048,512]{1,0:T(8,128)(2,1)}, u32[]{:S(2)}, u32[]{:S(2)}) collective-permute-start(bf16[2048,512]{1,0:T(8,128)(2,1)} %collective-permute-done.22.p4), channel_id=1, source_target_pairs={{0,4},{4,0},{8,12},{12,8},{1,5},{5,1},{9,13},{13,9},{2,6},{6,2},{1... | collective-permute-start | bytes 6291464 | tf_op jit(solution)/shard_map/ppermute | solution.py:174
  496.8 4.7 copy-start.7
  501.6 129.3 %collective-permute-start.17 = (bf16[2048,512]{1,0:T(8,128)(2,1)S(1)}, bf16[2048,512]{1,0:T(8,128)(2,1)S(1)}, u32[]{:S(2)}, u32[]{:S(2)}) collective-permute-start(bf16[2048,512]{1,0:T(8,128)(2,1)S(1)} %copy-done.7), channel_id=1, source_target_pairs={{0,4},{4,0},{8,12},{12,8},{1,5},{5,1},{9,13},{13,9},{2,6},{6,2},{1... | collective-permute-start | bytes 6291464 | tf_op jit(solution)/shard_map/ppermute | solution.py:172
  503.6 129.2 %collective-permute-start.14 = (bf16[1024,512]{1,0:T(8,128)(2,1)}, bf16[1024,512]{1,0:T(8,128)(2,1)S(1)}, u32[]{:S(2)}, u32[]{:S(2)}) collective-permute-start(bf16[1024,512]{1,0:T(8,128)(2,1)} %slice.52), channel_id=1, source_target_pairs={{0,0},{4,8},{8,4},{12,12},{1,1},{5,9},{9,5},{13,13},{2,2},{6,10},{... | collective-permute-start | bytes 3145736 | tf_op jit(solution)/shard_map/ppermute | solution.py:173
  505.5 170.4 %collective-permute-start.19 = (bf16[2048,512]{1,0:T(8,128)(2,1)}, bf16[2048,512]{1,0:T(8,128)(2,1)}, u32[]{:S(2)}, u32[]{:S(2)}) collective-permute-start(bf16[2048,512]{1,0:T(8,128)(2,1)} %collective-permute-done.18.p4), channel_id=1, source_target_pairs={{0,4},{4,0},{8,12},{12,8},{1,5},{5,1},{9,13},{13,9},{2,6},{6,2},{1... | collective-permute-start | bytes 6291464 | tf_op jit(solution)/shard_map/ppermute | solution.py:174
  541.0 189.2 %collective-permute-start.9 = (bf16[128,512]{1,0:T(8,128)(2,1)S(1)}, bf16[128,512]{1,0:T(8,128)(2,1)S(1)}, u32[]{:S(2)}, u32[]{:S(2)}) collective-permute-start(bf16[128,512]{1,0:T(8,128)(2,1)S(1)} %collective-permute-done.8.p4), channel_id=1, source_target_pairs={{0,4},{4,0},{8,12},{12,8},{1,5},{5,1},{9,13},{13,9},{2,6},{6,2},{1... | collective-permute-start | bytes 393224 | tf_op jit(solution)/shard_map/ppermute | solution.py:174
  586.0 145.4 %collective-permute-start.2 = (bf16[128,512]{1,0:T(8,128)(2,1)S(1)}, bf16[128,512]{1,0:T(8,128)(2,1)S(1)}, u32[]{:S(2)}, u32[]{:S(2)}) collective-permute-start(bf16[128,512]{1,0:T(8,128)(2,1)S(1)} %collective-permute-done.1.p4), channel_id=1, source_target_pairs={{0,4},{4,0},{8,12},{12,8},{1,5},{5,1},{9,13},{13,9},{2,6},{6,2},{1... | collective-permute-start | bytes 393224 | tf_op jit(solution)/shard_map/ppermute | solution.py:174
  630.9 97.6 %collective-permute-start.11 = (bf16[256,512]{1,0:T(8,128)(2,1)S(1)}, bf16[256,512]{1,0:T(8,128)(2,1)S(1)}, u32[]{:S(2)}, u32[]{:S(2)}) collective-permute-start(bf16[256,512]{1,0:T(8,128)(2,1)S(1)} %collective-permute-done.10.p4), channel_id=1, source_target_pairs={{0,4},{4,0},{8,12},{12,8},{1,5},{5,1},{9,13},{13,9},{2,6},{6,2},{1... | collective-permute-start | bytes 786440 | tf_op jit(solution)/shard_map/ppermute | solution.py:174
  632.9 93.1 %collective-permute-start.13 = (bf16[512,512]{1,0:T(8,128)(2,1)S(1)}, bf16[512,512]{1,0:T(8,128)(2,1)S(1)}, u32[]{:S(2)}, u32[]{:S(2)}) collective-permute-start(bf16[512,512]{1,0:T(8,128)(2,1)S(1)} %collective-permute-done.12.p4), channel_id=1, source_target_pairs={{0,4},{4,0},{8,12},{12,8},{1,5},{5,1},{9,13},{13,9},{2,6},{6,2},{1... | collective-permute-start | bytes 1572872 | tf_op jit(solution)/shard_map/ppermute | solution.py:174
  675.9 39.8 %collective-permute-start.15 = (bf16[1024,512]{1,0:T(8,128)(2,1)S(1)}, bf16[1024,512]{1,0:T(8,128)(2,1)S(1)}, u32[]{:S(2)}, u32[]{:S(2)}) collective-permute-start(bf16[1024,512]{1,0:T(8,128)(2,1)S(1)} %collective-permute-done.14.p4), channel_id=1, source_target_pairs={{0,4},{4,0},{8,12},{12,8},{1,5},{5,1},{9,13},{13,9},{2,6},{6,2},{1... | collective-permute-start | bytes 3145736 | tf_op jit(solution)/shard_map/ppermute | solution.py:174

commit v6 on v5

--- a/solution.py
+++ b/solution.py
@@ -9,10 +9,9 @@
 
 
 HALVES = 4
-GROUPS = (2048, 2048, 2048, 1024)
-TAIL = (512, 256, 128, 128)
+GROUPS = (1024, 1024, 1024, 1024, 1024, 1024, 1024)
+TAIL = (512, 384, 128)
 BM = 256
-LATE_STEPS = 1
 
 
 def _at_end(side):
@@ -91,7 +90,7 @@
 def _early_product(side, own, near, p2, p3, p4, b, off, size):
     depth = own.shape[1]
     total, cols = b.shape
-    bm = min(BM, size)
+    bm = BM if size % BM == 0 else BM // 2
     full = _rows(bm, depth, off)
     chunk = _rows(bm, depth, off % p3.shape[0])
     piece = _rows(bm, depth, 0)
@@ -110,7 +109,7 @@
 def _late_product(side, p5, b, early, c, off, size):
     depth = p5.shape[1]
     rows, cols = c.shape
-    bm = min(BM, size) // LATE_STEPS
+    bm = BM if size % BM == 0 else BM // 2
     return pl.pallas_call(
         functools.partial(_late_kernel, side),
         grid=(size // bm,),

time: 740 us -> 563 us (0.76)
  starting transfers between devices: 303 us -> 67.4 us
  waiting for transfers between devices: 311 us -> 369 us
    ppermute x4, starting transfers between devices: 155 us -> 2.54 us  [local(): p3 = [lax.ppermute(x, 'col', with_near) for x in p2]]
    ppermute x1, waiting for transfers between devices: 173 us -> 73.8 us  [local(): near = lax.ppermute(a, 'col', with_near)]
    ppermute x3, waiting for transfers between devices: 0.01 us -> 79.2 us  [local(): lax.ppermute(b_own, 'row', [(p, (p - s) % side) for p in range(side)])]
    ppermute x8 -> x10, starting transfers between devices: 82.7 us -> 14.6 us  [local(): p5 = [lax.ppermute(x, 'col', with_near) for x in p4]]
    ppermute x4, waiting for transfers between devices: 34.5 us -> 79.9 us  [local(): p3 = [lax.ppermute(x, 'col', with_near) for x in p2]]
    ppermute x8 -> x10, waiting for transfers between devices: 103 us -> 136 us  [local(): p5 = [lax.ppermute(x, 'col', with_near) for x in p4]]
    ppermute x8 -> x10, starting transfers between devices: 42.1 us -> 26.2 us  [local(): lax.ppermute(near[o:o + s], 'col', inner)]
    unnamed x32 -> x42, local copies, waits for them, and re-layouts: 18.6 us -> 16 us
  transfers between devices with their start and end apart: 28 -> 32, of which waited for: 6 -> 12; matrix products, arithmetic and copies ran while one was open for 1% -> 2% of each run, Pallas kernels for 12% -> 17%
where the time goes in v6:
time: 563 us; the launch traced here: 559 us
  waiting for transfers between devices  369 us (66%)
  Pallas kernels  97.3 us (17%)
  starting transfers between devices  67.4 us (12%)
  local copies, waits for them, and re-layouts  25.1 us (4%)
    ppermute x10, waiting for transfers between devices, local(): p5 = [lax.ppermute(x, 'col', with_near) for x in p4]  136 us
    ppermute x4, waiting for transfers between devices, local(): p3 = [lax.ppermute(x, 'col', with_near) for x in p2]  79.9 us
    ppermute x3, waiting for transfers between devices, local(): lax.ppermute(b_own, 'row', [(p, (p - s) % side) for p in range(side)])  79.2 us
    pallas_call x7, Pallas kernels, _group_product(): pl.pallas_call(functools.partial(_mm_kernel, side), grid=(size // BM,), o...  75.6 us
    ppermute x1, waiting for transfers between devices, local(): near = lax.ppermute(a, 'col', with_near)  73.8 us
    ppermute x10, starting transfers between devices, local(): lax.ppermute(near[o:o + s], 'col', inner)  26.2 us
    ppermute x4, starting transfers between devices, local(): lax.ppermute(a[h * step:(h + 1) * step], 'col', inner)  21.1 us
    unnamed x42, local copies, waits for them, and re-layouts  16 us
  transfers between devices with their start and end apart: 32, of which 12 were waited for; matrix products, arithmetic and copies ran while one was open for 2% of the time, Pallas kernels for 17%

profile of v6, /device:TPU:28, one launch (start us, length us, event | category | flops | bytes accessed | tf_op | source)
XLA Modules:
  0.0 559.3 jit_solution(12628586032255438442)
XLA Ops:
  1.6 5.1 fusion.1
  8.3 38.4 %collective-permute-done.3.refs_1_ = bf16[512,2048]{1,0:T(8,128)(2,1)S(1)} collective-permute-done((bf16[512,2048]{1,0:T(8,128)(2,1)}, bf16[512,2048]{1,0:T(8,128)(2,1)S(1)}, u32[]{:S(2)}, u32[]{:S(2)}) %collective-permute-start.3) | collective-permute-done | bytes 2097184 | tf_op jit(solution)/shard_map/ppermute | solution.py:176
  46.7 1.3 copy-done.13
  48.1 1.3 collective-permute-start.5
  49.4 40.8 %collective-permute-done.4.refs_2_ = bf16[512,2048]{1,0:T(8,128)(2,1)S(1)} collective-permute-done((bf16[512,2048]{1,0:T(8,128)(2,1)}, bf16[512,2048]{1,0:T(8,128)(2,1)S(1)}, u32[]{:S(2)}, u32[]{:S(2)}) %collective-permute-start.4) | collective-permute-done | bytes 2097184 | tf_op jit(solution)/shard_map/ppermute | solution.py:176
  90.2 17.2 %collective-permute-start.20 = (bf16[2048,512]{1,0:T(8,128)(2,1)}, bf16[2048,512]{1,0:T(8,128)(2,1)}, u32[]{:S(2)}, u32[]{:S(2)}) collective-permute-start(bf16[2048,512]{1,0:T(8,128)(2,1)} %get-tuple-element.13), channel_id=1, source_target_pairs={{0,0},{4,8},{8,4},{12,12},{1,1},{5,9},{9,5},{13,13},{2,2},{6,10},{... | collective-permute-start | bytes 6291464 | tf_op jit(solution)/shard_map/ppermute | solution.py:170
  107.4 2.3 collective-permute-start.14
  109.8 73.8 %collective-permute-done.near = bf16[8192,512]{1,0:T(8,128)(2,1)S(1)} collective-permute-done((bf16[8192,512]{1,0:T(8,128)(2,1)}, bf16[8192,512]{1,0:T(8,128)(2,1)S(1)}, u32[]{:S(2)}, u32[]{:S(2)}) %collective-permute-start) | collective-permute-done | bytes 8388640 | tf_op jit(solution)/shard_map/ppermute | solution.py:168
  184.0 3.1 fusion
  187.1 2.0 collective-permute-start.30
  189.2 1.9 collective-permute-start.28
  191.8 36.7 %collective-permute-done.27.p3 = bf16[2048,512]{1,0:T(8,128)(2,1)S(1)} collective-permute-done((bf16[2048,512]{1,0:T(8,128)(2,1)S(1)}, bf16[2048,512]{1,0:T(8,128)(2,1)S(1)}, u32[]{:S(2)}, u32[]{:S(2)}) %collective-permute-start.27) | collective-permute-done | bytes 2097184 | tf_op jit(solution)/shard_map/ppermute | solution.py:171
  228.5 1.3 copy-done.9
  230.3 43.2 %collective-permute-done.7.p3 = bf16[2048,512]{1,0:T(8,128)(2,1)S(1)} collective-permute-done((bf16[2048,512]{1,0:T(8,128)(2,1)S(1)}, bf16[2048,512]{1,0:T(8,128)(2,1)S(1)}, u32[]{:S(2)}, u32[]{:S(2)}) %collective-permute-start.7) | collective-permute-done | bytes 2097184 | tf_op jit(solution)/shard_map/ppermute | solution.py:171
  273.4 1.3 copy-done.3
  276.1 9.5 %collective-permute-start.24 = (bf16[1024,512]{1,0:T(8,128)(2,1)}, bf16[1024,512]{1,0:T(8,128)(2,1)}, u32[]{:S(2)}, u32[]{:S(2)}) collective-permute-start(bf16[1024,512]{1,0:T(8,128)(2,1)} %get-tuple-element.7), channel_id=1, source_target_pairs={{0,0},{4,8},{8,4},{12,12},{1,1},{5,9},{9,5},{13,13},{2,2},{6,10},{... | collective-permute-start | bytes 3145736 | tf_op jit(solution)/shard_map/ppermute | solution.py:172
  286.5 5.4 collective-permute-start.10
  291.9 1.6 copy-done.12
  293.5 1.6 copy-done.14
  295.1 1.6 copy-done.16
  296.7 3.0 stack_blocks.1.b_ref
  301.3 3.4 copy-done
  304.7 2.2 early_product.3.early
  306.9 3.8 early_product.4.early
  311.6 8.8 %collective-permute-start.29 = (bf16[1024,512]{1,0:T(8,128)(2,1)S(1)}, bf16[1024,512]{1,0:T(8,128)(2,1)S(1)}, u32[]{:S(2)}, u32[]{:S(2)}) collective-permute-start(bf16[1024,512]{1,0:T(8,128)(2,1)S(1)} %collective-permute-done.28.p4), channel_id=1, source_target_pairs={{0,4},{4,0},{8,12},{12,8},{1,5},{5,1},{9,13},{13,9},{2,6},{6,2},{1... | collective-permute-start | bytes 3145736 | tf_op jit(solution)/shard_map/ppermute | solution.py:173
  320.4 5.6 %early_product.5.early = f32[512,2048]{1,0:T(8,128)S(1)} custom-call(bf16[8192,512]{1,0:T(8,128)(2,1)S(1)} %copy-done, bf16[8192,512]{1,0:T(8,128)(2,1)S(1)} %copy-done.2, bf16[2048,512]{1,0:T(8,128)(2,1)S(1)} %collective-permute-done.6.p2, bf16[2048,512]{1,0:T(8,128)(2,1)S(1)} %copy-done.4, bf16[512,512]{1,0:T(8,128)(2,1)} %collective-permute-done.10.p4, ...), custom_call_target="tpu_custom_call" | custom-call | flops 4294967296 | bytes 4194304 | tf_op jit(solution)/shard_map/early_product/pallas_call | solution.py:97
  326.9 14.0 %collective-permute-done.31.p5 = bf16[1024,512]{1,0:T(8,128)(2,1)} collective-permute-done((bf16[1024,512]{1,0:T(8,128)(2,1)}, bf16[1024,512]{1,0:T(8,128)(2,1)}, u32[]{:S(2)}, u32[]{:S(2)}) %collective-permute-start.31) | collective-permute-done | bytes 1048608 | tf_op jit(solution)/shard_map/ppermute | solution.py:173
  341.4 11.4 %group_product.7.rest_0_ = bf16[8192,2048]{1,0:T(8,128)(2,1)} custom-call(bf16[8192,512]{1,0:T(8,128)(2,1)S(1)} %copy-done, bf16[8192,512]{1,0:T(8,128)(2,1)S(1)} %copy-done.2, bf16[2048,512]{1,0:T(8,128)(2,1)S(1)} %copy-done.8, bf16[2048,512]{1,0:T(8,128)(2,1)S(1)} %copy-done.10, bf16[1024,512]{1,0:T(8,128)(2,1)} %collective-permute-done.30.p4, ...), custom_call_target="tpu_custom_call" | custom-call | flops 8589934592 | bytes 8388608 | tf_op jit(solution)/shard_map/group_product/pallas_call | solution.py:77
  352.8 1.6 collective-permute-start.15
  354.4 1.9 collective-permute-start.16
  356.3 7.0 %collective-permute-done.29.p5 = bf16[1024,512]{1,0:T(8,128)(2,1)S(1)} collective-permute-done((bf16[1024,512]{1,0:T(8,128)(2,1)S(1)}, bf16[1024,512]{1,0:T(8,128)(2,1)S(1)}, u32[]{:S(2)}, u32[]{:S(2)}) %collective-permute-start.29) | collective-permute-done | bytes 1048608 | tf_op jit(solution)/shard_map/ppermute | solution.py:173
  363.8 10.3 %group_product.8.rest_0_ = bf16[8192,2048]{1,0:T(8,128)(2,1)} custom-call(bf16[8192,512]{1,0:T(8,128)(2,1)S(1)} %copy-done, bf16[8192,512]{1,0:T(8,128)(2,1)S(1)} %copy-done.2, bf16[2048,512]{1,0:T(8,128)(2,1)S(1)} %copy-done.8, bf16[2048,512]{1,0:T(8,128)(2,1)S(1)} %copy-done.10, ...), custom_call_target="tpu_custom_call", output_to_operand_aliasing={{}: (7, {})} | custom-call | flops 8589934592 | bytes 8388608 | tf_op jit(solution)/shard_map/group_product/pallas_call | solution.py:77
  374.1 1.9 collective-permute-start.12
  376.0 9.8 %collective-permute-done.25.p5 = bf16[1024,512]{1,0:T(8,128)(2,1)S(1)} collective-permute-done((bf16[1024,512]{1,0:T(8,128)(2,1)}, bf16[1024,512]{1,0:T(8,128)(2,1)S(1)}, u32[]{:S(2)}, u32[]{:S(2)}) %collective-permute-start.25) | collective-permute-done | bytes 1048608 | tf_op jit(solution)/shard_map/ppermute | solution.py:173
  388.4 11.5 %group_product.9.rest_0_ = bf16[8192,2048]{1,0:T(8,128)(2,1)} custom-call(bf16[8192,512]{1,0:T(8,128)(2,1)S(1)} %copy-done, bf16[8192,512]{1,0:T(8,128)(2,1)S(1)} %copy-done.2, bf16[2048,512]{1,0:T(8,128)(2,1)} %collective-permute-done.20.p2, bf16[2048,512]{1,0:T(8,128)(2,1)} %collective-permute-done.21.p3, ...), custom_call_target="tpu_custom_call", output_to_operand_aliasing={{}: (7, {})} | custom-call | flops 8589934592 | bytes 8388608 | tf_op jit(solution)/shard_map/group_product/pallas_call | solution.py:77
  399.9 1.6 collective-permute-start.2
  401.5 51.7 %collective-permute-done.23.p5 = bf16[1024,512]{1,0:T(8,128)(2,1)S(1)} collective-permute-done((bf16[1024,512]{1,0:T(8,128)(2,1)S(1)}, bf16[1024,512]{1,0:T(8,128)(2,1)S(1)}, u32[]{:S(2)}, u32[]{:S(2)}) %collective-permute-start.23) | collective-permute-done | bytes 1048608 | tf_op jit(solution)/shard_map/ppermute | solution.py:173
  453.6 11.4 %group_product.10.rest_0_ = bf16[8192,2048]{1,0:T(8,128)(2,1)} custom-call(bf16[8192,512]{1,0:T(8,128)(2,1)S(1)} %copy-done, bf16[8192,512]{1,0:T(8,128)(2,1)S(1)} %copy-done.2, bf16[2048,512]{1,0:T(8,128)(2,1)} %collective-permute-done.20.p2, bf16[2048,512]{1,0:T(8,128)(2,1)} %collective-permute-done.21.p3, ...), custom_call_target="tpu_custom_call", output_to_operand_aliasing={{}: (7, {})} | custom-call | flops 8589934592 | bytes 8388608 | tf_op jit(solution)/shard_map/group_product/pallas_call | solution.py:77
  465.1 1.6 collective-permute-start.9
  467.1 8.6 %collective-permute-done.19.p5 = bf16[1024,512]{1,0:T(8,128)(2,1)S(1)} collective-permute-done((bf16[1024,512]{1,0:T(8,128)(2,1)S(1)}, bf16[1024,512]{1,0:T(8,128)(2,1)S(1)}, u32[]{:S(2)}, u32[]{:S(2)}) %collective-permute-start.19) | collective-permute-done | bytes 1048608 | tf_op jit(solution)/shard_map/ppermute | solution.py:173
  476.1 10.3 %group_product.11.rest_0_ = bf16[8192,2048]{1,0:T(8,128)(2,1)} custom-call(bf16[8192,512]{1,0:T(8,128)(2,1)S(1)} %copy-done, bf16[8192,512]{1,0:T(8,128)(2,1)S(1)} %copy-done.2, bf16[2048,512]{1,0:T(8,128)(2,1)S(1)} %copy-done.6, bf16[2048,512]{1,0:T(8,128)(2,1)S(1)} %collective-permute-done.15.p3, ...), custom_call_target="tpu_custom_call", output_to_operand_aliasing={{}: (7, {})} | custom-call | flops 8589934592 | bytes 8388608 | tf_op jit(solution)/shard_map/group_product/pallas_call | solution.py:77
  486.4 14.5 %collective-permute-done.17.p5 = bf16[1024,512]{1,0:T(8,128)(2,1)S(1)} collective-permute-done((bf16[1024,512]{1,0:T(8,128)(2,1)S(1)}, bf16[1024,512]{1,0:T(8,128)(2,1)S(1)}, u32[]{:S(2)}, u32[]{:S(2)}) %collective-permute-start.17) | collective-permute-done | bytes 1048608 | tf_op jit(solution)/shard_map/ppermute | solution.py:173
  500.9 10.3 %group_product.12.rest_0_ = bf16[8192,2048]{1,0:T(8,128)(2,1)} custom-call(bf16[8192,512]{1,0:T(8,128)(2,1)S(1)} %copy-done, bf16[8192,512]{1,0:T(8,128)(2,1)S(1)} %copy-done.2, bf16[2048,512]{1,0:T(8,128)(2,1)S(1)} %copy-done.6, bf16[2048,512]{1,0:T(8,128)(2,1)S(1)} %collective-permute-done.15.p3, ...), custom_call_target="tpu_custom_call", output_to_operand_aliasing={{}: (7, {})} | custom-call | flops 8589934592 | bytes 8388608 | tf_op jit(solution)/shard_map/group_product/pallas_call | solution.py:77
  511.3 30.7 %collective-permute-done.13.p5 = bf16[1024,512]{1,0:T(8,128)(2,1)S(1)} collective-permute-done((bf16[1024,512]{1,0:T(8,128)(2,1)S(1)}, bf16[1024,512]{1,0:T(8,128)(2,1)S(1)}, u32[]{:S(2)}, u32[]{:S(2)}) %collective-permute-start.13) | collective-permute-done | bytes 1048608 | tf_op jit(solution)/shard_map/ppermute | solution.py:173
  541.9 10.3 %group_product.13.c_in = bf16[8192,2048]{1,0:T(8,128)(2,1)} custom-call(bf16[8192,512]{1,0:T(8,128)(2,1)S(1)} %copy-done, bf16[8192,512]{1,0:T(8,128)(2,1)S(1)} %copy-done.2, bf16[2048,512]{1,0:T(8,128)(2,1)S(1)} %collective-permute-done.6.p2, bf16[2048,512]{1,0:T(8,128)(2,1)S(1)} %copy-done.4, ...), custom_call_target="tpu_custom_call", output_to_operand_aliasing={{}: (7, {})} | custom-call | flops 8589934592 | bytes 8388608 | tf_op jit(solution)/shard_map/group_product/pallas_call | solution.py:77
  552.3 2.4 late_product.3.c_in
  554.7 2.5 late_product.4.c_in
  557.2 2.1 late_product.5
  (78 shorter events, 15.4 us)
Async XLA Ops:
  0.0 48.1 %copy-start.11 = (bf16[512,2048]{1,0:T(8,128)(2,1)S(1)}, bf16[512,2048]{1,0:T(8,128)(2,1)}, u32[]{:S(2)}) copy-start(bf16[512,2048]{1,0:T(8,128)(2,1)} %refs_0_.1) | copy-start | bytes 6291460
  0.0 183.5 %collective-permute-start = (bf16[8192,512]{1,0:T(8,128)(2,1)}, bf16[8192,512]{1,0:T(8,128)(2,1)S(1)}, u32[]{:S(2)}, u32[]{:S(2)}) collective-permute-start(bf16[8192,512]{1,0:T(8,128)(2,1)} %own.19), channel_id=1, source_target_pairs={{0,4},{4,0},{8,12},{12,8},{1,5},{5,1},{9,13},{13,9},{2,6},{6,2},{1... | collective-permute-start | bytes 25165832 | tf_op jit(solution)/shard_map/ppermute | solution.py:168
  0.5 46.3 %collective-permute-start.3 = (bf16[512,2048]{1,0:T(8,128)(2,1)}, bf16[512,2048]{1,0:T(8,128)(2,1)S(1)}, u32[]{:S(2)}, u32[]{:S(2)}) collective-permute-start(bf16[512,2048]{1,0:T(8,128)(2,1)} %refs_0_.1), channel_id=1, source_target_pairs={{0,3},{1,0},{2,1},{3,2},{4,7},{5,4},{6,5},{7,6},{8,11},{9,8},{10,9... | collective-permute-start | bytes 6291464 | tf_op jit(solution)/shard_map/ppermute | solution.py:176
  0.5 89.7 %collective-permute-start.4 = (bf16[512,2048]{1,0:T(8,128)(2,1)}, bf16[512,2048]{1,0:T(8,128)(2,1)S(1)}, u32[]{:S(2)}, u32[]{:S(2)}) collective-permute-start(bf16[512,2048]{1,0:T(8,128)(2,1)} %refs_0_.1), channel_id=1, source_target_pairs={{0,2},{1,3},{2,0},{3,1},{4,6},{5,7},{6,4},{7,5},{8,10},{9,11},{10,... | collective-permute-start | bytes 6291464 | tf_op jit(solution)/shard_map/ppermute | solution.py:176
  6.7 100.7 %collective-permute-start.26 = (bf16[2048,512]{1,0:T(8,128)(2,1)S(1)}, bf16[2048,512]{1,0:T(8,128)(2,1)S(1)}, u32[]{:S(2)}, u32[]{:S(2)}) collective-permute-start(bf16[2048,512]{1,0:T(8,128)(2,1)S(1)} %get-tuple-element.12), channel_id=1, source_target_pairs={{0,0},{4,8},{8,4},{12,12},{1,1},{5,9},{9,5},{13,13},{2,2},{6,10},{... | collective-permute-start | bytes 6291464 | tf_op jit(solution)/shard_map/ppermute | solution.py:170
  7.5 102.2 %collective-permute-start.6 = (bf16[2048,512]{1,0:T(8,128)(2,1)S(1)}, bf16[2048,512]{1,0:T(8,128)(2,1)S(1)}, u32[]{:S(2)}, u32[]{:S(2)}) collective-permute-start(bf16[2048,512]{1,0:T(8,128)(2,1)S(1)} %get-tuple-element.15), channel_id=1, source_target_pairs={{0,0},{4,8},{8,4},{12,12},{1,1},{5,9},{9,5},{13,13},{2,2},{6,10},{... | collective-permute-start | bytes 6291464 | tf_op jit(solution)/shard_map/ppermute | solution.py:170
  48.1 139.1 %collective-permute-start.5 = (bf16[512,2048]{1,0:T(8,128)(2,1)S(1)}, bf16[512,2048]{1,0:T(8,128)(2,1)}, u32[]{:S(2)}, u32[]{:S(2)}) collective-permute-start(bf16[512,2048]{1,0:T(8,128)(2,1)S(1)} %copy-done.11), channel_id=1, source_target_pairs={{0,1},{1,2},{2,3},{3,0},{4,5},{5,6},{6,7},{7,4},{8,9},{9,10},{10,1... | collective-permute-start | bytes 6291464 | tf_op jit(solution)/shard_map/ppermute | solution.py:176
  90.2 96.9 %copy-start.15 = (bf16[512,2048]{1,0:T(8,128)(2,1)}, bf16[512,2048]{1,0:T(8,128)(2,1)S(1)}, u32[]{:S(2)}) copy-start(bf16[512,2048]{1,0:T(8,128)(2,1)S(1)} %collective-permute-done.4.refs_2_) | copy-start | bytes 6291460
  90.2 99.0 %collective-permute-start.20 = (bf16[2048,512]{1,0:T(8,128)(2,1)}, bf16[2048,512]{1,0:T(8,128)(2,1)}, u32[]{:S(2)}, u32[]{:S(2)}) collective-permute-start(bf16[2048,512]{1,0:T(8,128)(2,1)} %get-tuple-element.13), channel_id=1, source_target_pairs={{0,0},{4,8},{8,4},{12,12},{1,1},{5,9},{9,5},{13,13},{2,2},{6,10},{... | collective-permute-start | bytes 6291464 | tf_op jit(solution)/shard_map/ppermute | solution.py:170
  107.4 79.7 %copy-start.7 = (bf16[2048,512]{1,0:T(8,128)(2,1)}, bf16[2048,512]{1,0:T(8,128)(2,1)S(1)}, u32[]{:S(2)}) copy-start(bf16[2048,512]{1,0:T(8,128)(2,1)S(1)} %collective-permute-done.26.p2) | copy-start | bytes 6291460
  107.4 83.6 %collective-permute-start.14 = (bf16[2048,512]{1,0:T(8,128)(2,1)}, bf16[2048,512]{1,0:T(8,128)(2,1)S(1)}, u32[]{:S(2)}, u32[]{:S(2)}) collective-permute-start(bf16[2048,512]{1,0:T(8,128)(2,1)} %get-tuple-element.14), channel_id=1, source_target_pairs={{0,0},{4,8},{8,4},{12,12},{1,1},{5,9},{9,5},{13,13},{2,2},{6,10},{... | collective-permute-start | bytes 6291464 | tf_op jit(solution)/shard_map/ppermute | solution.py:170
  109.8 118.7 %collective-permute-start.27 = (bf16[2048,512]{1,0:T(8,128)(2,1)S(1)}, bf16[2048,512]{1,0:T(8,128)(2,1)S(1)}, u32[]{:S(2)}, u32[]{:S(2)}) collective-permute-start(bf16[2048,512]{1,0:T(8,128)(2,1)S(1)} %collective-permute-done.26.p2), channel_id=1, source_target_pairs={{0,4},{4,0},{8,12},{12,8},{1,5},{5,1},{9,13},{13,9},{2,6},{6,2},{1... | collective-permute-start | bytes 6291464 | tf_op jit(solution)/shard_map/ppermute | solution.py:171
  183.5 102.0 %copy-start.1 = (bf16[8192,512]{1,0:T(8,128)(2,1)}, bf16[8192,512]{1,0:T(8,128)(2,1)S(1)}, u32[]{:S(2)}) copy-start(bf16[8192,512]{1,0:T(8,128)(2,1)S(1)} %collective-permute-done.near) | copy-start | bytes 25165828
  183.5 89.9 %collective-permute-start.7 = (bf16[2048,512]{1,0:T(8,128)(2,1)S(1)}, bf16[2048,512]{1,0:T(8,128)(2,1)S(1)}, u32[]{:S(2)}, u32[]{:S(2)}) collective-permute-start(bf16[2048,512]{1,0:T(8,128)(2,1)S(1)} %collective-permute-done.6.p2), channel_id=1, source_target_pairs={{0,4},{4,0},{8,12},{12,8},{1,5},{5,1},{9,13},{13,9},{2,6},{6,2},{1... | collective-permute-start | bytes 6291464 | tf_op jit(solution)/shard_map/ppermute | solution.py:171
  187.1 98.4 %collective-permute-start.30 = (bf16[1024,512]{1,0:T(8,128)(2,1)S(1)}, bf16[1024,512]{1,0:T(8,128)(2,1)}, u32[]{:S(2)}, u32[]{:S(2)}) collective-permute-start(bf16[1024,512]{1,0:T(8,128)(2,1)S(1)} %get-tuple-element.5), channel_id=1, source_target_pairs={{0,0},{4,8},{8,4},{12,12},{1,1},{5,9},{9,5},{13,13},{2,2},{6,10},{... | collective-permute-start | bytes 3145736 | tf_op jit(solution)/shard_map/ppermute | solution.py:172
  189.2 122.5 %collective-permute-start.28 = (bf16[1024,512]{1,0:T(8,128)(2,1)}, bf16[1024,512]{1,0:T(8,128)(2,1)S(1)}, u32[]{:S(2)}, u32[]{:S(2)}) collective-permute-start(bf16[1024,512]{1,0:T(8,128)(2,1)} %get-tuple-element.6), channel_id=1, source_target_pairs={{0,0},{4,8},{8,4},{12,12},{1,1},{5,9},{9,5},{13,13},{2,2},{6,10},{... | collective-permute-start | bytes 3145736 | tf_op jit(solution)/shard_map/ppermute | solution.py:172
  191.1 95.4 %copy-start.5 = (bf16[2048,512]{1,0:T(8,128)(2,1)}, bf16[2048,512]{1,0:T(8,128)(2,1)S(1)}, u32[]{:S(2)}) copy-start(bf16[2048,512]{1,0:T(8,128)(2,1)S(1)} %collective-permute-done.14.p2) | copy-start | bytes 6291460
  191.1 95.4 %collective-permute-start.8 = (bf16[384,512]{1,0:T(8,128)(2,1)S(1)}, bf16[384,512]{1,0:T(8,128)(2,1)S(1)}, u32[]{:S(2)}, u32[]{:S(2)}) collective-permute-start(bf16[384,512]{1,0:T(8,128)(2,1)S(1)} %slice.57), channel_id=1, source_target_pairs={{0,0},{4,8},{8,4},{12,12},{1,1},{5,9},{9,5},{13,13},{2,2},{6,10},{... | collective-permute-start | bytes 1179656 | tf_op jit(solution)/shard_map/ppermute | solution.py:172
  229.8 123.0 %collective-permute-start.21 = (bf16[2048,512]{1,0:T(8,128)(2,1)}, bf16[2048,512]{1,0:T(8,128)(2,1)}, u32[]{:S(2)}, u32[]{:S(2)}) collective-permute-start(bf16[2048,512]{1,0:T(8,128)(2,1)} %collective-permute-done.20.p2), channel_id=1, source_target_pairs={{0,4},{4,0},{8,12},{12,8},{1,5},{5,1},{9,13},{13,9},{2,6},{6,2},{1... | collective-permute-start | bytes 6291464 | tf_op jit(solution)/shard_map/ppermute | solution.py:171
  274.8 1.3 collective-permute-start.1
  276.1 50.0 %collective-permute-start.24 = (bf16[1024,512]{1,0:T(8,128)(2,1)}, bf16[1024,512]{1,0:T(8,128)(2,1)}, u32[]{:S(2)}, u32[]{:S(2)}) collective-permute-start(bf16[1024,512]{1,0:T(8,128)(2,1)} %get-tuple-element.7), channel_id=1, source_target_pairs={{0,0},{4,8},{8,4},{12,12},{1,1},{5,9},{9,5},{13,13},{2,2},{6,10},{... | collective-permute-start | bytes 3145736 | tf_op jit(solution)/shard_map/ppermute | solution.py:172
  285.6 55.4 %collective-permute-start.31 = (bf16[1024,512]{1,0:T(8,128)(2,1)}, bf16[1024,512]{1,0:T(8,128)(2,1)}, u32[]{:S(2)}, u32[]{:S(2)}) collective-permute-start(bf16[1024,512]{1,0:T(8,128)(2,1)} %collective-permute-done.30.p4), channel_id=1, source_target_pairs={{0,4},{4,0},{8,12},{12,8},{1,5},{5,1},{9,13},{13,9},{2,6},{6,2},{1... | collective-permute-start | bytes 3145736 | tf_op jit(solution)/shard_map/ppermute | solution.py:173
  286.5 24.2 %collective-permute-start.10 = (bf16[512,512]{1,0:T(8,128)(2,1)}, bf16[512,512]{1,0:T(8,128)(2,1)}, u32[]{:S(2)}, u32[]{:S(2)}) collective-permute-start(bf16[512,512]{1,0:T(8,128)(2,1)} %slice.58), channel_id=1, source_target_pairs={{0,0},{4,8},{8,4},{12,12},{1,1},{5,9},{9,5},{13,13},{2,2},{6,10},{... | collective-permute-start | bytes 1572872 | tf_op jit(solution)/shard_map/ppermute | solution.py:172
  291.9 1.6 copy-start.12
  293.5 1.6 copy-start.14
  295.1 1.6 copy-start.16
  296.7 4.0 copy-start.2
  296.7 4.6 copy-start.4
  301.3 3.4 copy-start
  306.9 3.9 copy-start.20
  310.7 15.3 %copy-start.19 = (bf16[1024,512]{1,0:T(8,128)(2,1)S(1)}, bf16[1024,512]{1,0:T(8,128)(2,1)}, u32[]{:S(2)}) copy-start(bf16[1024,512]{1,0:T(8,128)(2,1)} %get-tuple-element.9) | copy-start | bytes 3145732
  310.7 30.7 %copy-start.8 = (bf16[2048,512]{1,0:T(8,128)(2,1)S(1)}, bf16[2048,512]{1,0:T(8,128)(2,1)}, u32[]{:S(2)}) copy-start(bf16[2048,512]{1,0:T(8,128)(2,1)} %copy-done.7) | copy-start | bytes 6291460
  310.7 30.7 %copy-start.10 = (bf16[2048,512]{1,0:T(8,128)(2,1)S(1)}, bf16[2048,512]{1,0:T(8,128)(2,1)}, u32[]{:S(2)}) copy-start(bf16[2048,512]{1,0:T(8,128)(2,1)} %copy-done.9) | copy-start | bytes 6291460
  310.7 43.7 %collective-permute-start.22 = (bf16[1024,512]{1,0:T(8,128)(2,1)S(1)}, bf16[1024,512]{1,0:T(8,128)(2,1)S(1)}, u32[]{:S(2)}, u32[]{:S(2)}) collective-permute-start(bf16[1024,512]{1,0:T(8,128)(2,1)S(1)} %copy-done.20), channel_id=1, source_target_pairs={{0,0},{4,8},{8,4},{12,12},{1,1},{5,9},{9,5},{13,13},{2,2},{6,10},{... | collective-permute-start | bytes 3145736 | tf_op jit(solution)/shard_map/ppermute | solution.py:172
  311.6 51.7 %collective-permute-start.29 = (bf16[1024,512]{1,0:T(8,128)(2,1)S(1)}, bf16[1024,512]{1,0:T(8,128)(2,1)S(1)}, u32[]{:S(2)}, u32[]{:S(2)}) collective-permute-start(bf16[1024,512]{1,0:T(8,128)(2,1)S(1)} %collective-permute-done.28.p4), channel_id=1, source_target_pairs={{0,4},{4,0},{8,12},{12,8},{1,5},{5,1},{9,13},{13,9},{2,6},{6,2},{1... | collective-permute-start | bytes 3145736 | tf_op jit(solution)/shard_map/ppermute | solution.py:173
  326.0 26.8 %copy-start.6 = (bf16[2048,512]{1,0:T(8,128)(2,1)S(1)}, bf16[2048,512]{1,0:T(8,128)(2,1)}, u32[]{:S(2)}) copy-start(bf16[2048,512]{1,0:T(8,128)(2,1)} %copy-done.5) | copy-start | bytes 6291460
  326.0 48.0 %collective-permute-start.18 = (bf16[1024,512]{1,0:T(8,128)(2,1)S(1)}, bf16[1024,512]{1,0:T(8,128)(2,1)S(1)}, u32[]{:S(2)}, u32[]{:S(2)}) collective-permute-start(bf16[1024,512]{1,0:T(8,128)(2,1)S(1)} %copy-done.19), channel_id=1, source_target_pairs={{0,0},{4,8},{8,4},{12,12},{1,1},{5,9},{9,5},{13,13},{2,2},{6,10},{... | collective-permute-start | bytes 3145736 | tf_op jit(solution)/shard_map/ppermute | solution.py:172
  340.9 44.8 %collective-permute-start.25 = (bf16[1024,512]{1,0:T(8,128)(2,1)}, bf16[1024,512]{1,0:T(8,128)(2,1)S(1)}, u32[]{:S(2)}, u32[]{:S(2)}) collective-permute-start(bf16[1024,512]{1,0:T(8,128)(2,1)} %collective-permute-done.24.p4), channel_id=1, source_target_pairs={{0,4},{4,0},{8,12},{12,8},{1,5},{5,1},{9,13},{13,9},{2,6},{6,2},{1... | collective-permute-start | bytes 3145736 | tf_op jit(solution)/shard_map/ppermute | solution.py:173
  352.8 112.3 %collective-permute-start.15 = (bf16[2048,512]{1,0:T(8,128)(2,1)S(1)}, bf16[2048,512]{1,0:T(8,128)(2,1)S(1)}, u32[]{:S(2)}, u32[]{:S(2)}) collective-permute-start(bf16[2048,512]{1,0:T(8,128)(2,1)S(1)} %copy-done.6), channel_id=1, source_target_pairs={{0,4},{4,0},{8,12},{12,8},{1,5},{5,1},{9,13},{13,9},{2,6},{6,2},{1... | collective-permute-start | bytes 6291464 | tf_op jit(solution)/shard_map/ppermute | solution.py:171
  354.4 45.5 %collective-permute-start.16 = (bf16[1024,512]{1,0:T(8,128)(2,1)}, bf16[1024,512]{1,0:T(8,128)(2,1)S(1)}, u32[]{:S(2)}, u32[]{:S(2)}) collective-permute-start(bf16[1024,512]{1,0:T(8,128)(2,1)} %get-tuple-element.10), channel_id=1, source_target_pairs={{0,0},{4,8},{8,4},{12,12},{1,1},{5,9},{9,5},{13,13},{2,2},{6,10},{... | collective-permute-start | bytes 3145736 | tf_op jit(solution)/shard_map/ppermute | solution.py:172
  363.3 89.9 %collective-permute-start.23 = (bf16[1024,512]{1,0:T(8,128)(2,1)S(1)}, bf16[1024,512]{1,0:T(8,128)(2,1)S(1)}, u32[]{:S(2)}, u32[]{:S(2)}) collective-permute-start(bf16[1024,512]{1,0:T(8,128)(2,1)S(1)} %collective-permute-done.22.p4), channel_id=1, source_target_pairs={{0,4},{4,0},{8,12},{12,8},{1,5},{5,1},{9,13},{13,9},{2,6},{6,2},{1... | collective-permute-start | bytes 3145736 | tf_op jit(solution)/shard_map/ppermute | solution.py:173
  374.1 92.6 %collective-permute-start.12 = (bf16[1024,512]{1,0:T(8,128)(2,1)}, bf16[1024,512]{1,0:T(8,128)(2,1)S(1)}, u32[]{:S(2)}, u32[]{:S(2)}) collective-permute-start(bf16[1024,512]{1,0:T(8,128)(2,1)} %get-tuple-element.11), channel_id=1, source_target_pairs={{0,0},{4,8},{8,4},{12,12},{1,1},{5,9},{9,5},{13,13},{2,2},{6,10},{... | collective-permute-start | bytes 3145736 | tf_op jit(solution)/shard_map/ppermute | solution.py:172
  386.7 88.9 %collective-permute-start.19 = (bf16[1024,512]{1,0:T(8,128)(2,1)S(1)}, bf16[1024,512]{1,0:T(8,128)(2,1)S(1)}, u32[]{:S(2)}, u32[]{:S(2)}) collective-permute-start(bf16[1024,512]{1,0:T(8,128)(2,1)S(1)} %collective-permute-done.18.p4), channel_id=1, source_target_pairs={{0,4},{4,0},{8,12},{12,8},{1,5},{5,1},{9,13},{13,9},{2,6},{6,2},{1... | collective-permute-start | bytes 3145736 | tf_op jit(solution)/shard_map/ppermute | solution.py:173
  399.9 157.3 %collective-permute-start.2 = (bf16[128,512]{1,0:T(8,128)(2,1)}, bf16[128,512]{1,0:T(8,128)(2,1)}, u32[]{:S(2)}, u32[]{:S(2)}) collective-permute-start(bf16[128,512]{1,0:T(8,128)(2,1)} %collective-permute-done.1.p4), channel_id=1, source_target_pairs={{0,4},{4,0},{8,12},{12,8},{1,5},{5,1},{9,13},{13,9},{2,6},{6,2},{1... | collective-permute-start | bytes 393224 | tf_op jit(solution)/shard_map/ppermute | solution.py:173
  453.2 47.8 %collective-permute-start.17 = (bf16[1024,512]{1,0:T(8,128)(2,1)S(1)}, bf16[1024,512]{1,0:T(8,128)(2,1)S(1)}, u32[]{:S(2)}, u32[]{:S(2)}) collective-permute-start(bf16[1024,512]{1,0:T(8,128)(2,1)S(1)} %collective-permute-done.16.p4), channel_id=1, source_target_pairs={{0,4},{4,0},{8,12},{12,8},{1,5},{5,1},{9,13},{13,9},{2,6},{6,2},{1... | collective-permute-start | bytes 3145736 | tf_op jit(solution)/shard_map/ppermute | solution.py:173
  465.1 89.6 %collective-permute-start.9 = (bf16[384,512]{1,0:T(8,128)(2,1)S(1)}, bf16[384,512]{1,0:T(8,128)(2,1)S(1)}, u32[]{:S(2)}, u32[]{:S(2)}) collective-permute-start(bf16[384,512]{1,0:T(8,128)(2,1)S(1)} %collective-permute-done.8.p4), channel_id=1, source_target_pairs={{0,4},{4,0},{8,12},{12,8},{1,5},{5,1},{9,13},{13,9},{2,6},{6,2},{1... | collective-permute-start | bytes 1179656 | tf_op jit(solution)/shard_map/ppermute | solution.py:173
  466.6 85.6 %collective-permute-start.11 = (bf16[512,512]{1,0:T(8,128)(2,1)}, bf16[512,512]{1,0:T(8,128)(2,1)S(1)}, u32[]{:S(2)}, u32[]{:S(2)}) collective-permute-start(bf16[512,512]{1,0:T(8,128)(2,1)} %collective-permute-done.10.p4), channel_id=1, source_target_pairs={{0,4},{4,0},{8,12},{12,8},{1,5},{5,1},{9,13},{13,9},{2,6},{6,2},{1... | collective-permute-start | bytes 1572872 | tf_op jit(solution)/shard_map/ppermute | solution.py:173
  475.7 66.3 %collective-permute-start.13 = (bf16[1024,512]{1,0:T(8,128)(2,1)S(1)}, bf16[1024,512]{1,0:T(8,128)(2,1)S(1)}, u32[]{:S(2)}, u32[]{:S(2)}) collective-permute-start(bf16[1024,512]{1,0:T(8,128)(2,1)S(1)} %collective-permute-done.12.p4), channel_id=1, source_target_pairs={{0,4},{4,0},{8,12},{12,8},{1,5},{5,1},{9,13},{13,9},{2,6},{6,2},{1... | collective-permute-start | bytes 3145736 | tf_op jit(solution)/shard_map/ppermute | solution.py:173
  (5 other events, 6.2 us)
